TPU v7x, 32 devices: a whole 2x2x4 slice. The times are simulated.
32 devices in a mesh: row: 4 (over x, core), col: 4 (over z), head: 2 (over y).
Axes of the slice: x: 2, y: 2, z: 4, core: 2. Of those that a mesh axis runs over, the one named last changes fastest.
Arguments:
- query_map: bfloat16 [64, 128, 3072], P('row', 'col', 'head'), may hold values from -6 to 6
- key_map: bfloat16 [64, 128, 3072], P('row', 'col', 'head'), may hold values from -7 to 7
- value_map: bfloat16 [64, 128, 3072], P('row', 'col', 'head'), may hold values from -6 to 6
- window_mask: int32 [4, 4, 13, 13], P('row', 'col'), may hold values 0 or 1
- tile_radius: int32 [4, 4], P('row', 'col'), may hold values from 3 to 6, as said below
- dilation_per_tile: int32 [4, 4], P('row', 'col'), may hold values from 1 to 3, as said below
- rel_bias: float32 [48, 13, 13], P('head'), may hold values from -4 to 4
- out_weight: bfloat16 [3072, 3072], P('head'), may hold values from -0.109375 to 0.109375
Outputs:
- mixed: bfloat16 [64, 128, 3072], P('row', 'col', 'head')
Inputs may be any that keep to these rules, and one draw needn't show every extreme that they name: `tile_radius`: in each row of tiles, at least one tile has radius 6 and dilation 3. `dilation_per_tile`: in each row of tiles, at least one tile has radius 6 and dilation 3.
All inputs are finite; a program needn't handle non-finite values. No bound on the sum of `window_mask` on one device may be relied on, other than what follows from the above.
Results may differ from a plain program's by a relative error of at most 0.0073.
Values may be sent and summed in bfloat16 or wider, within the bound.
No kernel may reach another device: no remote copies, remote signals or barrier semaphores. Data moves between devices by JAX's collectives and lax.ppermute only.
A program may use at most 384 MiB of HBM per device.

v0:
```python
import math

import jax
import jax.numpy as jnp
from jax import lax
from jax.sharding import PartitionSpec as P

HEAD_DIM = 64
RADIUS_MAX = 6
WINDOW = 13
HALO = 18


def shifted(value, axis, steps):
    count = lax.axis_size(axis)
    leading, last = (max(0, -steps), min(count, count - steps))
    return lax.ppermute(value, axis, [(source, source + steps) for source in range(leading, last)])


def column_source(tile_block, shift_by):
    return shifted(tile_block, "col", shift_by)


def from_row(tile_block, shift_by):
    return shifted(tile_block, "row", shift_by)


def from_relay(tile_block, shift_by):
    return shifted(tile_block, "row", shift_by)


def add_cols(tile_block, halo_depth):
    block_width = tile_block.shape[2]
    left_cols = column_source(tile_block[:, :, block_width - halo_depth :], 1)
    right_cols = column_source(tile_block[:, :, :halo_depth], -1)
    return jnp.concatenate([left_cols, tile_block, right_cols], axis=2)


def add_rows(tile_block, halo_depth):
    block_height = tile_block.shape[1]
    spill_rows = halo_depth - block_height
    rows_above = from_row(tile_block, 1)
    rows_below = from_row(tile_block, -1)
    far_above = from_relay(rows_above[:, block_height - spill_rows :], 1)
    far_below = from_relay(rows_below[:, :spill_rows], -1)
    return jnp.concatenate([far_above, rows_above, tile_block, rows_below, far_below], axis=1)


def shards(
    query_map, key_map, value_map, window_mask, tile_radius, dilation_per_tile, rel_bias, out_weight
):
    tile_rows, tile_cols, features_dev = query_map.shape
    heads_dev = features_dev // HEAD_DIM
    halo_depth = HALO
    kv_pair = jnp.stack([key_map, value_map])
    widened_keys = add_cols(add_rows(kv_pair, halo_depth), halo_depth)
    key_span = tile_cols + 2 * halo_depth
    row_anchor = lax.axis_index("row") * tile_rows
    col_anchor = lax.axis_index("col") * tile_cols
    total_rows = tile_rows * lax.axis_size("row")
    total_cols = tile_cols * lax.axis_size("col")
    radius = tile_radius[0, 0]
    dilation = dilation_per_tile[0, 0]
    pattern = window_mask[0, 0]
    col_steps = jnp.arange(WINDOW, dtype=jnp.int32) - RADIUS_MAX
    column = jnp.arange(tile_cols, dtype=jnp.int32)
    key_spots = jnp.arange(key_span, dtype=jnp.int32)
    destination_tiles = column[None, :] + halo_depth + col_steps[:, None] * dilation
    onehot = (key_spots[None, None, :] == destination_tiles[:, :, None]).astype(jnp.float32)
    onehot_half = onehot.astype(jnp.bfloat16)
    col_global = col_anchor + column[None, :] + col_steps[:, None] * dilation
    column_offset = (
        (jnp.abs(col_steps)[:, None] <= radius) & (col_global >= 0) & (col_global < total_cols)
    )
    row_index = jnp.arange(tile_rows, dtype=jnp.int32)
    query_heads = query_map.reshape(tile_rows, tile_cols, heads_dev, HEAD_DIM)
    score_scale = 1.0 / math.sqrt(HEAD_DIM)
    highest = lax.Precision.HIGHEST
    score_list = []
    valid_list = []
    for offset in range(WINDOW):
        row_lift = offset - RADIUS_MAX
        row_start = halo_depth + row_lift * dilation
        key_strip = lax.dynamic_slice_in_dim(widened_keys[0], row_start, tile_rows, 0)
        key_strip = key_strip.reshape(tile_rows, key_span, heads_dev, HEAD_DIM)
        raw_score = jnp.einsum(
            "icnh,iknh->inck", query_heads, key_strip, preferred_element_type=jnp.float32
        )
        picked = jnp.einsum("inck,bck->incb", raw_score, onehot, precision=highest)
        chosen = (pattern[offset] == 1) | (col_steps == 0) & (row_lift == 0)
        row_global = row_anchor + row_index + row_lift * dilation
        row_fine = (abs(row_lift) <= radius) & (row_global >= 0) & (row_global < total_rows)
        col_valid = jnp.transpose(chosen[:, None] & column_offset)
        bias_row = rel_bias[:, offset, :]
        score_list.append(picked * score_scale + bias_row[None, :, None, :])
        valid_list.append(row_fine[:, None, None, None] & col_valid[None, None, :, :])
    scores = jnp.stack(score_list)
    valid_mask = jnp.stack(valid_list)
    peak_score = jnp.max(jnp.where(valid_mask, scores, -1e30), axis=(0, 4), keepdims=True)
    exponent = jnp.where(
        valid_mask, jnp.exp(jnp.where(valid_mask, scores - peak_score, -60.0)), 0.0
    )
    denominator = jnp.sum(exponent, axis=(0, 4), keepdims=True)
    weights = (exponent / denominator).astype(jnp.bfloat16)
    mixed_heads = jnp.zeros((tile_rows, tile_cols, heads_dev, HEAD_DIM), jnp.float32)
    for offset in range(WINDOW):
        row_start = halo_depth + (offset - RADIUS_MAX) * dilation
        values_slab = lax.dynamic_slice_in_dim(widened_keys[1], row_start, tile_rows, 0)
        values_slab = values_slab.reshape(tile_rows, key_span, heads_dev, HEAD_DIM)
        spread = jnp.einsum(
            "incb,bck->inck", weights[offset], onehot_half, preferred_element_type=jnp.float32
        ).astype(jnp.bfloat16)
        mixed_heads = mixed_heads + jnp.einsum(
            "inck,iknh->icnh", spread, values_slab, preferred_element_type=jnp.float32
        )
    attended = mixed_heads.reshape(tile_rows * tile_cols, features_dev).astype(jnp.bfloat16)
    partials = jnp.dot(attended, out_weight, preferred_element_type=jnp.float32)
    partials = partials.reshape(tile_rows, tile_cols, out_weight.shape[1])
    return lax.psum_scatter(partials, "head", scatter_dimension=2, tiled=True).astype(jnp.bfloat16)


def solution(mesh):
    placed = (
        P("row", "col", "head"),
        P("row", "col", "head"),
        P("row", "col", "head"),
        P("row", "col", None, None),
        P("row", "col"),
        P("row", "col"),
        P("head", None, None),
        P("head", None),
    )
    return jax.shard_map(
        shards, mesh=mesh, in_specs=placed, out_specs=P("row", "col", "head"), check_vma=False
    )
```

profile of v0, /device:TPU:0, one launch (start us, length us, event | category | flops | bytes accessed | tf_op | source)
XLA Modules:
  0.0 1193.9 jit_solution(15250712338779425406)
XLA Ops:
  16.6 33.4 %collective-permute-start.1 = (bf16[2,2,32,1536]{3,2,1,0:T(8,128)(2,1)S(1)}, bf16[2,2,32,1536]{3,2,1,0:T(8,128)(2,1)S(1)}, u32[]{:S(2)}, u32[]{:S(2)}) collective-permute-start(bf16[2,2,32,1536]{3,2,1,0:T(8,128)(2,1)S(1)} %slice.221), channel_id=1, source_target_pairs={{0,8},{8,16},{16,24},{1,9},{9,17},{17,25},{2,10},{10,18},{18,26},{... | collective-permute-start | bytes 1179656 | tf_op jit(solution)/shard_map/ppermute | solution.py:17
  59.5 13.7 %copy.129 = bf16[2,52,18,1536]{3,0,2,1:T(2,128)(2,1)} copy(bf16[2,52,18,1536]{3,2,1,0:T(8,128)(2,1)S(1)} %get-tuple-element.33) | data formatting | bytes 11501568 | tf_op jit(solution)/shard_map/slice | solution.py:34
  79.1 13.7 %copy.130 = bf16[2,52,18,1536]{3,0,2,1:T(2,128)(2,1)} copy(bf16[2,52,18,1536]{3,2,1,0:T(8,128)(2,1)S(1)} %get-tuple-element.34) | data formatting | bytes 11501568 | tf_op jit(solution)/shard_map/slice | solution.py:35
  106.2 90.1 %collective-permute-done.4 = bf16[2,52,18,1536]{3,0,2,1:T(2,128)(2,1)} collective-permute-done((bf16[2,52,18,1536]{3,0,2,1:T(2,128)(2,1)}, bf16[2,52,18,1536]{3,0,2,1:T(2,128)(2,1)}, u32[]{:S(2)}, u32[]{:S(2)}) %collective-permute-start.4) | collective-permute-done | bytes 5750816 | tf_op jit(solution)/shard_map/ppermute | solution.py:17
  203.2 13.9 %collective-permute-done.5 = bf16[2,52,18,1536]{3,0,2,1:T(2,128)(2,1)} collective-permute-done((bf16[2,52,18,1536]{3,0,2,1:T(2,128)(2,1)}, bf16[2,52,18,1536]{3,0,2,1:T(2,128)(2,1)}, u32[]{:S(2)}, u32[]{:S(2)}) %collective-permute-start.5) | collective-permute-done | bytes 5750816 | tf_op jit(solution)/shard_map/ppermute | solution.py:17
  224.0 23.9 %pad_maximum_fusion = bf16[2,52,68,1536]{3,2,1,0:T(8,128)(2,1)} fusion(bf16[2,52,18,1536]{3,2,1,0:T(8,128)(2,1)} %copy.132, bf16[2,52,32,1536]{3,2,1,0:T(8,128)(2,1)} %copy-done, bf16[2,52,18,1536]{3,2,1,0:T(8,128)(2,1)} %copy.131), kind=kLoop, calls=%fused_computation.4 | loop fusion | flops 65175552 | bytes 43450368 | tf_op jit(solution)/shard_map/concatenate | solution.py:36
  247.9 9.7 pad_maximum_fusion.1
  260.3 7.9 fusion.154
  268.2 54.7 %constant_dynamic-slice_fusion.10 = (bf16[1,16,68,1536]{3,2,1,0:T(8,128)(2,1)}, bf16[1,16,68,1536]{3,2,1,0:T(8,128)(2,1)}, bf16[1,16,68,1536]{3,2,1,0:T(8,128)(2...) fusion(bf16[1,52,68,1536]{3,2,1,0:T(8,128)(2,1)} %get-tuple-ele, ...), kind=kLoop, calls=%fused_computation.205 | loop fusion | bytes 160432176 | tf_op jit(solution)/shard_map/dynamic_slice | solution.py:108
  322.9 7.8 copy.241
  330.7 8.0 copy.242
  338.7 7.3 convolution_bitcast_fusion.12
  349.6 7.8 copy.243
  364.5 7.8 copy.244
  372.2 7.3 convolution_bitcast_fusion.9
  379.5 7.8 copy.245
  394.4 7.8 copy.246
  402.2 7.2 convolution_bitcast_fusion.7
  409.4 8.0 copy.247
  417.4 7.2 convolution_bitcast_fusion.6
  424.6 7.8 copy.248
  439.4 7.8 copy.249
  454.3 7.8 copy.250
  469.2 7.8 copy.251
  477.0 7.2 convolution_bitcast_fusion.2
  484.1 7.8 copy.252
  491.9 7.2 convolution_bitcast_fusion.1
  499.1 7.8 copy.253
  511.2 21.7 %bitcast_dynamic-update-slice_fusion.12 = f32[13,16,24,32,13]{2,4,1,3,0:T(8,128)} fusion(f32[16,24,32,68]{3,2,1,0:T(8,128)} %convolution_bitcast_fusion.12, f32[24,13]{0,1:T(8,128)S(1)} %copy-done.31, s32[13,32]{0,1:T(8,128)S(1)} %copy-done.16), kind=kOutput, calls=%fused_computation.58 | convolution fusion | flops 130698880 | bytes 7539552 | tf_op jit(solution)/shard_map/inck,bck->incb/dot_general | solution.py:89
  532.9 21.7 %bitcast_dynamic-update-slice_fusion.11 = f32[13,16,24,32,13]{2,4,1,3,0:T(8,128)} fusion(f32[13,16,24,32,13]{2,4,1,3,0:T(8,128)} %bitcast_dynamic-update-slice_fusion.12, f32[16,24,32,68]{3,2,1,0:T(8,128)} %convolution_bitcast_fusion.11, f32[24,13]{0,1:T(8,128)S(1)} %copy-done.30, s32[13,32]{0,1:T(8,128)S(1)} %copy-done.16), kind=kOutput, calls=%fused_computation.56 | convolution fusion | flops 130698880 | bytes 10488672 | tf_op jit(solution)/shard_map/inck,bck->incb/dot_general | solution.py:89
  554.7 18.6 %bitcast_dynamic-update-slice_fusion.10 = f32[13,16,24,32,13]{2,4,1,3,0:T(8,128)} fusion(f32[13,16,24,32,13]{2,4,1,3,0:T(8,128)} %bitcast_dynamic-update-slice_fusion.11, f32[16,24,32,68]{3,2,1,0:T(8,128)S(1)} %bitcast.357, f32[24,13]{0,1:T(8,128)S(1)} %copy-done.29, s32[13,32]{0,1:T(8,128)S(1)} %copy-done.16), kind=kOutput, calls=%fused_computation.54 | convolution fusion | flops 130698880 | bytes 7539552 | tf_op jit(solution)/shard_map/inck,bck->incb/dot_general | solution.py:89
  573.3 19.0 %bitcast_dynamic-update-slice_fusion.9 = f32[13,16,24,32,13]{2,4,1,3,0:T(8,128)} fusion(f32[13,16,24,32,13]{2,4,1,3,0:T(8,128)} %bitcast_dynamic-update-slice_fusion.10, f32[16,24,32,68]{3,2,1,0:T(8,128)S(1)} %bitcast.359, f32[24,13]{0,1:T(8,128)S(1)} %copy-done.28, s32[13,32]{0,1:T(8,128)S(1)} %copy-done.16), kind=kOutput, calls=%fused_computation.52 | convolution fusion | flops 130698880 | bytes 7539552 | tf_op jit(solution)/shard_map/inck,bck->incb/dot_general | solution.py:89
  592.4 18.8 %bitcast_dynamic-update-slice_fusion.8 = f32[13,16,24,32,13]{2,4,1,3,0:T(8,128)} fusion(f32[13,16,24,32,13]{2,4,1,3,0:T(8,128)} %bitcast_dynamic-update-slice_fusion.9, f32[16,24,32,68]{3,2,1,0:T(8,128)S(1)} %bitcast.361, f32[24,13]{0,1:T(8,128)S(1)} %copy-done.27, s32[13,32]{0,1:T(8,128)S(1)} %copy-done.16), kind=kOutput, calls=%fused_computation.50 | convolution fusion | flops 130698880 | bytes 7539552 | tf_op jit(solution)/shard_map/inck,bck->incb/dot_general | solution.py:89
  611.2 18.9 %bitcast_dynamic-update-slice_fusion.7 = f32[13,16,24,32,13]{2,4,1,3,0:T(8,128)} fusion(f32[13,16,24,32,13]{2,4,1,3,0:T(8,128)} %bitcast_dynamic-update-slice_fusion.8, f32[16,24,32,68]{3,2,1,0:T(8,128)S(1)} %bitcast.363, f32[24,13]{0,1:T(8,128)S(1)} %copy-done.26, s32[13,32]{0,1:T(8,128)S(1)} %copy-done.16), kind=kOutput, calls=%fused_computation.48 | convolution fusion | flops 130698880 | bytes 7539552 | tf_op jit(solution)/shard_map/inck,bck->incb/dot_general | solution.py:89
  630.1 18.9 %bitcast_dynamic-update-slice_fusion.6 = f32[13,16,24,32,13]{2,4,1,3,0:T(8,128)} fusion(f32[13,16,24,32,13]{2,4,1,3,0:T(8,128)} %bitcast_dynamic-update-slice_fusion.7, f32[16,24,32,68]{3,2,1,0:T(8,128)S(1)} %bitcast.365, f32[24,13]{0,1:T(8,128)S(1)} %copy-done.25, s32[13,32]{0,1:T(8,128)S(1)} %copy-done.16), kind=kOutput, calls=%fused_computation.46 | convolution fusion | flops 130698880 | bytes 7539552 | tf_op jit(solution)/shard_map/inck,bck->incb/dot_general | solution.py:89
  649.0 18.8 %bitcast_dynamic-update-slice_fusion.5 = f32[13,16,24,32,13]{2,4,1,3,0:T(8,128)} fusion(f32[13,16,24,32,13]{2,4,1,3,0:T(8,128)} %bitcast_dynamic-update-slice_fusion.6, f32[16,24,32,68]{3,2,1,0:T(8,128)S(1)} %bitcast.367, f32[24,13]{0,1:T(8,128)S(1)} %copy-done.24, s32[13,32]{0,1:T(8,128)S(1)} %copy-done.16), kind=kOutput, calls=%fused_computation.44 | convolution fusion | flops 130698880 | bytes 7539552 | tf_op jit(solution)/shard_map/inck,bck->incb/dot_general | solution.py:89
  667.9 19.1 %bitcast_dynamic-update-slice_fusion.4 = f32[13,16,24,32,13]{2,4,1,3,0:T(8,128)} fusion(f32[13,16,24,32,13]{2,4,1,3,0:T(8,128)} %bitcast_dynamic-update-slice_fusion.5, f32[16,24,32,68]{3,2,1,0:T(8,128)S(1)} %bitcast.369, f32[24,13]{0,1:T(8,128)S(1)} %copy-done.23, s32[13,32]{0,1:T(8,128)S(1)} %copy-done.16), kind=kOutput, calls=%fused_computation.42 | convolution fusion | flops 130698880 | bytes 7539552 | tf_op jit(solution)/shard_map/inck,bck->incb/dot_general | solution.py:89
  687.0 18.8 %bitcast_dynamic-update-slice_fusion.3 = f32[13,16,24,32,13]{2,4,1,3,0:T(8,128)} fusion(f32[13,16,24,32,13]{2,4,1,3,0:T(8,128)} %bitcast_dynamic-update-slice_fusion.4, f32[16,24,32,68]{3,2,1,0:T(8,128)S(1)} %bitcast.371, f32[24,13]{0,1:T(8,128)S(1)} %copy-done.22, s32[13,32]{0,1:T(8,128)S(1)} %copy-done.16), kind=kOutput, calls=%fused_computation.40 | convolution fusion | flops 130698880 | bytes 7539552 | tf_op jit(solution)/shard_map/inck,bck->incb/dot_general | solution.py:89
  705.8 18.8 %bitcast_dynamic-update-slice_fusion.2 = f32[13,16,24,32,13]{2,4,1,3,0:T(8,128)} fusion(f32[13,16,24,32,13]{2,4,1,3,0:T(8,128)} %bitcast_dynamic-update-slice_fusion.3, f32[16,24,32,68]{3,2,1,0:T(8,128)S(1)} %bitcast.373, f32[24,13]{0,1:T(8,128)S(1)} %copy-done.21, s32[13,32]{0,1:T(8,128)S(1)} %copy-done.16), kind=kOutput, calls=%fused_computation.38 | convolution fusion | flops 130698880 | bytes 7539552 | tf_op jit(solution)/shard_map/inck,bck->incb/dot_general | solution.py:89
  724.6 18.7 %bitcast_dynamic-update-slice_fusion.1 = f32[13,16,24,32,13]{2,4,1,3,0:T(8,128)} fusion(f32[13,16,24,32,13]{2,4,1,3,0:T(8,128)} %bitcast_dynamic-update-slice_fusion.2, f32[16,24,32,68]{3,2,1,0:T(8,128)S(1)} %bitcast.375, f32[24,13]{0,1:T(8,128)S(1)} %copy-done.20, s32[13,32]{0,1:T(8,128)S(1)} %copy-done.16), kind=kOutput, calls=%fused_computation.36 | convolution fusion | flops 130698880 | bytes 7539552 | tf_op jit(solution)/shard_map/inck,bck->incb/dot_general | solution.py:89
  743.4 18.9 %bitcast_dynamic-update-slice_fusion = f32[13,16,24,32,13]{2,4,1,3,0:T(8,128)} fusion(f32[13,16,24,32,13]{2,4,1,3,0:T(8,128)} %bitcast_dynamic-update-slice_fusion.1, f32[16,24,32,68]{3,2,1,0:T(8,128)S(1)} %convolution_bitcast_fusion, f32[24,13]{0,1:T(8,128)S(1)} %copy-done.19, s32[13,32]{0,1:T(8,128)S(1)} %copy-done.16), kind=kOutput, calls=%fused_computation.34 | convolution fusion | flops 130698880 | bytes 7539552 | tf_op jit(solution)/shard_map/inck,bck->incb/dot_general | solution.py:89
  762.3 21.8 %select_reduce_fusion = f32[16,24,32]{1,0,2:T(8,128)S(1)} fusion(f32[13,16,24,32,13]{2,4,1,3,0:T(8,128)} %bitcast_dynamic-update-slice_fusion, pred[13,16,32,13]{3,1,2,0:T(8,128)(4,1)S(1)} %copy-done.9), kind=kLoop, calls=%fused_computation.2 | loop fusion | flops 4141056 | bytes 8442368 | tf_op jit(solution)/shard_map/reduce_max | solution.py:99
  784.1 26.5 %fusion = f32[16,24,32]{1,0,2:T(8,128)S(1)} fusion(f32[13,16,24,32,13]{2,4,1,3,0:T(8,128)} %bitcast_dynamic-update-slice_fusion, f32[16,24,32]{1,0,2:T(8,128)S(1)} %select_reduce_fusion, pred[13,16,32,13]{3,1,2,0:T(8,128)(4,1)S(1)} %copy-done.9), kind=kLoop, calls=%fused_computation.3 | loop fusion | flops 8294400 | bytes 8491520 | tf_op jit(solution)/shard_map/reduce_sum | solution.py:103
  810.6 26.0 %divide_convert_fusion = bf16[13,16,24,32,13]{2,4,1,3,0:T(8,128)(2,1)S(1)} fusion(f32[13,16,24,32,13]{2,4,1,3,0:T(8,128)} %bitcast_dynamic-update-slice_fusion, f32[16,24,32]{1,0,2:T(8,128)S(1)} %fusion, f32[16,24,32]{1,0,2:T(8,128)S(1)} %select_reduce_fusion, pred[13,16,32,13]{3,1,2,0:T(8,128)(4,1)S(1)} %copy-done.9), kind=kLoop, calls=%fused_computation | loop fusion | flops 10383360 | bytes 12644864 | tf_op jit(solution)/shard_map/convert_element_type | solution.py:104
  873.1 7.8 copy.188
  886.3 7.9 copy.190
  899.6 7.9 copy.194
  912.9 8.0 copy.200
  926.2 7.9 copy.204
  939.6 7.9 copy.208
  952.8 8.1 copy.198
  960.9 10.0 fusion.51
  970.9 8.1 fusion.53
  979.0 9.0 fusion.49
  988.0 8.2 fusion.47
  996.2 9.5 fusion.45
  1005.7 8.1 fusion.43
  1013.9 8.3 fusion.39
  1022.1 9.1 fusion.37
  1036.6 9.9 fusion.33
  1051.7 8.1 fusion.29
  1059.8 28.9 %fusion.55 = bf16[16,32,24,64]{3,1,2,0:T(8,128)(2,1)} fusion(f32[16,24,64,32]{2,3,1,0:T(8,128)} %fusion.29, f32[16,24,64,32]{2,3,1,0:T(8,128)} %fusion.31, f32[16,24,64,32]{2,3,1,0:T(8,128)} %fusion.33, f32[16,24,64,32]{2,3,1,0:T(8,128)} %fusion.35, f32[16,24,64,32]{2,3,1,0:T(8,128)} %fusion.37, f32[16,24,64,32]{2,3,1,0:T(8,128)} %fusion.39, ...), kind=kOutput, calls=%fused_computation.102 | convolution fusion | flops 117178368 | bytes 44335104 | tf_op jit(solution)/shard_map/inck,iknh->icnh/dot_general | solution.py:113
  1094.9 9.8 fusion.1
  1104.7 78.8 %reduce-scatter.2.cloned.1.call-done = f32[16,32,1536]{2,1,0:T(8,128)} async-done(((f32[16,32,3072]{2,1,0:T(8,128)}), f32[16,32,1536]{2,1,0:T(8,128)}) %reduce-scatter.2.cloned.1.call-update) | async-done | bytes 3145744 | tf_op jit(solution)/shard_map/reduce_scatter | solution.py:119
  (234 shorter events, 186.0 us)
Async XLA Ops:
  6.5 1177.0 %reduce-scatter.2.cloned.1.call-start = ((), (), s32[]{:S(2)}) async-start(), calls=%async_computation.1 | async-start | bytes 9437184 | tf_op jit(solution)/shard_map/reduce_scatter | solution.py:119
  6.5 45.2 %copy-start.17 = (bf16[16,32,1536]{2,1,0:T(8,128)(2,1)S(1)}, bf16[16,32,1536]{2,1,0:T(8,128)(2,1)}, u32[]{:S(2)}) copy-start(bf16[16,32,1536]{2,1,0:T(8,128)(2,1)} %param.10) | copy-start | bytes 4718596
  6.5 45.2 %copy-start.18 = (bf16[16,32,1536]{2,1,0:T(8,128)(2,1)S(1)}, bf16[16,32,1536]{2,1,0:T(8,128)(2,1)}, u32[]{:S(2)}) copy-start(bf16[16,32,1536]{2,1,0:T(8,128)(2,1)} %param.9) | copy-start | bytes 4718596
  8.9 7.7 collective-permute-start
  11.5 38.6 %collective-permute-start.2 = (bf16[2,16,32,1536]{3,2,1,0:T(8,128)(2,1)S(1)}, bf16[2,16,32,1536]{3,2,1,0:T(8,128)(2,1)S(1)}, u32[]{:S(2)}, u32[]{:S(2)}) collective-permute-start(bf16[2,16,32,1536]{3,2,1,0:T(8,128)(2,1)S(1)} %pad_maximum_fusion.3), channel_id=1, source_target_pairs={{8,0},{16,8},{24,16},{9,1},{17,9},{25,17},{10,2},{18,10},{26,18},{... | collective-permute-start | bytes 9437192 | tf_op jit(solution)/shard_map/ppermute | solution.py:17
  16.6 34.8 %collective-permute-start.1 = (bf16[2,2,32,1536]{3,2,1,0:T(8,128)(2,1)S(1)}, bf16[2,2,32,1536]{3,2,1,0:T(8,128)(2,1)S(1)}, u32[]{:S(2)}, u32[]{:S(2)}) collective-permute-start(bf16[2,2,32,1536]{3,2,1,0:T(8,128)(2,1)S(1)} %slice.221), channel_id=1, source_target_pairs={{0,8},{8,16},{16,24},{1,9},{9,17},{17,25},{2,10},{10,18},{18,26},{... | collective-permute-start | bytes 1179656 | tf_op jit(solution)/shard_map/ppermute | solution.py:17
  50.1 5.6 collective-permute-start.3
  73.2 123.1 %collective-permute-start.4 = (bf16[2,52,18,1536]{3,0,2,1:T(2,128)(2,1)}, bf16[2,52,18,1536]{3,0,2,1:T(2,128)(2,1)}, u32[]{:S(2)}, u32[]{:S(2)}) collective-permute-start(bf16[2,52,18,1536]{3,0,2,1:T(2,128)(2,1)} %copy.129), channel_id=1, source_target_pairs={{0,2},{2,4},{4,6},{1,3},{3,5},{5,7},{8,10},{10,12},{12,14},{9,11},... | collective-permute-start | bytes 17252360 | tf_op jit(solution)/shard_map/ppermute | solution.py:17
  79.1 21.1 %copy-start.32 = (s32[1,1,13,13]{3,1,2,0:T(1,128)S(1)}, s32[1,1,13,13]{3,1,2,0:T(1,128)}, u32[]{:S(2)}) copy-start(s32[1,1,13,13]{3,1,2,0:T(1,128)} %param.11) | copy-start | bytes 2032
  92.8 124.3 %collective-permute-start.5 = (bf16[2,52,18,1536]{3,0,2,1:T(2,128)(2,1)}, bf16[2,52,18,1536]{3,0,2,1:T(2,128)(2,1)}, u32[]{:S(2)}, u32[]{:S(2)}) collective-permute-start(bf16[2,52,18,1536]{3,0,2,1:T(2,128)(2,1)} %copy.130), channel_id=1, source_target_pairs={{2,0},{4,2},{6,4},{3,1},{5,3},{7,5},{10,8},{12,10},{14,12},{11,9},... | collective-permute-start | bytes 17252360 | tf_op jit(solution)/shard_map/ppermute | solution.py:17
  247.9 12.4 %copy-start.1 = (bf16[2,52,68,1536]{3,2,1,0:T(8,128)(2,1)S(1)}, bf16[2,52,68,1536]{3,2,1,0:T(8,128)(2,1)}, u32[]{:S(2)}) copy-start(bf16[2,52,68,1536]{3,2,1,0:T(8,128)(2,1)} %pad_maximum_fusion) | copy-start | bytes 65175556
  511.2 21.7 %copy-start.30 = (f32[24,13]{0,1:T(8,128)S(1)}, f32[24,13]{0,1:T(8,128)}, u32[]{:S(2)}) copy-start(f32[24,13]{0,1:T(8,128)} %get-tuple-element.45) | copy-start | bytes 3748
  511.2 43.4 %slice-start = ((s8[6291456]{0:T(1024)(128)(4,1)}), s8[4194304]{0:T(1024)(128)(4,1)S(1)}, s32[]{:S(2)}) async-start(s8[6291456]{0:T(1024)(128)(4,1)} %bitcast.356), calls=%async_computation.2 | async-start | bytes 8388608
  532.9 21.7 %copy-start.29 = (f32[24,13]{0,1:T(8,128)S(1)}, f32[24,13]{0,1:T(8,128)}, u32[]{:S(2)}) copy-start(f32[24,13]{0,1:T(8,128)} %get-tuple-element.44) | copy-start | bytes 3748
  532.9 21.7 %slice-start.1 = ((s8[6291456]{0:T(1024)(128)(4,1)}), s8[2097152]{0:T(1024)(128)(4,1)S(1)}, s32[]{:S(2)}) async-start(s8[6291456]{0:T(1024)(128)(4,1)} %bitcast.356), calls=%async_computation.3 | async-start | bytes 4194304
  532.9 40.4 %slice-start.2 = ((s8[6291456]{0:T(1024)(128)(4,1)}), s8[4194304]{0:T(1024)(128)(4,1)S(1)}, s32[]{:S(2)}) async-start(s8[6291456]{0:T(1024)(128)(4,1)} %bitcast.358), calls=%async_computation.4 | async-start | bytes 8388608
  554.6 18.7 %copy-start.28 = (f32[24,13]{0,1:T(8,128)S(1)}, f32[24,13]{0,1:T(8,128)}, u32[]{:S(2)}) copy-start(f32[24,13]{0,1:T(8,128)} %get-tuple-element.43) | copy-start | bytes 3748
  554.6 18.7 %slice-start.3 = ((s8[6291456]{0:T(1024)(128)(4,1)}), s8[2097152]{0:T(1024)(128)(4,1)S(1)}, s32[]{:S(2)}) async-start(s8[6291456]{0:T(1024)(128)(4,1)} %bitcast.358), calls=%async_computation.5 | async-start | bytes 4194304
  554.6 37.7 %slice-start.4 = ((s8[6291456]{0:T(1024)(128)(4,1)}), s8[4194304]{0:T(1024)(128)(4,1)S(1)}, s32[]{:S(2)}) async-start(s8[6291456]{0:T(1024)(128)(4,1)} %bitcast.360), calls=%async_computation.6 | async-start | bytes 8388608
  573.3 19.0 %copy-start.27 = (f32[24,13]{0,1:T(8,128)S(1)}, f32[24,13]{0,1:T(8,128)}, u32[]{:S(2)}) copy-start(f32[24,13]{0,1:T(8,128)} %get-tuple-element.42) | copy-start | bytes 3748
  573.3 19.0 %slice-start.5 = ((s8[6291456]{0:T(1024)(128)(4,1)}), s8[2097152]{0:T(1024)(128)(4,1)S(1)}, s32[]{:S(2)}) async-start(s8[6291456]{0:T(1024)(128)(4,1)} %bitcast.360), calls=%async_computation.7 | async-start | bytes 4194304
  573.3 37.8 %slice-start.6 = ((s8[6291456]{0:T(1024)(128)(4,1)}), s8[4194304]{0:T(1024)(128)(4,1)S(1)}, s32[]{:S(2)}) async-start(s8[6291456]{0:T(1024)(128)(4,1)} %bitcast.362), calls=%async_computation.8 | async-start | bytes 8388608
  592.3 18.8 %copy-start.26 = (f32[24,13]{0,1:T(8,128)S(1)}, f32[24,13]{0,1:T(8,128)}, u32[]{:S(2)}) copy-start(f32[24,13]{0,1:T(8,128)} %get-tuple-element.41) | copy-start | bytes 3748
  592.4 18.8 %slice-start.7 = ((s8[6291456]{0:T(1024)(128)(4,1)}), s8[2097152]{0:T(1024)(128)(4,1)S(1)}, s32[]{:S(2)}) async-start(s8[6291456]{0:T(1024)(128)(4,1)} %bitcast.362), calls=%async_computation.9 | async-start | bytes 4194304
  592.4 37.7 %slice-start.8 = ((s8[6291456]{0:T(1024)(128)(4,1)}), s8[4194304]{0:T(1024)(128)(4,1)S(1)}, s32[]{:S(2)}) async-start(s8[6291456]{0:T(1024)(128)(4,1)} %bitcast.364), calls=%async_computation.10 | async-start | bytes 8388608
  611.2 18.9 %copy-start.25 = (f32[24,13]{0,1:T(8,128)S(1)}, f32[24,13]{0,1:T(8,128)}, u32[]{:S(2)}) copy-start(f32[24,13]{0,1:T(8,128)} %get-tuple-element.40) | copy-start | bytes 3748
  611.2 18.9 %slice-start.9 = ((s8[6291456]{0:T(1024)(128)(4,1)}), s8[2097152]{0:T(1024)(128)(4,1)S(1)}, s32[]{:S(2)}) async-start(s8[6291456]{0:T(1024)(128)(4,1)} %bitcast.364), calls=%async_computation.11 | async-start | bytes 4194304
  611.2 37.8 %slice-start.10 = ((s8[6291456]{0:T(1024)(128)(4,1)}), s8[4194304]{0:T(1024)(128)(4,1)S(1)}, s32[]{:S(2)}) async-start(s8[6291456]{0:T(1024)(128)(4,1)} %bitcast.366), calls=%async_computation.12 | async-start | bytes 8388608
  630.1 18.9 %copy-start.24 = (f32[24,13]{0,1:T(8,128)S(1)}, f32[24,13]{0,1:T(8,128)}, u32[]{:S(2)}) copy-start(f32[24,13]{0,1:T(8,128)} %get-tuple-element.39) | copy-start | bytes 3748
  630.1 18.9 %slice-start.11 = ((s8[6291456]{0:T(1024)(128)(4,1)}), s8[2097152]{0:T(1024)(128)(4,1)S(1)}, s32[]{:S(2)}) async-start(s8[6291456]{0:T(1024)(128)(4,1)} %bitcast.366), calls=%async_computation.13 | async-start | bytes 4194304
  630.1 37.8 %slice-start.12 = ((s8[6291456]{0:T(1024)(128)(4,1)}), s8[4194304]{0:T(1024)(128)(4,1)S(1)}, s32[]{:S(2)}) async-start(s8[6291456]{0:T(1024)(128)(4,1)} %bitcast.368), calls=%async_computation.14 | async-start | bytes 8388608
  649.0 18.9 %copy-start.23 = (f32[24,13]{0,1:T(8,128)S(1)}, f32[24,13]{0,1:T(8,128)}, u32[]{:S(2)}) copy-start(f32[24,13]{0,1:T(8,128)} %get-tuple-element.38) | copy-start | bytes 3748
  649.0 18.9 %slice-start.13 = ((s8[6291456]{0:T(1024)(128)(4,1)}), s8[2097152]{0:T(1024)(128)(4,1)S(1)}, s32[]{:S(2)}) async-start(s8[6291456]{0:T(1024)(128)(4,1)} %bitcast.368), calls=%async_computation.15 | async-start | bytes 4194304
  649.0 38.0 %slice-start.14 = ((s8[6291456]{0:T(1024)(128)(4,1)}), s8[4194304]{0:T(1024)(128)(4,1)S(1)}, s32[]{:S(2)}) async-start(s8[6291456]{0:T(1024)(128)(4,1)} %bitcast.370), calls=%async_computation.16 | async-start | bytes 8388608
  667.9 19.1 %copy-start.22 = (f32[24,13]{0,1:T(8,128)S(1)}, f32[24,13]{0,1:T(8,128)}, u32[]{:S(2)}) copy-start(f32[24,13]{0,1:T(8,128)} %get-tuple-element.37) | copy-start | bytes 3748
  667.9 19.1 %slice-start.15 = ((s8[6291456]{0:T(1024)(128)(4,1)}), s8[2097152]{0:T(1024)(128)(4,1)S(1)}, s32[]{:S(2)}) async-start(s8[6291456]{0:T(1024)(128)(4,1)} %bitcast.370), calls=%async_computation.17 | async-start | bytes 4194304
  667.9 37.9 %slice-start.16 = ((s8[6291456]{0:T(1024)(128)(4,1)}), s8[4194304]{0:T(1024)(128)(4,1)S(1)}, s32[]{:S(2)}) async-start(s8[6291456]{0:T(1024)(128)(4,1)} %bitcast.372), calls=%async_computation.18 | async-start | bytes 8388608
  687.0 18.8 %copy-start.21 = (f32[24,13]{0,1:T(8,128)S(1)}, f32[24,13]{0,1:T(8,128)}, u32[]{:S(2)}) copy-start(f32[24,13]{0,1:T(8,128)} %get-tuple-element.36) | copy-start | bytes 3748
  687.0 18.8 %slice-start.17 = ((s8[6291456]{0:T(1024)(128)(4,1)}), s8[2097152]{0:T(1024)(128)(4,1)S(1)}, s32[]{:S(2)}) async-start(s8[6291456]{0:T(1024)(128)(4,1)} %bitcast.372), calls=%async_computation.19 | async-start | bytes 4194304
  687.0 37.6 %slice-start.18 = ((s8[6291456]{0:T(1024)(128)(4,1)}), s8[4194304]{0:T(1024)(128)(4,1)S(1)}, s32[]{:S(2)}) async-start(s8[6291456]{0:T(1024)(128)(4,1)} %bitcast.374), calls=%async_computation.20 | async-start | bytes 8388608
  705.8 18.8 %copy-start.20 = (f32[24,13]{0,1:T(8,128)S(1)}, f32[24,13]{0,1:T(8,128)}, u32[]{:S(2)}) copy-start(f32[24,13]{0,1:T(8,128)} %get-tuple-element.47) | copy-start | bytes 3748
  705.8 18.8 %slice-start.19 = ((s8[6291456]{0:T(1024)(128)(4,1)}), s8[2097152]{0:T(1024)(128)(4,1)S(1)}, s32[]{:S(2)}) async-start(s8[6291456]{0:T(1024)(128)(4,1)} %bitcast.374), calls=%async_computation.21 | async-start | bytes 4194304
  724.6 18.8 %copy-start.19 = (f32[24,13]{0,1:T(8,128)S(1)}, f32[24,13]{0,1:T(8,128)}, u32[]{:S(2)}) copy-start(f32[24,13]{0,1:T(8,128)} %get-tuple-element.35) | copy-start | bytes 3748
  743.4 18.9 %copy-start.9 = (pred[13,16,32,13]{3,1,2,0:T(8,128)(4,1)S(1)}, pred[13,16,32,13]{3,1,2,0:T(8,128)(4,1)}, u32[]{:S(2)}) copy-start(pred[13,16,32,13]{3,1,2,0:T(8,128)(4,1)} %copy.134) | copy-start | bytes 259588
  870.4 10.6 copy-start.8
  952.8 18.1 %slice-start.32 = ((s8[6291456]{0:T(1024)(128)(4,1)}), s8[2097152]{0:T(1024)(128)(4,1)S(1)}, s32[]{:S(2)}) async-start(s8[6291456]{0:T(1024)(128)(4,1)} %bitcast.398), calls=%async_computation.34 | async-start | bytes 4194304
  960.9 10.0 slice-start.33
  970.9 8.1 copy-start.15
  970.9 17.1 %slice-start.30 = ((s8[6291456]{0:T(1024)(128)(4,1)}), s8[4194304]{0:T(1024)(128)(4,1)S(1)}, s32[]{:S(2)}) async-start(s8[6291456]{0:T(1024)(128)(4,1)} %bitcast.394), calls=%async_computation.32 | async-start | bytes 8388608
  979.0 9.0 slice-start.31
  988.0 8.2 copy-start.14
  988.0 17.7 %slice-start.28 = ((s8[6291456]{0:T(1024)(128)(4,1)}), s8[4194304]{0:T(1024)(128)(4,1)S(1)}, s32[]{:S(2)}) async-start(s8[6291456]{0:T(1024)(128)(4,1)} %bitcast.390), calls=%async_computation.30 | async-start | bytes 8388608
  996.2 9.5 slice-start.29
  996.2 17.6 %slice-start.26 = ((s8[6291456]{0:T(1024)(128)(4,1)}), s8[4194304]{0:T(1024)(128)(4,1)S(1)}, s32[]{:S(2)}) async-start(s8[6291456]{0:T(1024)(128)(4,1)} %bitcast.387), calls=%async_computation.28 | async-start | bytes 8388608
  1005.7 8.1 slice-start.27
  1013.8 8.3 copy-start.13
  1013.8 17.4 %slice-start.24 = ((s8[6291456]{0:T(1024)(128)(4,1)}), s8[4194304]{0:T(1024)(128)(4,1)S(1)}, s32[]{:S(2)}) async-start(s8[6291456]{0:T(1024)(128)(4,1)} %bitcast.383), calls=%async_computation.26 | async-start | bytes 8388608
  1022.1 9.1 slice-start.25
  1022.1 9.1 copy-start.12
  1031.2 15.2 %slice-start.20 = ((s8[6291456]{0:T(1024)(128)(4,1)}), s8[4194304]{0:T(1024)(128)(4,1)S(1)}, s32[]{:S(2)}) async-start(s8[6291456]{0:T(1024)(128)(4,1)} %bitcast.376), calls=%async_computation.22 | async-start | bytes 8388608
  1036.6 9.9 slice-start.21
  1036.6 9.9 copy-start.11
  1036.6 15.2 %slice-start.22 = ((s8[6291456]{0:T(1024)(128)(4,1)}), s8[4194304]{0:T(1024)(128)(4,1)S(1)}, s32[]{:S(2)}) async-start(s8[6291456]{0:T(1024)(128)(4,1)} %bitcast.379), calls=%async_computation.24 | async-start | bytes 8388608
  1051.7 8.1 copy-start.10
  (10 other events, 64.7 us)
Sparse Core Ops, SparseCore 0:
  1104.9 78.6 reduce-scatter.1
where the time goes:
time: 1200 us; the launch traced here: 1190 us
  matrix products  511 us (43%)
  local copies, waits for them, and re-layouts  315 us (26%)
  waiting for transfers between devices  190 us (16%)
  other arithmetic  116 us (10%)
  starting transfers between devices  46.3 us (4%)
  between operations  15.8 us (1%)
    dot_general x13, matrix products, shards(): picked = jnp.einsum('inck,bck->incb', raw_score, onehot, precision=highest)  251 us
    dynamic_slice x14, local copies, waits for them, and re-layouts, shards(): lax.dynamic_slice_in_dim(widened_keys[1], row_start, tile_rows, 0)  142 us
    dot_general x13, matrix products, shards(): jnp.einsum('inck,iknh->icnh', spread, values_slab, preferred_element_type...  128 us
    ppermute x6, waiting for transfers between devices, shifted(): lax.ppermute(value, axis, [(source, source + steps) for source in range(l...  111 us
    reshape x13, local copies, waits for them, and re-layouts, shards(): key_strip = key_strip.reshape(tile_rows, key_span, heads_dev, HEAD_DIM)  101 us
    dot_general x13, matrix products, shards(): jnp.einsum('icnh,iknh->inck', query_heads, key_strip, preferred_element_t...  86.8 us
    reduce_scatter x1, waiting for transfers between devices, shards(): lax.psum_scatter(partials, 'head', scatter_dimension=2, tiled=True)  78.8 us
    ppermute x6, starting transfers between devices, shifted(): lax.ppermute(value, axis, [(source, source + steps) for source in range(l...  46.3 us
  transfers between devices with their start and end apart: 7, of which 5 were waited for; matrix products, arithmetic and copies ran while one was open for 3% of the time, Pallas kernels for 0%

commit v1 on v0

v1 whole, which is shorter than its diff:
```python
import math

import jax
import jax.numpy as jnp
from jax import lax
from jax.experimental import pallas as pl
from jax.experimental.pallas import tpu as pltpu
from jax.sharding import PartitionSpec as P


HEAD_DIM = 64
RADIUS_MAX = 6
WINDOW = 13
HALO = 18
MASKED = -1e30
GROUP_HEADS = 4
GROUP_ROWS = 3
LAST_GROUPS = 1


def row_shift(value, steps):
    count = lax.axis_size("row")
    pairs = [(s, s + steps) for s in range(count) if 0 <= s + steps < count]
    return lax.ppermute(value, "row", pairs)


def col_shift_where(value, steps, row_ok):
    rows, cols = lax.axis_size("row"), lax.axis_size("col")
    pairs = [
        (r * cols + c, r * cols + c + steps)
        for r in range(rows)
        if row_ok(r)
        for c in range(cols)
        if 0 <= c + steps < cols
    ]
    return lax.ppermute(value, ("row", "col"), pairs)


def partner(value):
    count = lax.axis_size("row")
    return lax.ppermute(value, "row", [(s, s ^ 1) for s in range(count)])


def head_swap(value):
    return lax.ppermute(value, "head", [(0, 1), (1, 0)])


def head_partner(value):
    rows = lax.axis_size("row")
    pairs = [(2 * r + h, 2 * (r ^ 1) + 1 - h) for r in range(rows) for h in range(2)]
    return lax.ppermute(value, ("row", "head"), pairs)


def row_pair_swap(value):
    return lax.ppermute(value, "row", [(s, s ^ 2) for s in range(4)])


def tables_kernel(dims_ref, dims_row_ref, bias_ref, base_ref, *, slots):
    half = bias_ref.shape[0] // 2
    width = base_ref.shape[2]
    parity = dims_ref[2, 0]
    bias = jnp.where(parity == 0, bias_ref[:half], bias_ref[half:])
    index = lax.broadcasted_iota(jnp.int32, (1, WINDOW * WINDOW), 1)
    column = lax.broadcasted_iota(jnp.int32, (WINDOW * WINDOW, width), 0)
    lane = lax.broadcasted_iota(jnp.int32, (WINDOW * WINDOW, width), 1)
    for tile in range(2):
        radius, dilation = dims_ref[tile, 0], dims_ref[tile, 1]
        pattern = dims_row_ref[tile : tile + 1, 2:]
        up, side = index // WINDOW - RADIUS_MAX, index % WINDOW - RADIUS_MAX
        used = (jnp.abs(up) <= radius) & (jnp.abs(side) <= radius)
        used = used & ((pattern == 1) | ((up == 0) & (side == 0)))
        value = jnp.where(used, bias, MASKED)
        target = column // WINDOW * slots + (column % WINDOW - RADIUS_MAX) * dilation
        target = jnp.where(target < 0, target + width, target)
        spot = jnp.where(target == lane, 1.0, 0.0)
        placed = jnp.dot(value, spot, precision=lax.Precision.HIGHEST, preferred_element_type=jnp.float32)
        taken = jnp.max(spot, axis=0, keepdims=True)
        base_ref[tile] = jnp.where(taken > 0.0, placed, MASKED)


def tables(dims, bias, slots):
    half = bias.shape[0] // 2
    vmem = pl.BlockSpec(memory_space=pltpu.VMEM)

    def body(*refs):
        tables_kernel(*refs, slots=slots)

    return pl.pallas_call(
        body,
        out_shape=jax.ShapeDtypeStruct((2, half, (WINDOW + GROUP_ROWS) * slots), jnp.float32),
        in_specs=[pl.BlockSpec(memory_space=pltpu.SMEM), vmem, vmem],
        out_specs=vmem,
        name="tables",
    )(dims, dims, bias)


def give_half(parity, arrays):
    rows, cols, feats = arrays[0].shape
    half = feats // 2
    block = 4

    def body(parity_ref, *refs):
        for n, source in enumerate(refs[:-1]):
            refs[-1][n] = source[...]

    return pl.pallas_call(
        body,
        grid_spec=pltpu.PrefetchScalarGridSpec(
            num_scalar_prefetch=1,
            grid=(rows // block,),
            in_specs=[pl.BlockSpec((block, cols, half), lambda n, p: (n, 0, 1 - p[0]))] * len(arrays),
            out_specs=pl.BlockSpec((len(arrays), block, cols, half), lambda n, p: (0, n, 0, 0)),
        ),
        out_shape=jax.ShapeDtypeStruct((len(arrays), rows, cols, half), arrays[0].dtype),
        name="give_half",
    )(parity, *arrays)


def pack_kernel(flags_ref, key_ref, value_ref, recv_ref, *refs, low, edges):
    edge_refs, (right_ref, left_ref, mid_ref, sems) = refs[-4 - edges : -4], refs[-4:]
    rows, cols, half = recv_ref.shape[1:]
    feats = right_ref.shape[3]
    own_lanes = pl.ds(pl.multiple_of(flags_ref[0] * half + low, 256), feats)
    got_lanes = slice(low, low + feats)
    spill = HALO - rows

    def source(kv, own, *where):
        if own:
            return (key_ref, value_ref)[kv].at[(*where, own_lanes)]
        return recv_ref.at[(kv, *where, got_lanes)]

    made = []
    middles, others = [], []
    every = slice(None)
    for kv in range(2):
        for n, own in enumerate((True, False)):
            part = slice(n * rows, (n + 1) * rows)
            plans = [
                (source(kv, own, every, slice(cols // 2 - 8, cols // 2 + 8)), mid_ref.at[kv, part]),
                (source(kv, own, every, slice(cols - 16, cols)), right_ref.at[kv, part]),
                (source(kv, own, every, slice(0, 16)), left_ref.at[kv, part]),
            ]
            for index, (start, target) in enumerate(plans):
                copy = pltpu.make_async_copy(start, target, sems.at[len(made)])
                copy.start()
                made.append(copy)
                (others if index else middles).append(copy)
    sem0 = len(made)

    def edge_copies(n, own_near, downward):
        out_ref = edge_refs[n]
        copies = []
        for kv in range(2):
            far_rows = slice(rows - spill, rows) if downward else slice(0, spill)
            index = sem0 + 4 * n + 2 * kv
            copies.append(pltpu.make_async_copy(
                source(kv, own_near, every, every), out_ref.at[kv, 0:rows], sems.at[index]))
            copies.append(pltpu.make_async_copy(
                source(kv, not own_near, far_rows, every), out_ref.at[kv, rows:HALO], sems.at[index + 1]))
        return copies

    for n in range(edges):
        for code in range(4):
            own_near, downward = bool(code & 1), bool(code & 2)

            @pl.when(flags_ref[1 + n] == code)
            def _(n=n, own_near=own_near, downward=downward):
                for copy in edge_copies(n, own_near, downward):
                    copy.start()

    for copy in middles:
        copy.wait()
    for kv in range(2):
        for r in range(2 * rows):
            slot = r * 2
            spot = (kv, 2 * rows + slot // 16, slice(slot % 16, slot % 16 + 2))
            right_ref[spot] = mid_ref[kv, r, 6:8, :]
            left_ref[spot] = mid_ref[kv, r, 8:10, :]
    for copy in others:
        copy.wait()
    for n in range(edges):
        for copy in edge_copies(n, True, True):
            copy.wait()


def pack(flags, key_map, value_map, recv, low, feats, edges, after):
    _, rows, cols, _ = recv.shape
    hbm = pl.BlockSpec(memory_space=pl.ANY)
    vmem = pl.BlockSpec(memory_space=pltpu.VMEM)
    wire = jax.ShapeDtypeStruct((2, 2 * rows + 2 * rows * 2 // 16, 16, feats), recv.dtype)

    def body(*refs):
        pack_kernel(*refs, low=low, edges=edges)

    return pl.pallas_call(
        body,
        out_shape=[jax.ShapeDtypeStruct((2, HALO, cols, feats), recv.dtype)] * edges + [wire, wire],
        in_specs=[pl.BlockSpec(memory_space=pltpu.SMEM), hbm, hbm, hbm] + [hbm] * len(after),
        out_specs=[vmem] * (edges + 2),
        scratch_shapes=[
            pltpu.VMEM((2, 2 * rows, 16, feats), recv.dtype),
            pltpu.SemaphoreType.DMA((12 + 4 * edges,)),
        ],
        compiler_params=pltpu.CompilerParams(vmem_limit_bytes=40 * 1024 * 1024),
        name="pack",
    )(flags, key_map, value_map, recv, *after)


def pack_halo(middle, after):
    _, rows, cols, feats = middle.shape
    vmem = pl.BlockSpec(memory_space=pltpu.VMEM)
    tail = -(-rows * 2 // 16)
    wire = jax.ShapeDtypeStruct((2, rows + tail, 16, feats), middle.dtype)

    def body(in_ref, *refs):
        right_ref, left_ref = refs[-2:]
        for kv in range(2):
            right_ref[kv, 0:rows] = in_ref[kv, :, cols - 16 :, :]
            left_ref[kv, 0:rows] = in_ref[kv, :, 0:16, :]
            for ref in (right_ref, left_ref):
                ref[kv, rows + tail - 1] = jnp.zeros((16, feats), middle.dtype)
            for r in range(rows):
                slot = r * 2
                spot = (kv, rows + slot // 16, slice(slot % 16, slot % 16 + 2))
                right_ref[spot] = in_ref[kv, r, cols - HALO : cols - 16, :]
                left_ref[spot] = in_ref[kv, r, 16:HALO, :]

    return pl.pallas_call(
        body,
        out_shape=[wire, wire],
        in_specs=[vmem] + [pl.BlockSpec(memory_space=pl.ANY)] * len(after),
        out_specs=[vmem, vmem],
        compiler_params=pltpu.CompilerParams(vmem_limit_bytes=40 * 1024 * 1024),
        name="pack_halo",
    )(middle, *after)


def attend_kernel(meta_ref, base_ref, *refs, halos, low, total_cols):
    key_ref, value_ref, query_ref, recv_ref, side_right, side_left = refs[:6]
    halo_refs = refs[6 : 6 + 3 * halos]
    out_ref, slab_ref, q_ref, extra_ref, table_ref, rows_ref, sems = refs[-7:]
    groups, _, slab_rows, slots, feats = slab_ref.shape
    tile_rows, cols = q_ref.shape[2], q_ref.shape[3]
    half = recv_ref.shape[3]
    heads = feats // HEAD_DIM
    width = table_ref.shape[1]
    keys = (WINDOW + GROUP_ROWS - 1) * slots
    block = heads * cols
    own_row, other_row, pair_base, total_rows, own_off = [meta_ref[n] for n in (2, 3, 4, 5, 6)]
    parity, col_anchor = meta_ref[7], meta_ref[8]
    right_slots, extra_slots, left_slots = slice(cols, cols + 16), slice(cols + 16, cols + 32), slice(cols + 32, cols + 48)
    tail = 2 * tile_rows * 2 // 16
    halo_tail = -(-HALO * 2 // 16)

    def places(n):
        if n < 0:
            return [(own_off + own_row, tile_rows, 0), (own_off + other_row, tile_rows, tile_rows)]
        near, far = meta_ref[9 + 2 * n], meta_ref[10 + 2 * n]
        return [(near, tile_rows, 0), (far, HALO - tile_rows, tile_rows)]

    def copies(g):
        got = slice(low + g * feats, low + (g + 1) * feats)
        own = pl.ds(pl.multiple_of(parity * half + low + g * feats, feats), feats)
        here = slice(g * feats, (g + 1) * feats)
        made = []

        def add(source, target):
            made.append(pltpu.make_async_copy(source, target, sems.at[g, len(made)]))

        add(query_ref.at[:, :, own], q_ref.at[g, 0])
        add(recv_ref.at[2, :, :, got], q_ref.at[g, 1])
        for kv in range(2):
            slab = slab_ref.at[g, kv]
            add((key_ref, value_ref)[kv].at[:, :, own], slab.at[pl.ds(own_off + own_row, tile_rows), 0:cols])
            add(recv_ref.at[kv, :, :, got], slab.at[pl.ds(own_off + other_row, tile_rows), 0:cols])
            for n in range(-1, halos):
                if n < 0:
                    right, left, height, extra = side_right, side_left, 2 * tile_rows, 0
                else:
                    middle, right, left = halo_refs[3 * n : 3 * n + 3]
                    height, extra = HALO, tail + n * halo_tail
                for start, count, first in places(n):
                    rows = pl.ds(start, count)
                    part = slice(first, first + count)
                    if n >= 0:
                        add(middle.at[kv, part, :, here], slab.at[rows, 0:cols])
                    add(right.at[kv, part, :, here], slab.at[rows, right_slots])
                    add(left.at[kv, part, :, here], slab.at[rows, left_slots])
                count = tail if n < 0 else halo_tail
                for side, wire in enumerate((right, left)):
                    target = extra_ref.at[g, kv, side, extra : extra + count]
                    add(wire.at[kv, height : height + count, :, here], target)
        return made

    for g in range(groups):
        for copy in copies(g):
            copy.start()

    lane = lax.broadcasted_iota(jnp.int32, (1, width), 1)
    step = jnp.zeros((1, width), jnp.int32)
    for m in range(1, width // slots):
        step = step + jnp.where(lane >= m * slots, 1, 0)
    slot = lane - step * slots
    front_ok = jnp.where((slot < cols + HALO) & (col_anchor + slot < total_cols) & (lane < keys), 1, 0)
    back_ok = jnp.where((slot >= slots - HALO) & (col_anchor + slot >= slots) & (lane < keys), 2, 0)
    ok = jnp.broadcast_to(front_ok + back_ok, (cols, width))
    lane_head = lax.broadcasted_iota(jnp.int32, (cols, feats), 1) // HEAD_DIM
    scale = 1.0 / math.sqrt(HEAD_DIM)

    def fill_extras(g):
        for kv in range(2):
            slab_ref[g, kv, :, extra_slots, :] = jnp.zeros((slab_rows, 16, feats), jnp.bfloat16)
            for n in range(-1, halos):
                origin = 0 if n < 0 else tail + n * halo_tail
                for start, count, first in places(n):
                    for r in range(count):
                        at = (first + r) * 2
                        rows = slice(at % 16, at % 16 + 2)
                        where = origin + at // 16
                        slab_ref[g, kv, start + r, cols + 16 : cols + 18, :] = extra_ref[g, kv, 0, where, rows, :]
                        slab_ref[g, kv, start + r, cols + 30 : cols + 32, :] = extra_ref[g, kv, 1, where, rows, :]

    def one_tile(g, tile):
        dilation = meta_ref[tile]
        tile_row = meta_ref[2 + tile]
        for h in range(heads):
            base = jnp.broadcast_to(base_ref[tile, low // HEAD_DIM + g * heads + h][None, :], (cols, width))
            for n in range(GROUP_ROWS):
                front = pltpu.roll(base, n * slots, 1, stride=1, stride_axis=0)
                back = pltpu.roll(base, (n + 1) * slots, 1, stride=1, stride_axis=0)
                row0 = n * block + h * cols
                table_ref[row0 : row0 + cols, :] = jnp.where(
                    ok == 1, front, jnp.where(ok == 2, back, MASKED)
                )

        def unit(p, carry):
            first = (p // dilation) * (GROUP_ROWS * dilation) + p % dilation
            blocks = []
            for n in range(GROUP_ROWS):
                q_row = q_ref[g, tile, jnp.minimum(first + n * dilation, tile_rows - 1)]
                q_row = q_row.astype(jnp.float32) * scale
                blocks += [jnp.where(lane_head == h, q_row, 0.0).astype(jnp.bfloat16) for h in range(heads)]
            q_block = jnp.concatenate(blocks, axis=0)
            top = tile_row + first - RADIUS_MAX * dilation
            starts = [
                jnp.clip(own_off + top + m * dilation, 0, slab_rows - 1)
                for m in range(WINDOW + GROUP_ROWS - 1)
            ]
            k_rows = jnp.concatenate([slab_ref[g, 0, s] for s in starts], axis=0)
            v_rows = jnp.concatenate([slab_ref[g, 1, s] for s in starts], axis=0)
            scores = lax.dot_general(
                q_block, k_rows, (((1,), (1,)), ((), ())), preferred_element_type=jnp.float32
            )
            key_row = pair_base + top + step * dilation
            outside = jnp.where((key_row >= 0) & (key_row < total_rows), 0.0, MASKED)
            weights, sums = [], []
            for n in range(GROUP_ROWS):
                start = n * slots // 128 * 128
                stop = min(-(-(n + WINDOW) * slots // 128) * 128, keys)
                part = slice(n * block, (n + 1) * block)
                score = scores[part, start:stop] + table_ref[part, start:stop] + outside[:, start:stop]
                peak = jnp.max(score, axis=1, keepdims=True)
                exponent = jnp.exp(score - peak)
                sums.append(jnp.sum(exponent, axis=1, keepdims=True))
                pieces = [exponent.astype(jnp.bfloat16)]
                if start:
                    pieces.insert(0, jnp.zeros((block, start), jnp.bfloat16))
                if stop < keys:
                    pieces.append(jnp.zeros((block, keys - stop), jnp.bfloat16))
                weights.append(jnp.concatenate(pieces, axis=1))
            mixed = jnp.dot(
                jnp.concatenate(weights, axis=0), v_rows, preferred_element_type=jnp.float32
            ) / jnp.concatenate(sums, axis=0)
            for n in range(GROUP_ROWS):
                picked = mixed[n * block : n * block + cols]
                for h in range(1, heads):
                    row0 = n * block + h * cols
                    picked = jnp.where(lane_head == h, mixed[row0 : row0 + cols], picked)
                rows_ref[first + n * dilation] = picked.astype(jnp.bfloat16)
            return carry

        lax.fori_loop(0, -(-tile_rows // GROUP_ROWS), unit, 0, unroll=2)
        out_ref[tile, g] = rows_ref[0:tile_rows]

    for g in range(groups):
        for copy in copies(g):
            copy.wait()
        fill_extras(g)
        lax.fori_loop(0, 2, lambda tile, carry, g=g: (one_tile(g, tile), carry)[1], 0)


def attend(
    meta, base, key_map, value_map, query_map, recv, right, left, halos, after, low, all_feats, total_cols, slots
):
    _, tile_rows, cols, _ = recv.shape
    feats = GROUP_HEADS * HEAD_DIM
    groups = all_feats // feats
    slab_rows = 2 * tile_rows + HALO * len(halos)
    count = 2 * tile_rows * groups * GROUP_HEADS * cols * WINDOW * slots
    hbm = pl.BlockSpec(memory_space=pl.ANY)
    vmem = pl.BlockSpec(memory_space=pltpu.VMEM)
    flat = [array for halo in halos for array in halo] + list(after)
    tails = 2 * tile_rows * 2 // 16 + len(halos) * -(-HALO * 2 // 16)

    def body(*refs):
        attend_kernel(*refs, halos=len(halos), low=low, total_cols=total_cols)

    return pl.pallas_call(
        body,
        out_shape=jax.ShapeDtypeStruct((2, groups, tile_rows, cols, feats), jnp.bfloat16),
        in_specs=[pl.BlockSpec(memory_space=pltpu.SMEM), vmem] + [hbm] * (6 + len(flat)),
        out_specs=vmem,
        scratch_shapes=[
            pltpu.VMEM((groups, 2, slab_rows, slots, feats), jnp.bfloat16),
            pltpu.VMEM((groups, 2, tile_rows, cols, feats), jnp.bfloat16),
            pltpu.VMEM((groups, 2, 2, tails, 16, feats), jnp.bfloat16),
            pltpu.VMEM((GROUP_ROWS * GROUP_HEADS * cols, base.shape[2]), jnp.float32),
            pltpu.VMEM((tile_rows + 8, cols, feats), jnp.bfloat16),
            pltpu.SemaphoreType.DMA((groups, 2 + 2 * (8 + 8 * len(halos)))),
        ],
        compiler_params=pltpu.CompilerParams(vmem_limit_bytes=48 * 1024 * 1024),
        cost_estimate=pl.CostEstimate(
            flops=count * feats * 4, transcendentals=count, bytes_accessed=4 * groups * slab_rows * slots * feats
        ),
        name="attend",
    )(meta, base, key_map, value_map, query_map, recv, right, left, *flat)


def project(spots, pieces, out_weight, far_weights, low, half_feats, before, dtype):
    groups, tokens, feats = pieces[0].shape
    model = far_weights[0].shape[1]
    block = model // 3
    first = low // feats
    per_half = half_feats // feats
    columns = model // block
    whole = pl.BlockSpec((groups, tokens, feats), lambda n, spot: (0, 0, 0))
    column = pl.BlockSpec((tokens, block), lambda n, spot: (0, n))
    specs, arrays = [], []
    for source in range(4):
        for g in range(groups):
            if source < 2:

                def at(n, spot, source=source, g=g):
                    who = spot[0] if source == 0 else 1 - spot[0]
                    return who * per_half + first + g, spot[1] * columns + n

                arrays.append(out_weight)
            else:

                def at(n, spot, g=g):
                    return first + g, n

                arrays.append(far_weights[source - 2])
            specs.append(pl.BlockSpec((feats, block), at))
    extra = [] if before is None else [before]

    def body(spot_ref, *refs):
        lhs, rhs, out_ref = refs[:4], refs[4 : 4 + 4 * groups], refs[-1]
        total = refs[-2][...] if extra else None
        for source in range(4):
            for g in range(groups):
                term = jnp.dot(lhs[source][g], rhs[source * groups + g][...], preferred_element_type=jnp.float32)
                total = term if total is None else total + term
        out_ref[...] = total.astype(out_ref.dtype)

    return pl.pallas_call(
        body,
        grid_spec=pltpu.PrefetchScalarGridSpec(
            num_scalar_prefetch=1,
            grid=(columns,),
            in_specs=[whole] * 4 + specs + [column] * len(extra),
            out_specs=column,
        ),
        out_shape=jax.ShapeDtypeStruct((tokens, model), dtype),
        compiler_params=pltpu.CompilerParams(vmem_limit_bytes=40 * 1024 * 1024),
        cost_estimate=pl.CostEstimate(
            flops=8 * tokens * model * feats * groups,
            transcendentals=0,
            bytes_accessed=8 * model * feats * groups,
        ),
        name="project",
    )(spots, *pieces, *arrays, *extra)


def layer(
    query_map, key_map, value_map, window_mask, tile_radius, dilation_per_tile, rel_bias, out_weight
):
    tile_rows, tile_cols, features_dev = query_map.shape
    half_feats = features_dev // 2
    feats = GROUP_HEADS * HEAD_DIM
    slots = tile_cols + 48
    row_id = lax.axis_index("row")
    parity = row_id % 2
    pair_id = row_id // 2
    rows_count = lax.axis_size("row")
    pairs_count = rows_count // 2
    total_cols = tile_cols * lax.axis_size("col")
    tokens = tile_rows * tile_cols
    head_id = lax.axis_index("head")
    model_half = out_weight.shape[1] // 2

    given = give_half(parity.astype(jnp.int32)[None], (key_map, value_map, query_map))
    recv = partner(given)

    mine = jnp.concatenate([tile_radius[0], dilation_per_tile[0], window_mask[0, 0].reshape(-1)])
    others = partner(mine)
    who = jnp.full_like(mine, parity)
    dims = jnp.stack([mine, others, who])
    base = tables(dims, rel_bias.reshape(rel_bias.shape[0], -1), slots)

    spill = HALO - tile_rows
    pair_rows = 2 * tile_rows
    first_pair = pair_id == 0
    if pairs_count == 1:
        own_off, spots, downs = 0, [], []
    elif pairs_count == 2:
        own_off = jnp.where(first_pair, 0, HALO)
        spots = [jnp.where(first_pair, pair_rows, spill), jnp.where(first_pair, pair_rows + tile_rows, 0)]
        downs = [first_pair.astype(jnp.int32)]
    else:
        own_off = HALO
        spots = [spill, 0, HALO + pair_rows, HALO + pair_rows + tile_rows]
        downs = [1, 0]
    meta = [dims[0, 1], dims[1, 1], parity * tile_rows, (1 - parity) * tile_rows]
    meta += [pair_id * pair_rows, tile_rows * rows_count, own_off, parity]
    meta += [lax.axis_index("col") * tile_cols, *spots]
    meta = jnp.stack([jnp.asarray(item, jnp.int32) for item in meta])
    flags = [parity] + [2 * down + jnp.where(parity == down, 1, 0) for down in downs]
    flags = jnp.stack([jnp.asarray(item, jnp.int32) for item in flags])

    total_groups = half_feats // feats
    spans = [(0, total_groups - LAST_GROUPS), (total_groups - LAST_GROUPS, total_groups)]
    packs, after = [], []
    for low, high in spans:
        packed = pack(
            flags, key_map, value_map, recv, low * feats, (high - low) * feats, len(downs), after
        )
        after = [packed[-1]]
        packs.append(packed)
    ready = []
    for *edges, right, left in packs:
        middles = []
        if pairs_count == 2:
            middles = [(row_pair_swap(edges[0]), lambda r: True)]
        elif pairs_count > 2:
            middles = [
                (row_shift(edges[0], 2), lambda r: r >= 2),
                (row_shift(edges[1], -2), lambda r: r < rows_count - 2),
            ]
        left_in = col_shift_where(right, 1, lambda r: True)
        right_in = col_shift_where(left, -1, lambda r: True)
        halos = []
        for middle, row_ok in middles:
            right_out, left_out = pack_halo(middle, after)
            after = [left_out]
            halos.append(
                (middle, col_shift_where(left_out, -1, row_ok), col_shift_where(right_out, 1, row_ok))
            )
        ready.append((right_in, left_in, halos))

    give = lax.dynamic_slice(out_weight, (parity * half_feats, (1 - head_id) * model_half), (half_feats, model_half))
    far_weight = head_swap(give)
    corner = jnp.stack([parity, head_id]).astype(jnp.int32)

    exchanged = []
    for (low, high), (right_in, left_in, halos) in zip(spans, ready):
        done = attend(
            meta, base, key_map, value_map, query_map, recv, right_in, left_in, halos, after,
            low * feats, (high - low) * feats, total_cols, slots,
        )
        if not exchanged:
            far_weights = [far_weight, partner(lax.optimization_barrier((far_weight, done))[0])]
        after = [done]
        own, other = done[0], done[1]
        pieces = [own, partner(other), head_swap(own), head_partner(other)]
        exchanged.append([piece.reshape(high - low, tokens, feats) for piece in pieces])
    acc = None
    for (low, high), pieces in zip(spans, exchanged):
        dtype = jnp.bfloat16 if high == total_groups else jnp.float32
        acc = project(corner, pieces, out_weight, far_weights, low * feats, half_feats, acc, dtype)
    return acc.reshape(tile_rows, tile_cols, model_half)


def solution(mesh):
    placed = (
        P("row", "col", "head"),
        P("row", "col", "head"),
        P("row", "col", "head"),
        P("row", "col", None, None),
        P("row", "col"),
        P("row", "col"),
        P("head", None, None),
        P("head", None),
    )
    return jax.shard_map(layer, mesh=mesh, in_specs=placed, out_specs=P("row", "col", "head"), check_vma=False)
```

time: 1200 us -> 172 us (0.14)
  matrix products: 511 us -> 0 us
  local copies, waits for them, and re-layouts: 315 us -> 13.6 us
  waiting for transfers between devices: 190 us -> 43.3 us
  other arithmetic: 116 us -> 0.92 us
  Pallas kernels: 0 us -> 77 us
  between operations: 15.8 us -> 1.54 us
  starting transfers between devices: 46.3 us -> 34.2 us
    dot_general x53 -> x0, matrix products: 511 us -> none  [the longest x13 251 us: shards(): picked = jnp.einsum('inck,bck->incb', raw_score, onehot, precision=highest)]
    dynamic_slice x14 -> x1, local copies, waits for them, and re-layouts: 142 us -> 3.39 us  [layer(): lax.dynamic_slice(out_weight, (parity * half_feats, (1 - head_id) * model...]
    reshape x14 -> x2, local copies, waits for them, and re-layouts: 105 us -> 3.1 us  [layer(): base = tables(dims, rel_bias.reshape(rel_bias.shape[0], -1), slots)]
    reduce_scatter x1 -> x0, waiting for transfers between devices: 78.8 us -> none  [shards(): lax.psum_scatter(partials, 'head', scatter_dimension=2, tiled=True)]
    pallas_call x0 -> x10, Pallas kernels: none -> 77 us  [the longest x2 49.4 us: attend(): pl.pallas_call(body, out_shape=jax.ShapeDtypeStruct((2, groups, tile_rows...]
    ppermute x6 -> x20, waiting for transfers between devices: 111 us -> 43.3 us  [the longest x2 16.8 us: row_pair_swap(): return lax.ppermute(value, 'row', [(s, s ^ 2) for s in range(4)])]
    slice x6 -> x2, local copies, waits for them, and re-layouts: 38.4 us -> 1.26 us  [the longest x1 0.66 us: layer(): dims[1, 1]]
    convert_element_type x2 -> x0, other arithmetic: 29.2 us -> none  [the longest x1 26 us: shards(): weights = (exponent / denominator).astype(jnp.bfloat16)]
  transfers between devices with their start and end apart: 7 -> 20, of which waited for: 5 -> 9; matrix products, arithmetic and copies ran while one was open for 3% -> 6% of each run, Pallas kernels for 0% -> 37%
where the time goes in v1:
time: 172 us; the launch traced here: 171 us
  Pallas kernels  77 us (45%)
  waiting for transfers between devices  43.3 us (25%)
  starting transfers between devices  34.2 us (20%)
  local copies, waits for them, and re-layouts  13.6 us (8%)
    pallas_call x2, Pallas kernels, attend(): pl.pallas_call(body, out_shape=jax.ShapeDtypeStruct((2, groups, tile_rows...  49.4 us
    ppermute x8, starting transfers between devices, col_shift_where(): return lax.ppermute(value, ('row', 'col'), pairs)  25 us
    ppermute x2, waiting for transfers between devices, row_pair_swap(): return lax.ppermute(value, 'row', [(s, s ^ 2) for s in range(4)])  16.8 us
    ppermute x8, waiting for transfers between devices, col_shift_where(): return lax.ppermute(value, ('row', 'col'), pairs)  15.8 us
    pallas_call x2, Pallas kernels, project(): pl.pallas_call(body, grid_spec=pltpu.PrefetchScalarGridSpec(num_scalar_pr...  11 us
    pallas_call x2, Pallas kernels, pack(): pl.pallas_call(body, out_shape=[jax.ShapeDtypeStruct((2, HALO, cols, feat...  7.51 us
    ppermute x3, waiting for transfers between devices, head_swap(): return lax.ppermute(value, 'head', [(0, 1), (1, 0)])  6.23 us
    ppermute x5, waiting for transfers between devices, partner(): return lax.ppermute(value, 'row', [(s, s ^ 1) for s in range(count)])  4.44 us
  transfers between devices with their start and end apart: 20, of which 9 were waited for; matrix products, arithmetic and copies ran while one was open for 6% of the time, Pallas kernels for 37%

profile of v1, /device:TPU:0, one launch (start us, length us, event | category | flops | bytes accessed | tf_op | source)
XLA Modules:
  0.0 170.5 jit_solution(7020172691268640271)
XLA Ops:
  0.0 4.1 %give_half.1 = bf16[3,16,32,768]{3,2,1,0:T(8,128)(2,1)} custom-call(s32[1]{0:T(128)} %bitcast.parity_ref, bf16[16,32,1536]{2,1,0:T(8,128)(2,1)} %refs_2_.9, bf16[16,32,1536]{2,1,0:T(8,128)(2,1)} %refs_3_.3, bf16[16,32,1536]{2,1,0:T(8,128)(2,1)} %refs_4_.5), custom_call_target="tpu_custom_call" | custom-call | tf_op jit(solution)/shard_map/give_half/pallas_call | solution.py:106
  4.1 0.5 collective-permute-start.1
  4.6 0.1 pad_add_fusion.2.refs_0_
  4.7 4.4 %collective-permute-done.1.refs_3_.refs_5_ = bf16[3,16,32,768]{3,2,1,0:T(8,128)(2,1)} collective-permute-done((bf16[3,16,32,768]{3,2,1,0:T(8,128)(2,1)}, bf16[3,16,32,768]{3,2,1,0:T(8,128)(2,1)}, u32[]{:S(2)}, u32[]{:S(2)}) %collective-permute-start.1) | collective-permute-done | bytes 2359328 | tf_op jit(solution)/shard_map/ppermute | solution.py:41
  9.1 4.5 %pack.2 = (bf16[2,18,32,512]{3,2,1,0:T(8,128)(2,1)}, bf16[2,36,16,512]{3,2,1,0:T(8,128)(2,1)}, bf16[2,36,16,512]{3,2,1,0:T(8,128)(2,1)}) custom-call(s32[2]{0:T(128)S(1)} %pad_add_fusion.2.refs_0_, bf16[16,32,1536]{2,1,0:T(8,128)(2,1)S(1)} %copy-done, bf16[16,32,1536]{2,1,0:T(8,128)(2,1)S(1)} %copy-done.3, ...), custom_call_target="tpu_custom_call" | custom-call | tf_op jit(solution)/shard_map/pack/pallas_call | solution.py:195
  13.6 2.4 %collective-permute-start.5 = (bf16[2,18,32,512]{3,2,1,0:T(8,128)(2,1)}, bf16[2,18,32,512]{3,2,1,0:T(8,128)(2,1)S(1)}, u32[]{:S(2)}, u32[]{:S(2)}) collective-permute-start(bf16[2,18,32,512]{3,2,1,0:T(8,128)(2,1)} %get-tuple-element.20), channel_id=1, source_target_pairs={{0,16},{8,24},{16,0},{24,8},{1,17},{9,25},{17,1},{25,9},{2,18},{10... | collective-permute-start | bytes 3538952 | tf_op jit(solution)/shard_map/ppermute | solution.py:55
  16.1 3.4 %dynamic_slice.3 = bf16[768,1536]{1,0:T(8,128)(2,1)} dynamic-slice(bf16[1536,3072]{1,0:T(8,128)(2,1)} %refs_5_.3, s32[]{:T(128)S(6)} %select_n.36, s32[]{:T(128)S(6)} %select_n.37), dynamic_slice_sizes={768,1536} | dynamic-slice | bytes 4718596 | tf_op jit(solution)/shard_map/dynamic_slice | solution.py:561
  19.5 1.5 collective-permute-start.15
  21.0 3.0 %pack.3 = (bf16[2,18,32,256]{3,2,1,0:T(8,128)(2,1)}, bf16[2,36,16,256]{3,2,1,0:T(8,128)(2,1)S(1)}, bf16[2,36,16,256]{3,2,1,0:T(8,128)(2,1)S(1)}) custom-call(s32[2]{0:T(128)S(1)} %pad_add_fusion.2.refs_0_, bf16[16,32,1536]{2,1,0:T(8,128)(2,1)S(1)} %copy-done.1, bf16[16,32,1536]{2,1,0:T(8,128)(2,1)S(1)} %copy-done.4, ...), custom_call_target="tpu_custom_call" | custom-call | tf_op jit(solution)/shard_map/pack/pallas_call | solution.py:195
  24.0 0.8 copy-done.6
  24.8 0.8 copy-done.10
  25.7 0.8 collective-permute-start.4
  26.5 1.3 collective-permute-start.8
  27.7 5.7 %collective-permute-start.9 = (bf16[2,36,16,512]{3,2,1,0:T(8,128)(2,1)}, bf16[2,36,16,512]{3,2,1,0:T(8,128)(2,1)}, u32[]{:S(2)}, u32[]{:S(2)}) collective-permute-start(bf16[2,36,16,512]{3,2,1,0:T(8,128)(2,1)} %get-tuple-element.24), channel_id=1, source_target_pairs={{0,2},{2,4},{4,6},{8,10},{10,12},{12,14},{16,18},{18,20},{20,22},{... | collective-permute-start | bytes 3538952 | tf_op jit(solution)/shard_map/ppermute | solution.py:36
  33.4 0.1 reshape_squeeze.9
  34.8 0.1 pad_add_fusion
  34.9 8.2 %collective-permute-done.5.in_ref.refs_8_ = bf16[2,18,32,512]{3,2,1,0:T(8,128)(2,1)S(1)} collective-permute-done((bf16[2,18,32,512]{3,2,1,0:T(8,128)(2,1)}, bf16[2,18,32,512]{3,2,1,0:T(8,128)(2,1)S(1)}, u32[]{:S(2)}, u32[]{:S(2)}) %collective-permute-start.5) | collective-permute-done | bytes 1179680 | tf_op jit(solution)/shard_map/ppermute | solution.py:55
  43.1 0.1 collective-permute-start
  43.2 1.4 copy-done.7
  44.6 1.2 pack_halo.2
  45.8 0.0 collective-permute-done
  45.8 1.3 collective-permute-start.10
  47.1 8.6 %collective-permute-done.4.in_ref.refs_8_ = bf16[2,18,32,256]{3,2,1,0:T(8,128)(2,1)} collective-permute-done((bf16[2,18,32,256]{3,2,1,0:T(8,128)(2,1)}, bf16[2,18,32,256]{3,2,1,0:T(8,128)(2,1)}, u32[]{:S(2)}, u32[]{:S(2)}) %collective-permute-start.4) | collective-permute-done | bytes 589856 | tf_op jit(solution)/shard_map/ppermute | solution.py:55
  55.8 4.3 %collective-permute-start.11 = (bf16[2,21,16,512]{3,2,1,0:T(8,128)(2,1)}, bf16[2,21,16,512]{3,2,1,0:T(8,128)(2,1)}, u32[]{:S(2)}, u32[]{:S(2)}) collective-permute-start(bf16[2,21,16,512]{3,2,1,0:T(8,128)(2,1)} %get-tuple-element.25), channel_id=1, source_target_pairs={{0,2},{2,4},{4,6},{8,10},{10,12},{12,14},{16,18},{18,20},{20,22},{... | collective-permute-start | bytes 2064392 | tf_op jit(solution)/shard_map/ppermute | solution.py:36
  60.1 0.1 pad.4.clone
  60.2 0.6 slice.24
  60.8 1.5 reshape.24
  62.3 1.6 copy.10.refs_2_
  63.9 0.7 slice.25
  64.5 0.7 add_add_fusion.refs_0_.refs_1_
  65.2 2.6 %tables.1.refs_1_ = f32[2,12,1280]{2,1,0:T(8,128)} custom-call(s32[3,171]{1,0:T(4,128)} %add_add_fusion.refs_0_.refs_1_, s32[3,171]{1,0:T(4,128)} %add_add_fusion.refs_0_.refs_1_, f32[24,169]{1,0:T(8,128)} %copy.10.refs_2_), custom_call_target="tpu_custom_call" | custom-call | tf_op jit(solution)/shard_map/tables/pallas_call | solution.py:88
  67.8 1.4 stack.62.refs_0_
  69.2 1.1 pack_halo.3
  70.4 0.0 collective-permute-done.8.refs_6_
  70.4 0.0 collective-permute-done.9.refs_7_
  70.4 0.2 collective-permute-done.10.refs_9_
  70.6 2.8 %collective-permute-done.11.refs_10_ = bf16[2,21,16,512]{3,2,1,0:T(8,128)(2,1)} collective-permute-done((bf16[2,21,16,512]{3,2,1,0:T(8,128)(2,1)}, bf16[2,21,16,512]{3,2,1,0:T(8,128)(2,1)}, u32[]{:S(2)}, u32[]{:S(2)}) %collective-permute-start.11) | collective-permute-done | bytes 688160 | tf_op jit(solution)/shard_map/ppermute | solution.py:36
  73.4 0.9 copy-done.9
  74.4 32.4 %attend.2.refs_11_ = bf16[2,2,16,32,256]{4,3,2,1,0:T(8,128)(2,1)S(1)} custom-call(s32[11]{0:T(128)S(1)} %stack.62.refs_0_, f32[2,12,1280]{2,1,0:T(8,128)S(1)} %copy-done.9, bf16[16,32,1536]{2,1,0:T(8,128)(2,1)} %refs_2_.9, bf16[16,32,1536]{2,1,0:T(8,128)(2,1)} %refs_3_.3, bf16[16,32,1536]{2,1,0:T(8,128)(2,1)} %refs_4_.5, ...), custom_call_target="tpu_custom_call" | custom-call | flops 8724152320 | bytes 8192000 | tf_op jit(solution)/shard_map/attend/pallas_call | solution.py:408
  106.8 0.0 copy-start.2
  106.8 0.1 collective-permute-start.16
  106.9 1.4 collective-permute-start.2
  108.3 5.0 %collective-permute-start.3 = (bf16[2,36,16,256]{3,2,1,0:T(8,128)(2,1)S(1)}, bf16[2,36,16,256]{3,2,1,0:T(8,128)(2,1)S(1)}, u32[]{:S(2)}, u32[]{:S(2)}) collective-permute-start(bf16[2,36,16,256]{3,2,1,0:T(8,128)(2,1)S(1)} %copy-done.11), channel_id=1, source_target_pairs={{0,2},{2,4},{4,6},{8,10},{10,12},{12,14},{16,18},{18,20},{20,22},{... | collective-permute-start | bytes 1769480 | tf_op jit(solution)/shard_map/ppermute | solution.py:36
  113.3 1.3 collective-permute-start.6
  114.6 4.7 %collective-permute-start.7 = (bf16[2,21,16,256]{3,2,1,0:T(8,128)(2,1)S(1)}, bf16[2,21,16,256]{3,2,1,0:T(8,128)(2,1)S(1)}, u32[]{:S(2)}, u32[]{:S(2)}) collective-permute-start(bf16[2,21,16,256]{3,2,1,0:T(8,128)(2,1)S(1)} %get-tuple-element.23), channel_id=1, source_target_pairs={{0,2},{2,4},{4,6},{8,10},{10,12},{12,14},{16,18},{18,20},{20,22},{... | collective-permute-start | bytes 1032200 | tf_op jit(solution)/shard_map/ppermute | solution.py:36
  119.4 0.1 pad_add_fusion.1.spot_ref
  119.4 0.2 slice_bitcast_fusion.3
  119.6 5.9 %collective-permute-done.2.refs_6_ = bf16[2,36,16,256]{3,2,1,0:T(8,128)(2,1)S(1)} collective-permute-done((bf16[2,36,16,256]{3,2,1,0:T(8,128)(2,1)S(1)}, bf16[2,36,16,256]{3,2,1,0:T(8,128)(2,1)S(1)}, u32[]{:S(2)}, u32[]{:S(2)}) %collective-permute-start.2) | collective-permute-done | bytes 589856 | tf_op jit(solution)/shard_map/ppermute | solution.py:36
  125.5 0.0 collective-permute-start.17
  125.5 1.5 collective-permute-done.3.refs_7_
  127.0 0.2 collective-permute-start.19
  127.1 5.4 %collective-permute-done.6.refs_9_ = bf16[2,21,16,256]{3,2,1,0:T(8,128)(2,1)S(1)} collective-permute-done((bf16[2,21,16,256]{3,2,1,0:T(8,128)(2,1)S(1)}, bf16[2,21,16,256]{3,2,1,0:T(8,128)(2,1)S(1)}, u32[]{:S(2)}, u32[]{:S(2)}) %collective-permute-start.6) | collective-permute-done | bytes 344096 | tf_op jit(solution)/shard_map/ppermute | solution.py:36
  132.5 1.5 collective-permute-start.18
  134.0 0.0 collective-permute-done.7.refs_10_
  134.1 17.0 %attend.3 = bf16[2,1,16,32,256]{4,3,2,1,0:T(8,128)(2,1)S(1)} custom-call(s32[11]{0:T(128)S(1)} %stack.62.refs_0_, f32[2,12,1280]{2,1,0:T(8,128)S(1)} %copy-done.9, bf16[16,32,1536]{2,1,0:T(8,128)(2,1)S(1)} %copy-done.2, bf16[16,32,1536]{2,1,0:T(8,128)(2,1)} %refs_3_.3, bf16[16,32,1536]{2,1,0:T(8,128)(2,1)} %refs_4_.5, ...), custom_call_target="tpu_custom_call" | custom-call | flops 4362076160 | bytes 4096000 | tf_op jit(solution)/shard_map/attend/pallas_call | solution.py:408
  151.0 0.1 slice_bitcast_fusion.2
  151.1 0.1 collective-permute-start.12
  151.2 0.0 collective-permute-done.17
  151.2 1.3 collective-permute-start.14
  152.4 0.9 collective-permute-start.13
  153.3 5.9 %project.2.refs_8_ = f32[512,1536]{1,0:T(8,128)S(1)} custom-call(s32[2]{0:T(128)S(1)} %pad_add_fusion.1.spot_ref, bf16[2,512,256]{2,1,0:T(8,128)(2,1)S(1)} %bitcast.38, bf16[2,512,256]{2,1,0:T(8,128)(2,1)S(1)} %bitcast.40, bf16[2,512,256]{2,1,0:T(8,128)(2,1)S(1)} %bitcast.42, bf16[2,512,256]{2,1,0:T(8,128)(2,1)S(1)} %bitcast.41, bf16[1536,3072]{1,0:T(8,128)(2,1)} %refs_5_.3, ...), custom_call_target="tpu_custom_call" | custom-call | flops 3221225472 | bytes 6291456 | tf_op jit(solution)/shard_map/project/pallas_call | solution.py:466
  159.2 0.0 collective-permute-done.12
  159.2 6.2 %collective-permute-done.13 = bf16[1,16,32,256]{3,2,1,0:T(8,128)(2,1)S(1)} collective-permute-done((bf16[1,16,32,256]{3,2,1,0:T(8,128)(2,1)S(1)}, bf16[1,16,32,256]{3,2,1,0:T(8,128)(2,1)S(1)}, u32[]{:S(2)}, u32[]{:S(2)}) %collective-permute-start.13) | collective-permute-done | bytes 262176 | tf_op jit(solution)/shard_map/ppermute | solution.py:45
  165.5 5.0 %project.3 = bf16[512,1536]{1,0:T(8,128)(2,1)} custom-call(s32[2]{0:T(128)S(1)} %pad_add_fusion.1.spot_ref, bf16[1,512,256]{2,1,0:T(8,128)(2,1)S(1)} %bitcast.39, bf16[1,512,256]{2,1,0:T(8,128)(2,1)S(1)} %bitcast.43, bf16[1,512,256]{2,1,0:T(8,128)(2,1)S(1)} %bitcast.45, bf16[1,512,256]{2,1,0:T(8,128)(2,1)S(1)} %bitcast.44, bf16[1536,3072]{1,0:T(8,128)(2,1)} %refs_5_.3, ...), custom_call_target="tpu_custom_call" | custom-call | flops 1610612736 | bytes 3145728 | tf_op jit(solution)/shard_map/project/pallas_call | solution.py:466
  (27 shorter events, 0.1 us)
Async XLA Ops:
  0.0 9.1 %copy-start = (bf16[16,32,1536]{2,1,0:T(8,128)(2,1)S(1)}, bf16[16,32,1536]{2,1,0:T(8,128)(2,1)}, u32[]{:S(2)}) copy-start(bf16[16,32,1536]{2,1,0:T(8,128)(2,1)} %refs_2_.9) | copy-start | bytes 4718596
  0.0 9.1 %copy-start.3 = (bf16[16,32,1536]{2,1,0:T(8,128)(2,1)S(1)}, bf16[16,32,1536]{2,1,0:T(8,128)(2,1)}, u32[]{:S(2)}) copy-start(bf16[16,32,1536]{2,1,0:T(8,128)(2,1)} %refs_3_.3) | copy-start | bytes 4718596
  4.1 5.0 %collective-permute-start.1 = (bf16[3,16,32,768]{3,2,1,0:T(8,128)(2,1)}, bf16[3,16,32,768]{3,2,1,0:T(8,128)(2,1)}, u32[]{:S(2)}, u32[]{:S(2)}) collective-permute-start(bf16[3,16,32,768]{3,2,1,0:T(8,128)(2,1)} %give_half.1), channel_id=1, source_target_pairs={{0,8},{8,0},{16,24},{24,16},{1,9},{9,1},{17,25},{25,17},{2,10},{10... | collective-permute-start | bytes 7077896 | tf_op jit(solution)/shard_map/ppermute | solution.py:41
  13.6 29.5 %collective-permute-start.5 = (bf16[2,18,32,512]{3,2,1,0:T(8,128)(2,1)}, bf16[2,18,32,512]{3,2,1,0:T(8,128)(2,1)S(1)}, u32[]{:S(2)}, u32[]{:S(2)}) collective-permute-start(bf16[2,18,32,512]{3,2,1,0:T(8,128)(2,1)} %get-tuple-element.20), channel_id=1, source_target_pairs={{0,16},{8,24},{16,0},{24,8},{1,17},{9,25},{17,1},{25,9},{2,18},{10... | collective-permute-start | bytes 3538952 | tf_op jit(solution)/shard_map/ppermute | solution.py:55
  16.1 4.9 %copy-start.1 = (bf16[16,32,1536]{2,1,0:T(8,128)(2,1)S(1)}, bf16[16,32,1536]{2,1,0:T(8,128)(2,1)}, u32[]{:S(2)}) copy-start(bf16[16,32,1536]{2,1,0:T(8,128)(2,1)} %refs_2_.9) | copy-start | bytes 4718596
  16.1 4.9 %copy-start.4 = (bf16[16,32,1536]{2,1,0:T(8,128)(2,1)S(1)}, bf16[16,32,1536]{2,1,0:T(8,128)(2,1)}, u32[]{:S(2)}) copy-start(bf16[16,32,1536]{2,1,0:T(8,128)(2,1)} %refs_3_.3) | copy-start | bytes 4718596
  19.5 87.3 %collective-permute-start.15 = (bf16[768,1536]{1,0:T(8,128)(2,1)}, bf16[768,1536]{1,0:T(8,128)(2,1)S(1)}, u32[]{:S(2)}, u32[]{:S(2)}) collective-permute-start(bf16[768,1536]{1,0:T(8,128)(2,1)} %dynamic_slice.3), channel_id=1, source_target_pairs={{0,1},{1,0},{2,3},{3,2},{4,5},{5,4},{6,7},{7,6},{8,9},{9,8},{10,11... | collective-permute-start | bytes 7077896 | tf_op jit(solution)/shard_map/ppermute | solution.py:45
  21.0 12.4 %copy-start.12 = (s32[1,1,13,13]{3,1,2,0:T(1,128)S(1)}, s32[1,1,13,13]{3,1,2,0:T(1,128)}, u32[]{:S(2)}) copy-start(s32[1,1,13,13]{3,1,2,0:T(1,128)} %param.11) | copy-start | bytes 2032
  24.0 0.8 copy-start.6
  24.8 0.8 copy-start.10
  25.7 30.1 %collective-permute-start.4 = (bf16[2,18,32,256]{3,2,1,0:T(8,128)(2,1)}, bf16[2,18,32,256]{3,2,1,0:T(8,128)(2,1)}, u32[]{:S(2)}, u32[]{:S(2)}) collective-permute-start(bf16[2,18,32,256]{3,2,1,0:T(8,128)(2,1)} %get-tuple-element.19), channel_id=1, source_target_pairs={{0,16},{8,24},{16,0},{24,8},{1,17},{9,25},{17,1},{25,9},{2,18},{10... | collective-permute-start | bytes 1769480 | tf_op jit(solution)/shard_map/ppermute | solution.py:55
  26.5 43.9 %collective-permute-start.8 = (bf16[2,36,16,512]{3,2,1,0:T(8,128)(2,1)}, bf16[2,36,16,512]{3,2,1,0:T(8,128)(2,1)}, u32[]{:S(2)}, u32[]{:S(2)}) collective-permute-start(bf16[2,36,16,512]{3,2,1,0:T(8,128)(2,1)} %get-tuple-element.16.refs_4_), channel_id=1, source_target_pairs={{2,0},{4,2},{6,4},{10,8},{12,10},{14,12},{18,16},{20,18},{22,20},{... | collective-permute-start | bytes 3538952 | tf_op jit(solution)/shard_map/ppermute | solution.py:36
  27.7 42.6 %collective-permute-start.9 = (bf16[2,36,16,512]{3,2,1,0:T(8,128)(2,1)}, bf16[2,36,16,512]{3,2,1,0:T(8,128)(2,1)}, u32[]{:S(2)}, u32[]{:S(2)}) collective-permute-start(bf16[2,36,16,512]{3,2,1,0:T(8,128)(2,1)} %get-tuple-element.24), channel_id=1, source_target_pairs={{0,2},{2,4},{4,6},{8,10},{10,12},{12,14},{16,18},{18,20},{20,22},{... | collective-permute-start | bytes 3538952 | tf_op jit(solution)/shard_map/ppermute | solution.py:36
  43.1 27.3 %copy-start.5 = (bf16[2,18,32,512]{3,2,1,0:T(8,128)(2,1)}, bf16[2,18,32,512]{3,2,1,0:T(8,128)(2,1)S(1)}, u32[]{:S(2)}) copy-start(bf16[2,18,32,512]{3,2,1,0:T(8,128)(2,1)S(1)} %collective-permute-done.5.in_ref.refs_8_) | copy-start | bytes 3538948
  43.1 2.7 %collective-permute-start = (s32[171]{0:T(256)S(1)}, s32[171]{0:T(256)S(1)}, u32[]{:S(2)}, u32[]{:S(2)}) collective-permute-start(s32[171]{0:T(256)S(1)} %pad_add_fusion), channel_id=1, source_target_pairs={{0,8},{8,0},{16,24},{24,16},{1,9},{9,1},{17,25},{25,17},{2,10},{10... | collective-permute-start | bytes 2060 | tf_op jit(solution)/shard_map/ppermute | solution.py:41
  43.2 1.4 copy-start.7
  45.8 24.8 %collective-permute-start.10 = (bf16[2,21,16,512]{3,2,1,0:T(8,128)(2,1)}, bf16[2,21,16,512]{3,2,1,0:T(8,128)(2,1)}, u32[]{:S(2)}, u32[]{:S(2)}) collective-permute-start(bf16[2,21,16,512]{3,2,1,0:T(8,128)(2,1)} %get-tuple-element.21.refs_0_), channel_id=1, source_target_pairs={{2,0},{4,2},{6,4},{10,8},{12,10},{14,12},{18,16},{20,18},{22,20},{... | collective-permute-start | bytes 2064392 | tf_op jit(solution)/shard_map/ppermute | solution.py:36
  55.8 17.7 %collective-permute-start.11 = (bf16[2,21,16,512]{3,2,1,0:T(8,128)(2,1)}, bf16[2,21,16,512]{3,2,1,0:T(8,128)(2,1)}, u32[]{:S(2)}, u32[]{:S(2)}) collective-permute-start(bf16[2,21,16,512]{3,2,1,0:T(8,128)(2,1)} %get-tuple-element.25), channel_id=1, source_target_pairs={{0,2},{2,4},{4,6},{8,10},{10,12},{12,14},{16,18},{18,20},{20,22},{... | collective-permute-start | bytes 2064392 | tf_op jit(solution)/shard_map/ppermute | solution.py:36
  73.4 0.9 copy-start.9
  74.3 32.5 %copy-start.8 = (bf16[2,36,16,256]{3,2,1,0:T(8,128)(2,1)S(1)}, bf16[2,36,16,256]{3,2,1,0:T(8,128)(2,1)}, u32[]{:S(2)}) copy-start(bf16[2,36,16,256]{3,2,1,0:T(8,128)(2,1)} %copy-done.6) | copy-start | bytes 1769476
  74.4 34.0 %copy-start.11 = (bf16[2,36,16,256]{3,2,1,0:T(8,128)(2,1)S(1)}, bf16[2,36,16,256]{3,2,1,0:T(8,128)(2,1)}, u32[]{:S(2)}) copy-start(bf16[2,36,16,256]{3,2,1,0:T(8,128)(2,1)} %copy-done.10) | copy-start | bytes 1769476
  106.8 27.3 %copy-start.2 = (bf16[16,32,1536]{2,1,0:T(8,128)(2,1)S(1)}, bf16[16,32,1536]{2,1,0:T(8,128)(2,1)}, u32[]{:S(2)}) copy-start(bf16[16,32,1536]{2,1,0:T(8,128)(2,1)} %refs_2_.9) | copy-start | bytes 4718596
  106.8 46.5 %collective-permute-start.16 = (bf16[768,1536]{1,0:T(8,128)(2,1)S(1)}, bf16[768,1536]{1,0:T(8,128)(2,1)S(1)}, u32[]{:S(2)}, u32[]{:S(2)}) collective-permute-start(bf16[768,1536]{1,0:T(8,128)(2,1)S(1)} %collective-permute-done.15.refs_8_.refs_9_.refs_6_), channel_id=1, source_target_pairs={{0,8},{8,0},{16,24},{24,16},{1,9},{9,1},{17,25},{25,17},{2,10},{10... | collective-permute-start | bytes 7077896 | tf_op jit(solution)/shard_map/ppermute | solution.py:41
  106.9 18.6 %collective-permute-start.2 = (bf16[2,36,16,256]{3,2,1,0:T(8,128)(2,1)S(1)}, bf16[2,36,16,256]{3,2,1,0:T(8,128)(2,1)S(1)}, u32[]{:S(2)}, u32[]{:S(2)}) collective-permute-start(bf16[2,36,16,256]{3,2,1,0:T(8,128)(2,1)S(1)} %copy-done.8), channel_id=1, source_target_pairs={{2,0},{4,2},{6,4},{10,8},{12,10},{14,12},{18,16},{20,18},{22,20},{... | collective-permute-start | bytes 1769480 | tf_op jit(solution)/shard_map/ppermute | solution.py:36
  108.3 18.6 %collective-permute-start.3 = (bf16[2,36,16,256]{3,2,1,0:T(8,128)(2,1)S(1)}, bf16[2,36,16,256]{3,2,1,0:T(8,128)(2,1)S(1)}, u32[]{:S(2)}, u32[]{:S(2)}) collective-permute-start(bf16[2,36,16,256]{3,2,1,0:T(8,128)(2,1)S(1)} %copy-done.11), channel_id=1, source_target_pairs={{0,2},{2,4},{4,6},{8,10},{10,12},{12,14},{16,18},{18,20},{20,22},{... | collective-permute-start | bytes 1769480 | tf_op jit(solution)/shard_map/ppermute | solution.py:36
  113.3 19.2 %collective-permute-start.6 = (bf16[2,21,16,256]{3,2,1,0:T(8,128)(2,1)S(1)}, bf16[2,21,16,256]{3,2,1,0:T(8,128)(2,1)S(1)}, u32[]{:S(2)}, u32[]{:S(2)}) collective-permute-start(bf16[2,21,16,256]{3,2,1,0:T(8,128)(2,1)S(1)} %get-tuple-element.22.refs_11_), channel_id=1, source_target_pairs={{2,0},{4,2},{6,4},{10,8},{12,10},{14,12},{18,16},{20,18},{22,20},{... | collective-permute-start | bytes 1032200 | tf_op jit(solution)/shard_map/ppermute | solution.py:36
  114.6 19.4 %collective-permute-start.7 = (bf16[2,21,16,256]{3,2,1,0:T(8,128)(2,1)S(1)}, bf16[2,21,16,256]{3,2,1,0:T(8,128)(2,1)S(1)}, u32[]{:S(2)}, u32[]{:S(2)}) collective-permute-start(bf16[2,21,16,256]{3,2,1,0:T(8,128)(2,1)S(1)} %get-tuple-element.23), channel_id=1, source_target_pairs={{0,2},{2,4},{4,6},{8,10},{10,12},{12,14},{16,18},{18,20},{20,22},{... | collective-permute-start | bytes 1032200 | tf_op jit(solution)/shard_map/ppermute | solution.py:36
  125.5 25.7 %collective-permute-start.17 = (bf16[2,16,32,256]{3,2,1,0:T(8,128)(2,1)S(1)}, bf16[2,16,32,256]{3,2,1,0:T(8,128)(2,1)S(1)}, u32[]{:S(2)}, u32[]{:S(2)}) collective-permute-start(bf16[2,16,32,256]{3,2,1,0:T(8,128)(2,1)S(1)} %get-tuple-element.28), channel_id=1, source_target_pairs={{0,8},{8,0},{16,24},{24,16},{1,9},{9,1},{17,25},{25,17},{2,10},{10... | collective-permute-start | bytes 1572872 | tf_op jit(solution)/shard_map/ppermute | solution.py:41
  127.0 26.3 %collective-permute-start.19 = (bf16[2,16,32,256]{3,2,1,0:T(8,128)(2,1)S(1)}, bf16[2,16,32,256]{3,2,1,0:T(8,128)(2,1)S(1)}, u32[]{:S(2)}, u32[]{:S(2)}) collective-permute-start(bf16[2,16,32,256]{3,2,1,0:T(8,128)(2,1)S(1)} %get-tuple-element.28), channel_id=1, source_target_pairs={{0,9},{1,8},{8,1},{9,0},{16,25},{17,24},{24,17},{25,16},{2,11},{3,... | collective-permute-start | bytes 1572872 | tf_op jit(solution)/shard_map/ppermute | solution.py:51
  132.5 19.9 %collective-permute-start.18 = (bf16[2,16,32,256]{3,2,1,0:T(8,128)(2,1)S(1)}, bf16[2,16,32,256]{3,2,1,0:T(8,128)(2,1)S(1)}, u32[]{:S(2)}, u32[]{:S(2)}) collective-permute-start(bf16[2,16,32,256]{3,2,1,0:T(8,128)(2,1)S(1)} %get-tuple-element.27), channel_id=1, source_target_pairs={{0,1},{1,0},{2,3},{3,2},{4,5},{5,4},{6,7},{7,6},{8,9},{9,8},{10,11... | collective-permute-start | bytes 1572872 | tf_op jit(solution)/shard_map/ppermute | solution.py:45
  151.1 8.1 %collective-permute-start.12 = (bf16[1,16,32,256]{3,2,1,0:T(8,128)(2,1)S(1)}, bf16[1,16,32,256]{3,2,1,0:T(8,128)(2,1)S(1)}, u32[]{:S(2)}, u32[]{:S(2)}) collective-permute-start(bf16[1,16,32,256]{3,2,1,0:T(8,128)(2,1)S(1)} %get-tuple-element.31), channel_id=1, source_target_pairs={{0,8},{8,0},{16,24},{24,16},{1,9},{9,1},{17,25},{25,17},{2,10},{10... | collective-permute-start | bytes 786440 | tf_op jit(solution)/shard_map/ppermute | solution.py:41
  151.2 14.3 %collective-permute-start.14 = (bf16[1,16,32,256]{3,2,1,0:T(8,128)(2,1)S(1)}, bf16[1,16,32,256]{3,2,1,0:T(8,128)(2,1)S(1)}, u32[]{:S(2)}, u32[]{:S(2)}) collective-permute-start(bf16[1,16,32,256]{3,2,1,0:T(8,128)(2,1)S(1)} %get-tuple-element.31), channel_id=1, source_target_pairs={{0,9},{1,8},{8,1},{9,0},{16,25},{17,24},{24,17},{25,16},{2,11},{3,... | collective-permute-start | bytes 786440 | tf_op jit(solution)/shard_map/ppermute | solution.py:51
  152.4 13.0 %collective-permute-start.13 = (bf16[1,16,32,256]{3,2,1,0:T(8,128)(2,1)S(1)}, bf16[1,16,32,256]{3,2,1,0:T(8,128)(2,1)S(1)}, u32[]{:S(2)}, u32[]{:S(2)}) collective-permute-start(bf16[1,16,32,256]{3,2,1,0:T(8,128)(2,1)S(1)} %get-tuple-element.30), channel_id=1, source_target_pairs={{0,1},{1,0},{2,3},{3,2},{4,5},{5,4},{6,7},{7,6},{8,9},{9,8},{10,11... | collective-permute-start | bytes 786440 | tf_op jit(solution)/shard_map/ppermute | solution.py:45

commit v2 on v1

v2 whole, which is shorter than its diff:
```python
import math

import jax
import jax.numpy as jnp
from jax import lax
from jax.experimental import pallas as pl
from jax.experimental.pallas import tpu as pltpu
from jax.sharding import PartitionSpec as P


HEAD_DIM = 64
RADIUS_MAX = 6
WINDOW = 13
HALO = 18
MASKED = -1e30
GROUP_HEADS = 4
GROUP_ROWS = 3


def row_shift(value, steps):
    count = lax.axis_size("row")
    pairs = [(s, s + steps) for s in range(count) if 0 <= s + steps < count]
    return lax.ppermute(value, "row", pairs)


def col_swap_where(value, odd, row_ok):
    rows, cols = lax.axis_size("row"), lax.axis_size("col")
    pairs = []
    for r in range(rows):
        for c in range(odd, cols - 1, 2):
            if row_ok(r):
                low = r * cols + c
                pairs += [(low, low + 1), (low + 1, low)]
    return lax.ppermute(value, ("row", "col"), pairs)


def partner(value):
    count = lax.axis_size("row")
    return lax.ppermute(value, "row", [(s, s ^ 1) for s in range(count)])


def head_swap(value):
    return lax.ppermute(value, "head", [(0, 1), (1, 0)])


def head_partner(value):
    rows = lax.axis_size("row")
    pairs = [(2 * r + h, 2 * (r ^ 1) + 1 - h) for r in range(rows) for h in range(2)]
    return lax.ppermute(value, ("row", "head"), pairs)


def row_pair_swap(value):
    return lax.ppermute(value, "row", [(s, s ^ 2) for s in range(4)])


def tables_kernel(dims_ref, dims_row_ref, bias_ref, base_ref, *, slots):
    half = bias_ref.shape[0] // 2
    width = base_ref.shape[2]
    parity = lax.axis_index("row") % 2
    bias = jnp.where(parity == 0, bias_ref[:half], bias_ref[half:])
    index = lax.broadcasted_iota(jnp.int32, (1, WINDOW * WINDOW), 1)
    column = lax.broadcasted_iota(jnp.int32, (WINDOW * WINDOW, width), 0)
    lane = lax.broadcasted_iota(jnp.int32, (WINDOW * WINDOW, width), 1)
    for tile in range(2):
        radius, dilation = dims_ref[tile, 0], dims_ref[tile, 1]
        pattern = dims_row_ref[tile : tile + 1, 2:]
        up, side = index // WINDOW - RADIUS_MAX, index % WINDOW - RADIUS_MAX
        used = (jnp.abs(up) <= radius) & (jnp.abs(side) <= radius)
        used = used & ((pattern == 1) | ((up == 0) & (side == 0)))
        value = jnp.where(used, bias, MASKED)
        target = column // WINDOW * slots + (column % WINDOW - RADIUS_MAX) * dilation
        target = jnp.where(target < 0, target + width, target)
        spot = jnp.where(target == lane, 1.0, 0.0)
        placed = jnp.dot(value, spot, precision=lax.Precision.HIGHEST, preferred_element_type=jnp.float32)
        taken = jnp.max(spot, axis=0, keepdims=True)
        base_ref[tile] = jnp.where(taken > 0.0, placed, MASKED)


def tables(dims, bias, slots):
    half = bias.shape[0] // 2
    vmem = pl.BlockSpec(memory_space=pltpu.VMEM)

    def body(*refs):
        tables_kernel(*refs, slots=slots)

    return pl.pallas_call(
        body,
        out_shape=jax.ShapeDtypeStruct((2, half, (WINDOW + GROUP_ROWS) * slots), jnp.float32),
        in_specs=[pl.BlockSpec(memory_space=pltpu.SMEM), vmem, vmem],
        out_specs=vmem,
        name="tables",
    )(dims, dims, bias)


def give_half(parity, parts, feats):
    rows, cols, all_feats = parts[0][0].shape
    per_half = all_feats // 2 // feats
    block = 8

    def body(parity_ref, *refs):
        for n, source in enumerate(refs[:-1]):
            refs[-1][n] = source[...]

    def spec(chunk):
        return pl.BlockSpec((block, cols, feats), lambda n, p: (n, 0, (1 - p[0]) * per_half + chunk))

    return pl.pallas_call(
        body,
        grid_spec=pltpu.PrefetchScalarGridSpec(
            num_scalar_prefetch=1,
            grid=(rows // block,),
            in_specs=[spec(chunk) for _, chunk in parts],
            out_specs=pl.BlockSpec((len(parts), block, cols, feats), lambda n, p: (0, n, 0, 0)),
        ),
        out_shape=jax.ShapeDtypeStruct((len(parts), rows, cols, feats), parts[0][0].dtype),
        name="give_half",
    )(parity, *[array for array, _ in parts])


def place():
    row = lax.axis_index("row")
    return row % 2, row // 2, lax.axis_index("col") % 2


def send_out(sources, targets, sems, swap):
    for flip in range(2):

        @pl.when(swap == flip)
        def _(flip=flip):
            made = [
                pltpu.make_async_copy(source, targets[n ^ flip], sems[n]) for n, source in enumerate(sources)
            ]
            for copy in made:
                copy.start()
            for copy in made:
                copy.wait()


def pack_kernel(key_ref, value_ref, recv_ref, *refs, low, downs, edge_lows, halos, wires):
    edges = len(downs) * len(edge_lows)
    rows, cols = recv_ref.shape[1:3]
    half = key_ref.shape[2] // 2
    middle_refs = refs[:halos]
    out_refs, (right_ref, left_ref, mid_ref, edge_ref, sems) = refs[-5 - edges - 2 * wires : -5], refs[-5:]
    edge_outs, wire_outs = out_refs[:edges], out_refs[edges:]
    feats = right_ref.shape[3]
    parity, pair, col_parity = place()
    spill = HALO - rows
    every = slice(None)

    def source(kv, own, start, *where):
        if own:
            lanes = pl.ds(pl.multiple_of(parity * half + start, feats), feats)
            return (key_ref, value_ref)[kv].at[(*where, lanes)]
        return recv_ref.at[(2 * (start // feats) + kv, *where, every)]

    count = 0
    middles, others = [], []

    def start_copy(begin, target, group):
        nonlocal count
        copy = pltpu.make_async_copy(begin, target, sems.at[count])
        count += 1
        copy.start()
        group.append(copy)

    def columns(begin, part, top):
        height = part.stop - part.start
        for kv in range(2):
            start_copy(begin(kv, slice(cols // 2 - 8, cols // 2 + 8)), mid_ref.at[kv, part], middles)
            body = slice(top, top + height)
            start_copy(begin(kv, slice(cols - 16, cols)), right_ref.at[kv, body], others)
            start_copy(begin(kv, slice(0, 16)), left_ref.at[kv, body], others)

    if wires:
        for n, own in enumerate((True, False)):
            part = slice(n * rows, (n + 1) * rows)
            columns(lambda kv, at, own=own: source(kv, own, low, every, at), part, n * rows)
        for n, middle in enumerate(middle_refs):
            part = slice(2 * rows + n * HALO, 2 * rows + (n + 1) * HALO)
            top = wire_rows(2 * rows) + n * wire_rows(HALO)
            columns(lambda kv, at, middle=middle: middle.at[kv, :, at], part, top)

    def edge_copies(chunk, n, own_near, downward):
        copies = []
        spot = chunk * len(downs) + n
        for kv in range(2):
            far_rows = slice(rows - spill, rows) if downward else slice(0, spill)
            index = count + 4 * spot + 2 * kv
            near, far = edge_ref.at[spot, kv, 0:rows], edge_ref.at[spot, kv, rows:HALO]
            begin = edge_lows[chunk]
            near_from = source(kv, own_near, begin, every, every)
            far_from = source(kv, not own_near, begin, far_rows, every)
            copies.append(pltpu.make_async_copy(near_from, near, sems.at[index]))
            copies.append(pltpu.make_async_copy(far_from, far, sems.at[index + 1]))
        return copies

    for n, down in enumerate(downs if edge_lows else []):
        goes_down = jnp.where(pair == 0, 1, 0) if down is None else down
        code = jnp.where(parity == goes_down, 1, 0) + 2 * goes_down
        for case in range(4):

            @pl.when(code == case)
            def _(n=n, case=case):
                for chunk in range(len(edge_lows)):
                    for copy in edge_copies(chunk, n, bool(case & 1), bool(case & 2)):
                        copy.start()

    def pair_up(first, height, top):
        for kv in range(2):
            if height * 2 % 16:
                for ref in (right_ref, left_ref):
                    ref[kv, top + wire_rows(height) - 1] = jnp.zeros((16, feats), recv_ref.dtype)
            for r in range(height):
                slot = r * 2
                spot = (kv, top + height + slot // 16, slice(slot % 16, slot % 16 + 2))
                right_ref[spot] = mid_ref[kv, first + r, 6:8, :]
                left_ref[spot] = mid_ref[kv, first + r, 8:10, :]

    sent = []
    if edge_lows:
        for chunk in range(len(edge_lows)):
            for n in range(len(downs)):
                for copy in edge_copies(chunk, n, True, True):
                    copy.wait()
        for n in range(edges):
            sent.append(pltpu.make_async_copy(edge_ref.at[n], edge_outs[n], sems.at[count + 4 * edges + n]))
            sent[-1].start()
    if wires:
        for copy in middles:
            copy.wait()
        pair_up(0, 2 * rows, 0)
        for n in range(halos):
            pair_up(2 * rows + n * HALO, HALO, wire_rows(2 * rows) + n * wire_rows(HALO))
        for copy in others:
            copy.wait()
        last = count + 5 * edges
        send_out([right_ref, left_ref], wire_outs, [sems.at[last], sems.at[last + 1]], col_parity)
    for copy in sent:
        copy.wait()


def wire_rows(height):
    return height + -(-height * (HALO - 16) // 16)


def pack(key_map, value_map, recv, low, feats, downs, edge_lows, middles, wires, after):
    _, rows, cols, _ = recv.shape
    edges, halos = len(downs) * len(edge_lows), len(middles)
    hbm = pl.BlockSpec(memory_space=pltpu.HBM)
    height = wire_rows(2 * rows) + halos * wire_rows(HALO)
    wire = jax.ShapeDtypeStruct((2, height, 16, feats), recv.dtype)

    def body(*refs):
        pack_kernel(*refs, low=low, downs=downs, edge_lows=edge_lows, halos=halos, wires=wires)

    return pl.pallas_call(
        body,
        out_shape=[jax.ShapeDtypeStruct((2, HALO, cols, feats), recv.dtype)] * edges + [wire, wire] * wires,
        in_specs=[hbm] * (3 + halos + len(after)),
        out_specs=[hbm] * (edges + 2 * wires),
        scratch_shapes=[
            pltpu.VMEM((2, height, 16, feats), recv.dtype),
            pltpu.VMEM((2, height, 16, feats), recv.dtype),
            pltpu.VMEM((2, 2 * rows + halos * HALO, 16, feats), recv.dtype),
            pltpu.VMEM((max(edges, 1), 2, HALO, cols, feats), recv.dtype),
            pltpu.SemaphoreType.DMA((14 + 6 * halos + 5 * edges,)),
        ],
        compiler_params=pltpu.CompilerParams(vmem_limit_bytes=40 * 1024 * 1024),
        name="pack",
    )(key_map, value_map, recv, *middles, *after)


def pack_halo(middle, after):
    _, rows, cols, feats = middle.shape
    vmem = pl.BlockSpec(memory_space=pltpu.VMEM)
    hbm = pl.BlockSpec(memory_space=pltpu.HBM)
    height = wire_rows(rows)
    tail = height - rows
    wire = jax.ShapeDtypeStruct((2, height, 16, feats), middle.dtype)

    def body(in_ref, *refs):
        first_out, second_out, right_ref, left_ref, sems = refs[-5:]
        for kv in range(2):
            right_ref[kv, 0:rows] = in_ref[kv, :, cols - 16 :, :]
            left_ref[kv, 0:rows] = in_ref[kv, :, 0:16, :]
            for ref in (right_ref, left_ref):
                ref[kv, rows + tail - 1] = jnp.zeros((16, feats), middle.dtype)
            for r in range(rows):
                slot = r * 2
                spot = (kv, rows + slot // 16, slice(slot % 16, slot % 16 + 2))
                right_ref[spot] = in_ref[kv, r, cols - HALO : cols - 16, :]
                left_ref[spot] = in_ref[kv, r, 16:HALO, :]
        send_out([right_ref, left_ref], [first_out, second_out], [sems.at[0], sems.at[1]], place()[2])

    return pl.pallas_call(
        body,
        out_shape=[wire, wire],
        in_specs=[vmem] + [hbm] * len(after),
        out_specs=[hbm, hbm],
        scratch_shapes=[pltpu.VMEM(wire.shape, wire.dtype)] * 2 + [pltpu.SemaphoreType.DMA((2,))],
        compiler_params=pltpu.CompilerParams(vmem_limit_bytes=40 * 1024 * 1024),
        name="pack_halo",
    )(middle, *after)


def attend_kernel(dims_ref, base_ref, *refs, halos, joined, low, tiles, recv_at, query_at):
    key_ref, value_ref, query_ref, recv_ref, side_first, side_second = refs[:6]
    per_halo = 1 if joined else 3
    halo_refs = refs[6 : 6 + per_halo * halos]
    out_ref, slab_ref, q_ref, extra_ref, table_ref, rows_ref, sems = refs[-7:]
    groups, _, slab_rows, slots, feats = slab_ref.shape
    tile_rows, cols = q_ref.shape[2], q_ref.shape[3]
    half = key_ref.shape[2] // 2
    heads = feats // HEAD_DIM
    width = table_ref.shape[1]
    keys = (WINDOW + GROUP_ROWS - 1) * slots
    block = heads * cols
    parity, pair, col_parity = place()
    own_row, other_row = parity * tile_rows, (1 - parity) * tile_rows
    spill, pair_rows = HALO - tile_rows, 2 * tile_rows
    pair_base = pair * pair_rows
    total_rows = tile_rows * lax.axis_size("row")
    total_cols = cols * lax.axis_size("col")
    col_anchor = lax.axis_index("col") * cols
    if halos == 0:
        own_off, spots = 0, []
    elif halos == 1:
        own_off = jnp.where(pair == 0, 0, HALO)
        spots = [(jnp.where(pair == 0, pair_rows, spill), jnp.where(pair == 0, pair_rows + tile_rows, 0))]
    else:
        own_off = HALO
        spots = [(spill, 0), (HALO + pair_rows, HALO + pair_rows + tile_rows)]
    slots_at = [cols + 32 * col_parity, cols + 32 * (1 - col_parity)]
    slots_at = [pl.ds(pl.multiple_of(at, 16), 16) for at in slots_at]
    sides_at = [col_parity, 1 - col_parity]
    extra_slots = slice(cols + 16, cols + 32)
    tail = 2 * tile_rows * 2 // 16
    halo_tail = -(-HALO * 2 // 16)

    def places(n):
        if n < 0:
            return [(own_off + own_row, tile_rows, 0), (own_off + other_row, tile_rows, tile_rows)]
        near, far = spots[n]
        return [(near, tile_rows, 0), (far, HALO - tile_rows, tile_rows)]

    def copies(g):
        own = pl.ds(pl.multiple_of(parity * half + low + g * feats, feats), feats)
        here = pl.ds(pl.multiple_of(g * feats, feats), feats)
        made = []

        def add(source, target):
            made.append(pltpu.make_async_copy(source, target, sems.at[g, len(made)]))

        add(query_ref.at[:, :, own], q_ref.at[g, 0])
        add(recv_ref.at[query_at], q_ref.at[g, 1])
        for kv in range(2):
            slab = slab_ref.at[g, kv]
            add((key_ref, value_ref)[kv].at[:, :, own], slab.at[pl.ds(own_off + own_row, tile_rows), 0:cols])
            add(recv_ref.at[recv_at + kv], slab.at[pl.ds(own_off + other_row, tile_rows), 0:cols])
            for n in range(-1, halos):
                wires, top, height, extra = (side_first, side_second), 0, 2 * tile_rows, 0
                if n >= 0:
                    height, extra = HALO, tail + n * halo_tail
                    middle = halo_refs[per_halo * n]
                    if joined:
                        top = wire_rows(2 * tile_rows) + n * wire_rows(HALO)
                    else:
                        wires = halo_refs[3 * n + 1 : 3 * n + 3]
                for start, count, first in places(n):
                    rows = pl.ds(start, count)
                    if n >= 0:
                        add(middle.at[kv, first : first + count, :, here], slab.at[rows, 0:cols])
                    part = slice(top + first, top + first + count)
                    for wire, at in zip(wires, slots_at):
                        add(wire.at[kv, part, :, here], slab.at[rows, at])
                count = tail if n < 0 else halo_tail
                for side, wire in zip(sides_at, wires):
                    target = extra_ref.at[g, kv, side, extra : extra + count]
                    add(wire.at[kv, top + height : top + height + count, :, here], target)
        return made

    def start_group(g, carry):
        for copy in copies(g):
            copy.start()
        return carry

    lax.fori_loop(0, groups, start_group, 0)

    lane = lax.broadcasted_iota(jnp.int32, (1, width), 1)
    step = jnp.zeros((1, width), jnp.int32)
    for m in range(1, width // slots):
        step = step + jnp.where(lane >= m * slots, 1, 0)
    slot = lane - step * slots
    front_ok = jnp.where((slot < cols + HALO) & (col_anchor + slot < total_cols) & (lane < keys), 1, 0)
    back_ok = jnp.where((slot >= slots - HALO) & (col_anchor + slot >= slots) & (lane < keys), 2, 0)
    ok = jnp.broadcast_to(front_ok + back_ok, (cols, width))
    lane_head = lax.broadcasted_iota(jnp.int32, (cols, feats), 1) // HEAD_DIM
    scale = 1.0 / math.sqrt(HEAD_DIM)

    def fill_extras(g):
        for kv in range(2):
            slab_ref[g, kv, :, extra_slots, :] = jnp.zeros((slab_rows, 16, feats), jnp.bfloat16)
            for n in range(-1, halos):
                origin = 0 if n < 0 else tail + n * halo_tail
                for start, count, first in places(n):
                    for r in range(count):
                        at = (first + r) * 2
                        rows = slice(at % 16, at % 16 + 2)
                        where = origin + at // 16
                        slab_ref[g, kv, start + r, cols + 16 : cols + 18, :] = extra_ref[g, kv, 0, where, rows, :]
                        slab_ref[g, kv, start + r, cols + 30 : cols + 32, :] = extra_ref[g, kv, 1, where, rows, :]

    def fill_table(g, tile):
        for h in range(heads):
            head = low // HEAD_DIM + g * heads + h
            base = jnp.broadcast_to(base_ref[tile, pl.ds(head, 1), :], (cols, width))
            for n in range(GROUP_ROWS):
                front = pltpu.roll(base, n * slots, 1, stride=1, stride_axis=0)
                back = pltpu.roll(base, (n + 1) * slots, 1, stride=1, stride_axis=0)
                row0 = n * block + h * cols
                table_ref[row0 : row0 + cols, :] = jnp.where(
                    ok == 1, front, jnp.where(ok == 2, back, MASKED)
                )

    def one_tile(g, tile):
        dilation = dims_ref[tile, 1]
        tile_row = jnp.where(tile == 0, own_row, other_row)

        def unit(p, carry):
            first = (p // dilation) * (GROUP_ROWS * dilation) + p % dilation
            blocks = []
            for n in range(GROUP_ROWS):
                q_row = q_ref[g, tile, jnp.minimum(first + n * dilation, tile_rows - 1)]
                q_row = q_row.astype(jnp.float32) * scale
                blocks += [jnp.where(lane_head == h, q_row, 0.0).astype(jnp.bfloat16) for h in range(heads)]
            q_block = jnp.concatenate(blocks, axis=0)
            top = tile_row + first - RADIUS_MAX * dilation
            starts = [
                jnp.clip(own_off + top + m * dilation, 0, slab_rows - 1)
                for m in range(WINDOW + GROUP_ROWS - 1)
            ]
            k_rows = jnp.concatenate([slab_ref[g, 0, s] for s in starts], axis=0)
            v_rows = jnp.concatenate([slab_ref[g, 1, s] for s in starts], axis=0)
            scores = lax.dot_general(
                q_block, k_rows, (((1,), (1,)), ((), ())), preferred_element_type=jnp.float32
            )
            key_row = pair_base + top + step * dilation
            outside = jnp.where((key_row >= 0) & (key_row < total_rows), 0.0, MASKED)
            weights, sums = [], []
            for n in range(GROUP_ROWS):
                start = n * slots // 128 * 128
                stop = min(-(-(n + WINDOW) * slots // 128) * 128, keys)
                part = slice(n * block, (n + 1) * block)
                score = scores[part, start:stop] + table_ref[part, start:stop] + outside[:, start:stop]
                peak = jnp.max(score, axis=1, keepdims=True)
                exponent = jnp.exp(score - peak)
                sums.append(jnp.sum(exponent, axis=1, keepdims=True))
                pieces = [exponent.astype(jnp.bfloat16)]
                if start:
                    pieces.insert(0, jnp.zeros((block, start), jnp.bfloat16))
                if stop < keys:
                    pieces.append(jnp.zeros((block, keys - stop), jnp.bfloat16))
                weights.append(jnp.concatenate(pieces, axis=1))
            mixed = jnp.dot(
                jnp.concatenate(weights, axis=0), v_rows, preferred_element_type=jnp.float32
            ) / jnp.concatenate(sums, axis=0)
            for n in range(GROUP_ROWS):
                picked = mixed[n * block : n * block + cols]
                for h in range(1, heads):
                    row0 = n * block + h * cols
                    picked = jnp.where(lane_head == h, mixed[row0 : row0 + cols], picked)
                rows_ref[first + n * dilation] = picked.astype(jnp.bfloat16)
            return carry

        lax.fori_loop(0, -(-tile_rows // GROUP_ROWS), unit, 0, unroll=True)
        out_ref[tile - tiles[0], g] = rows_ref[0:tile_rows]

    def one_group(g, carry):
        fill_table(g, tiles[0])
        for copy in copies(g):
            copy.wait()
        fill_extras(g)

        def tile_step(tile, inner):
            @pl.when(tile > tiles[0])
            def _():
                fill_table(g, tile)

            one_tile(g, tile)
            return inner

        lax.fori_loop(tiles[0], tiles[-1] + 1, tile_step, 0)
        return carry

    lax.fori_loop(0, groups, one_group, 0)


def attend(
    dims, base, key_map, value_map, query_map, recv, first, second, halos, joined, after,
    low, all_feats, slots, tiles, recv_at, query_at,
):
    _, tile_rows, cols, _ = recv.shape
    feats = GROUP_HEADS * HEAD_DIM
    groups = all_feats // feats
    slab_rows = 2 * tile_rows + HALO * len(halos)
    count = len(tiles) * tile_rows * groups * GROUP_HEADS * cols * WINDOW * slots
    hbm = pl.BlockSpec(memory_space=pltpu.HBM)
    vmem = pl.BlockSpec(memory_space=pltpu.VMEM)
    flat = [array for halo in halos for array in halo] + list(after)
    tails = 2 * tile_rows * 2 // 16 + len(halos) * -(-HALO * 2 // 16)

    def body(*refs):
        attend_kernel(*refs, halos=len(halos), joined=joined, low=low, tiles=tiles, recv_at=recv_at, query_at=query_at)

    return pl.pallas_call(
        body,
        out_shape=jax.ShapeDtypeStruct((len(tiles), groups, tile_rows, cols, feats), jnp.bfloat16),
        in_specs=[pl.BlockSpec(memory_space=pltpu.SMEM), vmem] + [hbm] * (6 + len(flat)),
        out_specs=vmem,
        scratch_shapes=[
            pltpu.VMEM((groups, 2, slab_rows, slots, feats), jnp.bfloat16),
            pltpu.VMEM((groups, 2, tile_rows, cols, feats), jnp.bfloat16),
            pltpu.VMEM((groups, 2, 2, tails, 16, feats), jnp.bfloat16),
            pltpu.VMEM((GROUP_ROWS * GROUP_HEADS * cols, base.shape[2]), jnp.float32),
            pltpu.VMEM((tile_rows + 8, cols, feats), jnp.bfloat16),
            pltpu.SemaphoreType.DMA((groups, 2 + 2 * (8 + 8 * len(halos)))),
        ],
        compiler_params=pltpu.CompilerParams(vmem_limit_bytes=48 * 1024 * 1024),
        cost_estimate=pl.CostEstimate(
            flops=count * feats * 4, transcendentals=count, bytes_accessed=4 * groups * slab_rows * slots * feats
        ),
        name="attend",
    )(dims, base, key_map, value_map, query_map, recv, first, second, *flat)


def project(spots, terms, out_weight, far_weights, half_feats, before, dtype):
    tokens, feats = terms[0][2].shape
    model = far_weights[0].shape[1]
    block = model // 3
    per_half = half_feats // feats
    columns = model // block
    whole = pl.BlockSpec((tokens, feats), lambda n, spot: (0, 0))
    column = pl.BlockSpec((tokens, block), lambda n, spot: (0, n))
    specs, arrays, pieces = [], [], []
    for index, source, piece in terms:
        if source < 2:

            def at(n, spot, source=source, index=index):
                who = spot[0] if source == 0 else 1 - spot[0]
                return who * per_half + index, spot[1] * columns + n

            arrays.append(out_weight)
        else:

            def at(n, spot, index=index):
                return index, n

            arrays.append(far_weights[source - 2])
        pieces.append(piece)
        specs.append(pl.BlockSpec((feats, block), at))
    extra = [] if before is None else [before]
    count = len(pieces)

    def body(spot_ref, *refs):
        total = refs[-2][...] if extra else None
        for lhs, rhs in zip(refs[:count], refs[count : 2 * count]):
            term = jnp.dot(lhs[...], rhs[...], preferred_element_type=jnp.float32)
            total = term if total is None else total + term
        refs[-1][...] = total.astype(dtype)

    return pl.pallas_call(
        body,
        grid_spec=pltpu.PrefetchScalarGridSpec(
            num_scalar_prefetch=1,
            grid=(columns,),
            in_specs=[whole] * count + specs + [column] * len(extra),
            out_specs=column,
        ),
        out_shape=jax.ShapeDtypeStruct((tokens, model), dtype),
        compiler_params=pltpu.CompilerParams(vmem_limit_bytes=40 * 1024 * 1024),
        cost_estimate=pl.CostEstimate(
            flops=2 * tokens * model * feats * count,
            transcendentals=0,
            bytes_accessed=2 * model * feats * count,
        ),
        name="project",
    )(spots, *pieces, *arrays, *extra)


def layer(
    query_map, key_map, value_map, window_mask, tile_radius, dilation_per_tile, rel_bias, out_weight
):
    tile_rows, tile_cols, features_dev = query_map.shape
    half_feats = features_dev // 2
    feats = GROUP_HEADS * HEAD_DIM
    slots = tile_cols + 48
    row_id = lax.axis_index("row")
    parity = row_id % 2
    rows_count = lax.axis_size("row")
    pairs_count = rows_count // 2
    tokens = tile_rows * tile_cols
    head_id = lax.axis_index("head")
    model_half = out_weight.shape[1] // 2

    total_groups = half_feats // feats
    parts = [(array, n) for n in range(total_groups) for array in (key_map, value_map)]
    parts += [(query_map, n) for n in range(total_groups)]
    given = give_half(parity.astype(jnp.int32)[None], parts, feats)
    recv = partner(given)

    mine = jnp.concatenate([tile_radius[0], dilation_per_tile[0], window_mask[0, 0].reshape(-1)])
    others = partner(mine)
    dims = jnp.stack([mine, others])
    base = tables(dims, rel_bias.reshape(rel_bias.shape[0], -1), slots)

    downs = {1: [], 2: [None]}.get(pairs_count, [1, 0])
    lows = [n * feats for n in range(total_groups)]
    *edges, first, second = pack(
        key_map, value_map, recv, 0, feats, downs, lows[:1], [], True, []
    )
    if downs and lows[1:]:
        edges += pack(key_map, value_map, recv, 0, feats, downs, lows[1:], [], False, [second])
    middles = []
    for n in range(total_groups):
        if pairs_count == 2:
            middles.append([row_pair_swap(edges[n])])
        else:
            own = edges[n * len(downs) : (n + 1) * len(downs)]
            middles.append([row_shift(edge, 2 if down else -2) for edge, down in zip(own, downs)])
    row_oks = {1: [lambda r: True], 2: [lambda r: r >= 2, lambda r: r < rows_count - 2]}.get(len(downs), [])
    order = []

    def prepare(n):
        halos, wires = [], [first, second]
        if n == 0:
            for middle, row_ok in zip(middles[n], row_oks):
                outs = pack_halo(middle, order[-1:])
                order.append(outs[1])
                halos.append((middle, *[col_swap_where(wire, odd, row_ok) for odd, wire in enumerate(outs)]))
        else:
            wires = pack(key_map, value_map, recv, lows[n], feats, downs, [], middles[n], True, order[-1:])
            order.append(wires[1])
            halos = [(middle,) for middle in middles[n]]
        sides = [col_swap_where(wire, odd, lambda r: True) for odd, wire in enumerate(wires)]
        return sides, halos

    give = lax.dynamic_slice(out_weight, (parity * half_feats, (1 - head_id) * model_half), (half_feats, model_half))
    far_weight = head_swap(give)
    corner = jnp.stack([parity, head_id]).astype(jnp.int32)

    calls = [(n, tiles) for n in range(total_groups - 1) for tiles in ((0, 1),)]
    calls += [(total_groups - 1, (0,)), (total_groups - 1, (1,))]
    exchanged = []
    ready = [prepare(n) for n in range(min(2, total_groups))]
    for index, (n, tiles) in enumerate(calls):
        sides, halos = ready[n]
        done = attend(
            dims, base, key_map, value_map, query_map, recv, *sides, halos, n > 0, order[-1:],
            lows[n], feats, slots, tiles, 2 * n, 2 * total_groups + n,
        )
        if index == len(calls) - 2:
            far_weights = [far_weight, partner(lax.optimization_barrier((far_weight, done))[0])]
        order.append(done)
        if len(ready) < total_groups:
            ready.append(prepare(len(ready)))
        if 0 in tiles:
            own = done[0]
            exchanged += [(n, 0, own), (n, 2, head_swap(own))]
        if 1 in tiles:
            other = done[-1]
            exchanged += [(n, 1, partner(other)), (n, 3, head_partner(other))]
    exchanged = [(n, source, piece.reshape(tokens, feats)) for n, source, piece in exchanged]
    acc = project(corner, exchanged[:-1], out_weight, far_weights, half_feats, None, jnp.float32)
    acc = project(corner, exchanged[-1:], out_weight, far_weights, half_feats, acc, jnp.bfloat16)
    return acc.reshape(tile_rows, tile_cols, model_half)


def solution(mesh):
    placed = (
        P("row", "col", "head"),
        P("row", "col", "head"),
        P("row", "col", "head"),
        P("row", "col", None, None),
        P("row", "col"),
        P("row", "col"),
        P("head", None, None),
        P("head", None),
    )
    return jax.shard_map(layer, mesh=mesh, in_specs=placed, out_specs=P("row", "col", "head"), check_vma=False)
```

time: 172 us -> 146 us (0.85)
  Pallas kernels: 77 us -> 68.1 us
  waiting for transfers between devices: 43.3 us -> 34.5 us
  starting transfers between devices: 34.2 us -> 29.5 us
  local copies, waits for them, and re-layouts: 13.6 us -> 9.45 us
    ppermute x8, waiting for transfers between devices: 15.8 us -> 4.85 us  [col_swap_where(): return lax.ppermute(value, ('row', 'col'), pairs)]
    ppermute x8, starting transfers between devices: 25 us -> 14.5 us  [col_swap_where(): return lax.ppermute(value, ('row', 'col'), pairs)]
    ppermute x2 -> x3, waiting for transfers between devices: 16.8 us -> 8.82 us  [row_pair_swap(): return lax.ppermute(value, 'row', [(s, s ^ 2) for s in range(4)])]
    pallas_call x4 -> x5, Pallas kernels: 51.7 us -> 44.6 us  [the longest x4 42.7 us: attend(): pl.pallas_call(body, out_shape=jax.ShapeDtypeStruct((len(tiles), groups,...]
    ppermute x3 -> x4, waiting for transfers between devices: 6.23 us -> 13.1 us  [head_swap(): return lax.ppermute(value, 'head', [(0, 1), (1, 0)])]
    ppermute x2 -> x3, waiting for transfers between devices: 0.01 us -> 3.39 us  [head_partner(): return lax.ppermute(value, ('row', 'head'), pairs)]
    ppermute x2 -> x3, starting transfers between devices: 1.43 us -> 4.47 us  [head_partner(): return lax.ppermute(value, ('row', 'head'), pairs)]
    ppermute x2 -> x3, starting transfers between devices: 3.21 us -> 5.28 us  [row_pair_swap(): return lax.ppermute(value, 'row', [(s, s ^ 2) for s in range(4)])]
  transfers between devices with their start and end apart: 20 -> 24, of which waited for: 9 -> 8; matrix products, arithmetic and copies ran while one was open for 6% -> 5% of each run, Pallas kernels for 37% -> 42%
where the time goes in v2:
time: 146 us; the launch traced here: 144 us
  Pallas kernels  68.1 us (47%)
  waiting for transfers between devices  34.5 us (24%)
  starting transfers between devices  29.5 us (20%)
  local copies, waits for them, and re-layouts  9.45 us (6%)
  between operations  1.56 us (1%)
    pallas_call x4, Pallas kernels, attend(): pl.pallas_call(body, out_shape=jax.ShapeDtypeStruct((len(tiles), groups,...  42.7 us
    ppermute x8, starting transfers between devices, col_swap_where(): return lax.ppermute(value, ('row', 'col'), pairs)  14.5 us
    ppermute x4, waiting for transfers between devices, head_swap(): return lax.ppermute(value, 'head', [(0, 1), (1, 0)])  13.1 us
    pallas_call x2, Pallas kernels, project(): pl.pallas_call(body, grid_spec=pltpu.PrefetchScalarGridSpec(num_scalar_pr...  10.6 us
    ppermute x3, waiting for transfers between devices, row_pair_swap(): return lax.ppermute(value, 'row', [(s, s ^ 2) for s in range(4)])  8.82 us
    pallas_call x4, Pallas kernels, pack(): pl.pallas_call(body, out_shape=[jax.ShapeDtypeStruct((2, HALO, cols, feat...  7.24 us
    ppermute x3, starting transfers between devices, row_pair_swap(): return lax.ppermute(value, 'row', [(s, s ^ 2) for s in range(4)])  5.28 us
    ppermute x8, waiting for transfers between devices, col_swap_where(): return lax.ppermute(value, ('row', 'col'), pairs)  4.85 us
  transfers between devices with their start and end apart: 24, of which 8 were waited for; matrix products, arithmetic and copies ran while one was open for 5% of the time, Pallas kernels for 42%

profile of v2, /device:TPU:0, one launch (start us, length us, event | category | flops | bytes accessed | tf_op | source)
XLA Modules:
  0.0 143.9 jit_solution(981915977401923164)
XLA Ops:
  0.0 3.0 %give_half.1 = bf16[9,16,32,256]{3,2,1,0:T(8,128)(2,1)} custom-call(s32[1]{0:T(128)} %bitcast.parity_ref, bf16[16,32,1536]{2,1,0:T(8,128)(2,1)} %refs_2_.9, bf16[16,32,1536]{2,1,0:T(8,128)(2,1)} %refs_3_.9, bf16[16,32,1536]{2,1,0:T(8,128)(2,1)} %refs_2_.9, bf16[16,32,1536]{2,1,0:T(8,128)(2,1)} %refs_3_.9, bf16[16,32,1536]{2,1,0:T(8,128)(2,1)} %refs_2_.9, ...), custom_call_target="tpu_custom_call" | custom-call | tf_op jit(solution)/shard_map/give_half/pallas_call | solution.py:107
  3.0 0.5 collective-permute-start.1
  3.5 4.4 %collective-permute-done.1.refs_2_.refs_5_ = bf16[9,16,32,256]{3,2,1,0:T(8,128)(2,1)S(1)} collective-permute-done((bf16[9,16,32,256]{3,2,1,0:T(8,128)(2,1)}, bf16[9,16,32,256]{3,2,1,0:T(8,128)(2,1)S(1)}, u32[]{:S(2)}, u32[]{:S(2)}) %collective-permute-start.1) | collective-permute-done | bytes 2359328 | tf_op jit(solution)/shard_map/ppermute | solution.py:39
  7.9 1.9 %pack.4 = (bf16[2,18,32,256]{3,2,1,0:T(8,128)(2,1)}, bf16[2,36,16,256]{3,2,1,0:T(8,128)(2,1)}, bf16[2,36,16,256]{3,2,1,0:T(8,128)(2,1)}) custom-call(bf16[16,32,1536]{2,1,0:T(8,128)(2,1)S(1)} %copy-done, bf16[16,32,1536]{2,1,0:T(8,128)(2,1)S(1)} %copy-done.1, bf16[9,16,32,256]{3,2,1,0:T(8,128)(2,1)S(1)} %collective-permute-done.1.refs_2_.refs_5_), custom_call_target="tpu_custom_call" | custom-call | tf_op jit(solution)/shard_map/pack/pallas_call | solution.py:257
  9.8 0.1 copy-done.3
  10.0 2.9 %collective-permute-start.5 = (bf16[2,18,32,256]{3,2,1,0:T(8,128)(2,1)}, bf16[2,18,32,256]{3,2,1,0:T(8,128)(2,1)}, u32[]{:S(2)}, u32[]{:S(2)}) collective-permute-start(bf16[2,18,32,256]{3,2,1,0:T(8,128)(2,1)} %get-tuple-element.20), channel_id=1, source_target_pairs={{0,16},{8,24},{16,0},{24,8},{1,17},{9,25},{17,1},{25,9},{2,18},{10... | collective-permute-start | bytes 1769480 | tf_op jit(solution)/shard_map/ppermute | solution.py:53
  12.9 1.6 %collective-permute-start.3 = (bf16[2,36,16,256]{3,2,1,0:T(8,128)(2,1)}, bf16[2,36,16,256]{3,2,1,0:T(8,128)(2,1)}, u32[]{:S(2)}, u32[]{:S(2)}) collective-permute-start(bf16[2,36,16,256]{3,2,1,0:T(8,128)(2,1)} %get-tuple-element.19), channel_id=1, source_target_pairs={{0,2},{2,0},{4,6},{6,4},{8,10},{10,8},{12,14},{14,12},{16,18},{18,... | collective-permute-start | bytes 1769480 | tf_op jit(solution)/shard_map/ppermute | solution.py:34
  14.5 3.4 %dynamic_slice.3 = bf16[768,1536]{1,0:T(8,128)(2,1)} dynamic-slice(bf16[1536,3072]{1,0:T(8,128)(2,1)} %refs_21_.1, s32[]{:T(128)S(6)} %select_n.14, s32[]{:T(128)S(6)} %select_n.15), dynamic_slice_sizes={768,1536} | dynamic-slice | bytes 4718596 | tf_op jit(solution)/shard_map/dynamic_slice | solution.py:648
  17.9 1.5 %collective-permute-start.14 = (bf16[768,1536]{1,0:T(8,128)(2,1)}, bf16[768,1536]{1,0:T(8,128)(2,1)}, u32[]{:S(2)}, u32[]{:S(2)}) collective-permute-start(bf16[768,1536]{1,0:T(8,128)(2,1)} %dynamic_slice.3), channel_id=1, source_target_pairs={{0,1},{1,0},{2,3},{3,2},{4,5},{5,4},{6,7},{7,6},{8,9},{9,8},{10,11... | collective-permute-start | bytes 7077896 | tf_op jit(solution)/shard_map/ppermute | solution.py:43
  19.4 1.1 pack.5
  20.6 0.9 copy-done.9
  21.5 0.6 collective-permute-start.8
  22.1 1.5 %collective-permute-start.4 = (bf16[2,36,16,256]{3,2,1,0:T(8,128)(2,1)}, bf16[2,36,16,256]{3,2,1,0:T(8,128)(2,1)}, u32[]{:S(2)}, u32[]{:S(2)}) collective-permute-start(bf16[2,36,16,256]{3,2,1,0:T(8,128)(2,1)} %get-tuple-element.17.refs_3_), channel_id=1, source_target_pairs={{2,4},{4,2},{10,12},{12,10},{18,20},{20,18},{26,28},{28,26},{3,5},... | collective-permute-start | bytes 1769480 | tf_op jit(solution)/shard_map/ppermute | solution.py:34
  23.6 0.1 reshape_squeeze.12
  25.0 0.1 pad_add_fusion.1
  25.0 2.4 %collective-permute-done.5.in_ref.refs_8_ = bf16[2,18,32,256]{3,2,1,0:T(8,128)(2,1)} collective-permute-done((bf16[2,18,32,256]{3,2,1,0:T(8,128)(2,1)}, bf16[2,18,32,256]{3,2,1,0:T(8,128)(2,1)}, u32[]{:S(2)}, u32[]{:S(2)}) %collective-permute-start.5) | collective-permute-done | bytes 589856 | tf_op jit(solution)/shard_map/ppermute | solution.py:53
  27.4 0.0 collective-permute-start
  27.4 1.9 %pack_halo.1 = (bf16[2,21,16,256]{3,2,1,0:T(8,128)(2,1)}, bf16[2,21,16,256]{3,2,1,0:T(8,128)(2,1)S(1)}) custom-call(bf16[2,18,32,256]{3,2,1,0:T(8,128)(2,1)} %collective-permute-done.5.in_ref.refs_8_), custom_call_target="tpu_custom_call" | custom-call | tf_op jit(solution)/shard_map/pack_halo/pallas_call | solution.py:296
  29.3 0.0 collective-permute-done
  29.3 2.2 %collective-permute-start.6 = (bf16[2,21,16,256]{3,2,1,0:T(8,128)(2,1)}, bf16[2,21,16,256]{3,2,1,0:T(8,128)(2,1)}, u32[]{:S(2)}, u32[]{:S(2)}) collective-permute-start(bf16[2,21,16,256]{3,2,1,0:T(8,128)(2,1)} %get-tuple-element.21), channel_id=1, source_target_pairs={{0,2},{2,0},{4,6},{6,4},{8,10},{10,8},{12,14},{14,12},{16,18},{18,... | collective-permute-start | bytes 1032200 | tf_op jit(solution)/shard_map/ppermute | solution.py:34
  31.5 0.0 collective-permute-done.3.refs_6_
  31.5 1.4 collective-permute-start.7
  32.9 6.5 %collective-permute-done.8.refs_3_.refs_8_ = bf16[2,18,32,256]{3,2,1,0:T(8,128)(2,1)} collective-permute-done((bf16[2,18,32,256]{3,2,1,0:T(8,128)(2,1)}, bf16[2,18,32,256]{3,2,1,0:T(8,128)(2,1)}, u32[]{:S(2)}, u32[]{:S(2)}) %collective-permute-start.8) | collective-permute-done | bytes 589856 | tf_op jit(solution)/shard_map/ppermute | solution.py:53
  39.4 1.7 %collective-permute-start.2 = (bf16[2,18,32,256]{3,2,1,0:T(8,128)(2,1)}, bf16[2,18,32,256]{3,2,1,0:T(8,128)(2,1)}, u32[]{:S(2)}, u32[]{:S(2)}) collective-permute-start(bf16[2,18,32,256]{3,2,1,0:T(8,128)(2,1)} %copy-done.9), channel_id=1, source_target_pairs={{0,16},{8,24},{16,0},{24,8},{1,17},{9,25},{17,1},{25,9},{2,18},{10... | collective-permute-start | bytes 1769480 | tf_op jit(solution)/shard_map/ppermute | solution.py:53
  41.2 1.5 %reshape.33 = f32[24,169]{0,1:T(8,128)} reshape(f32[24,13,13]{0,2,1:T(8,128)} %param.14) | data formatting | bytes 32448 | tf_op jit(solution)/shard_map/reshape | solution.py:615
  42.7 1.6 %copy.10.refs_2_ = f32[24,169]{1,0:T(8,128)} copy(f32[24,169]{0,1:T(8,128)} %reshape.33) | data formatting | bytes 32448 | tf_op jit(solution)/shard_map/reshape | solution.py:615
  44.3 0.6 pad_add_fusion.refs_0_.refs_1_
  44.8 2.6 %tables.1.refs_1_ = f32[2,12,1280]{2,1,0:T(8,128)} custom-call(s32[2,171]{1,0:T(2,128)} %pad_add_fusion.refs_0_.refs_1_, s32[2,171]{1,0:T(2,128)} %pad_add_fusion.refs_0_.refs_1_, f32[24,169]{1,0:T(8,128)} %copy.10.refs_2_), custom_call_target="tpu_custom_call" | custom-call | tf_op jit(solution)/shard_map/tables/pallas_call | solution.py:86
  47.5 1.7 %copy-done.5 = bf16[9,16,32,256]{3,2,1,0:T(8,128)(2,1)S(1)} copy-done((bf16[9,16,32,256]{3,2,1,0:T(8,128)(2,1)S(1)}, bf16[9,16,32,256]{3,2,1,0:T(8,128)(2,1)}, u32[]{:S(2)}) %copy-start.5) | copy-done | bytes 2359320
  49.2 2.1 %pack.6 = (bf16[2,57,16,256]{3,2,1,0:T(8,128)(2,1)S(1)}, bf16[2,57,16,256]{3,2,1,0:T(8,128)(2,1)S(1)}) custom-call(bf16[16,32,1536]{2,1,0:T(8,128)(2,1)S(1)} %copy-done, bf16[16,32,1536]{2,1,0:T(8,128)(2,1)S(1)} %copy-done.1, bf16[9,16,32,256]{3,2,1,0:T(8,128)(2,1)S(1)} %copy-done.5, bf16[2,18,32,256]{3,2,1,0:T(8,128)(2,1)} %collective-permute-done.8.refs_3_.refs_8_, ...), custom_call_target="tpu_custom_call" | custom-call | tf_op jit(solution)/shard_map/pack/pallas_call | solution.py:257
  51.3 1.6 %collective-permute-start.11 = (bf16[2,57,16,256]{3,2,1,0:T(8,128)(2,1)S(1)}, bf16[2,57,16,256]{3,2,1,0:T(8,128)(2,1)S(1)}, u32[]{:S(2)}, u32[]{:S(2)}) collective-permute-start(bf16[2,57,16,256]{3,2,1,0:T(8,128)(2,1)S(1)} %get-tuple-element.27), channel_id=1, source_target_pairs={{0,2},{2,0},{4,6},{6,4},{8,10},{10,8},{12,14},{14,12},{16,18},{18,... | collective-permute-start | bytes 2801672 | tf_op jit(solution)/shard_map/ppermute | solution.py:34
  52.9 0.8 collective-permute-start.12
  53.8 0.0 collective-permute-done.7.refs_10_
  53.8 14.0 %attend.4.refs_4_ = bf16[2,1,16,32,256]{4,3,2,1,0:T(8,128)(2,1)S(1)} custom-call(s32[2,171]{1,0:T(2,128)S(1)} %copy-done.8, f32[2,12,1280]{2,1,0:T(8,128)S(1)} %copy-done.7, bf16[16,32,1536]{2,1,0:T(8,128)(2,1)S(1)} %copy-done, bf16[16,32,1536]{2,1,0:T(8,128)(2,1)} %refs_3_.9, bf16[16,32,1536]{2,1,0:T(8,128)(2,1)} %refs_4_.9, ...), custom_call_target="tpu_custom_call" | custom-call | flops 4362076160 | bytes 4096000 | tf_op jit(solution)/shard_map/attend/pallas_call | solution.py:516
  67.9 2.1 %pack.7 = (bf16[2,57,16,256]{3,2,1,0:T(8,128)(2,1)S(1)}, bf16[2,57,16,256]{3,2,1,0:T(8,128)(2,1)S(1)}) custom-call(bf16[16,32,1536]{2,1,0:T(8,128)(2,1)S(1)} %copy-done, bf16[16,32,1536]{2,1,0:T(8,128)(2,1)S(1)} %copy-done.2, bf16[9,16,32,256]{3,2,1,0:T(8,128)(2,1)S(1)} %copy-done.6, bf16[2,18,32,256]{3,2,1,0:T(8,128)(2,1)} %collective-permute-done.2.refs_3_.refs_8_, ...), custom_call_target="tpu_custom_call" | custom-call | tf_op jit(solution)/shard_map/pack/pallas_call | solution.py:257
  70.0 4.5 %collective-permute-start.9 = (bf16[2,57,16,256]{3,2,1,0:T(8,128)(2,1)S(1)}, bf16[2,57,16,256]{3,2,1,0:T(8,128)(2,1)S(1)}, u32[]{:S(2)}, u32[]{:S(2)}) collective-permute-start(bf16[2,57,16,256]{3,2,1,0:T(8,128)(2,1)S(1)} %get-tuple-element.25), channel_id=1, source_target_pairs={{0,2},{2,0},{4,6},{6,4},{8,10},{10,8},{12,14},{14,12},{16,18},{18,... | collective-permute-start | bytes 2801672 | tf_op jit(solution)/shard_map/ppermute | solution.py:34
  74.5 0.9 collective-permute-start.10
  75.4 0.0 collective-permute-done.12.refs_7_
  75.4 13.5 %attend.5.refs_9_ = bf16[2,1,16,32,256]{4,3,2,1,0:T(8,128)(2,1)S(1)} custom-call(s32[2,171]{1,0:T(2,128)S(1)} %copy-done.8, f32[2,12,1280]{2,1,0:T(8,128)S(1)} %copy-done.7, bf16[16,32,1536]{2,1,0:T(8,128)(2,1)S(1)} %copy-done, bf16[16,32,1536]{2,1,0:T(8,128)(2,1)} %refs_3_.9, bf16[16,32,1536]{2,1,0:T(8,128)(2,1)} %refs_4_.9, ...), custom_call_target="tpu_custom_call" | custom-call | flops 4362076160 | bytes 4096000 | tf_op jit(solution)/shard_map/attend/pallas_call | solution.py:516
  88.8 4.8 %collective-permute-done.9.refs_6_ = bf16[2,57,16,256]{3,2,1,0:T(8,128)(2,1)S(1)} collective-permute-done((bf16[2,57,16,256]{3,2,1,0:T(8,128)(2,1)S(1)}, bf16[2,57,16,256]{3,2,1,0:T(8,128)(2,1)S(1)}, u32[]{:S(2)}, u32[]{:S(2)}) %collective-permute-start.9) | collective-permute-done | bytes 933920 | tf_op jit(solution)/shard_map/ppermute | solution.py:34
  93.7 0.0 collective-permute-done.10.refs_7_
  93.7 7.6 %attend.6.refs_9_ = bf16[1,1,16,32,256]{4,3,2,1,0:T(8,128)(2,1)S(1)} custom-call(s32[2,171]{1,0:T(2,128)S(1)} %copy-done.8, f32[2,12,1280]{2,1,0:T(8,128)S(1)} %copy-done.7, bf16[16,32,1536]{2,1,0:T(8,128)(2,1)S(1)} %copy-done, bf16[16,32,1536]{2,1,0:T(8,128)(2,1)} %refs_3_.9, bf16[16,32,1536]{2,1,0:T(8,128)(2,1)} %refs_4_.9, ...), custom_call_target="tpu_custom_call" | custom-call | flops 2181038080 | bytes 4096000 | tf_op jit(solution)/shard_map/attend/pallas_call | solution.py:516
  101.3 0.0 collective-permute-done.14.refs_12_.refs_16_.refs_20_
  101.3 0.1 collective-permute-start.15
  101.4 0.1 slice_bitcast_fusion.1
  101.5 0.6 collective-permute-start.17
  102.0 1.2 collective-permute-start.18
  103.2 0.5 collective-permute-start.16
  103.7 0.1 slice_bitcast_fusion
  103.8 1.6 %collective-permute-start.19 = (bf16[1,16,32,256]{3,2,1,0:T(8,128)(2,1)S(1)}, bf16[1,16,32,256]{3,2,1,0:T(8,128)(2,1)S(1)}, u32[]{:S(2)}, u32[]{:S(2)}) collective-permute-start(bf16[1,16,32,256]{3,2,1,0:T(8,128)(2,1)S(1)} %get-tuple-element.30), channel_id=1, source_target_pairs={{0,1},{1,0},{2,3},{3,2},{4,5},{5,4},{6,7},{7,6},{8,9},{9,8},{10,11... | collective-permute-start | bytes 786440 | tf_op jit(solution)/shard_map/ppermute | solution.py:43
  105.4 7.6 %attend.7 = bf16[1,1,16,32,256]{4,3,2,1,0:T(8,128)(2,1)S(1)} custom-call(s32[2,171]{1,0:T(2,128)S(1)} %copy-done.8, f32[2,12,1280]{2,1,0:T(8,128)S(1)} %copy-done.7, bf16[16,32,1536]{2,1,0:T(8,128)(2,1)S(1)} %copy-done, bf16[16,32,1536]{2,1,0:T(8,128)(2,1)} %refs_3_.9, bf16[16,32,1536]{2,1,0:T(8,128)(2,1)} %refs_4_.9, bf16[9,16,32,256]{3,2,1,0:T(8,128)(2,1)} %copy-done.3, ...), custom_call_target="tpu_custom_call" | custom-call | flops 2181038080 | bytes 4096000 | tf_op jit(solution)/shard_map/attend/pallas_call | solution.py:516
  113.0 3.5 %collective-permute-done.16 = bf16[1,16,32,256]{3,2,1,0:T(8,128)(2,1)S(1)} collective-permute-done((bf16[1,16,32,256]{3,2,1,0:T(8,128)(2,1)S(1)}, bf16[1,16,32,256]{3,2,1,0:T(8,128)(2,1)S(1)}, u32[]{:S(2)}, u32[]{:S(2)}) %collective-permute-start.16) | collective-permute-done | bytes 262176 | tf_op jit(solution)/shard_map/ppermute | solution.py:43
  116.5 0.0 collective-permute-start.20
  116.5 0.0 collective-permute-done.17
  116.5 1.6 %collective-permute-start.21 = (bf16[1,16,32,256]{3,2,1,0:T(8,128)(2,1)S(1)}, bf16[1,16,32,256]{3,2,1,0:T(8,128)(2,1)S(1)}, u32[]{:S(2)}, u32[]{:S(2)}) collective-permute-start(bf16[1,16,32,256]{3,2,1,0:T(8,128)(2,1)S(1)} %get-tuple-element.29), channel_id=1, source_target_pairs={{0,9},{1,8},{8,1},{9,0},{16,25},{17,24},{24,17},{25,16},{2,11},{3,... | collective-permute-start | bytes 786440 | tf_op jit(solution)/shard_map/ppermute | solution.py:49
  118.1 0.5 collective-permute-start.22
  118.7 3.5 %collective-permute-done.19 = bf16[1,16,32,256]{3,2,1,0:T(8,128)(2,1)S(1)} collective-permute-done((bf16[1,16,32,256]{3,2,1,0:T(8,128)(2,1)S(1)}, bf16[1,16,32,256]{3,2,1,0:T(8,128)(2,1)S(1)}, u32[]{:S(2)}, u32[]{:S(2)}) %collective-permute-start.19) | collective-permute-done | bytes 262176 | tf_op jit(solution)/shard_map/ppermute | solution.py:43
  122.1 0.1 pad_add_fusion.2.spot_ref
  122.2 1.6 %collective-permute-start.13 = (bf16[1,16,32,256]{3,2,1,0:T(8,128)(2,1)S(1)}, bf16[1,16,32,256]{3,2,1,0:T(8,128)(2,1)S(1)}, u32[]{:S(2)}, u32[]{:S(2)}) collective-permute-start(bf16[1,16,32,256]{3,2,1,0:T(8,128)(2,1)S(1)} %bitcast.46), channel_id=1, source_target_pairs={{0,9},{1,8},{8,1},{9,0},{16,25},{17,24},{24,17},{25,16},{2,11},{3,... | collective-permute-start | bytes 786440 | tf_op jit(solution)/shard_map/ppermute | solution.py:49
  123.8 3.4 %collective-permute-done.21 = bf16[1,16,32,256]{3,2,1,0:T(8,128)(2,1)S(1)} collective-permute-done((bf16[1,16,32,256]{3,2,1,0:T(8,128)(2,1)S(1)}, bf16[1,16,32,256]{3,2,1,0:T(8,128)(2,1)S(1)}, u32[]{:S(2)}, u32[]{:S(2)}) %collective-permute-start.21) | collective-permute-done | bytes 262176 | tf_op jit(solution)/shard_map/ppermute | solution.py:49
  127.2 6.1 %collective-permute-done.22 = bf16[1,16,32,256]{3,2,1,0:T(8,128)(2,1)S(1)} collective-permute-done((bf16[1,16,32,256]{3,2,1,0:T(8,128)(2,1)S(1)}, bf16[1,16,32,256]{3,2,1,0:T(8,128)(2,1)S(1)}, u32[]{:S(2)}, u32[]{:S(2)}) %collective-permute-start.22) | collective-permute-done | bytes 262176 | tf_op jit(solution)/shard_map/ppermute | solution.py:43
  133.4 7.6 %project.2.refs_2_ = f32[512,1536]{1,0:T(8,128)S(1)} custom-call(s32[2]{0:T(128)S(1)} %pad_add_fusion.2.spot_ref, bf16[512,256]{1,0:T(8,128)(2,1)S(1)} %bitcast.35, bf16[512,256]{1,0:T(8,128)(2,1)S(1)} %bitcast.39, bf16[512,256]{1,0:T(8,128)(2,1)S(1)} %bitcast.37, bf16[512,256]{1,0:T(8,128)(2,1)S(1)} %bitcast.38, bf16[512,256]{1,0:T(8,128)(2,1)S(1)} %bitcast.36, ...), custom_call_target="tpu_custom_call" | custom-call | flops 4429185024 | bytes 8650752 | tf_op jit(solution)/shard_map/project/pallas_call | solution.py:572
  141.0 0.0 collective-permute-done.13
  141.0 2.9 %project.3 = bf16[512,1536]{1,0:T(8,128)(2,1)} custom-call(s32[2]{0:T(128)S(1)} %pad_add_fusion.2.spot_ref, bf16[512,256]{1,0:T(8,128)(2,1)S(1)} %bitcast.47, bf16[768,1536]{1,0:T(8,128)(2,1)S(1)} %collective-permute-done.15.refs_14_.refs_18_.refs_1_, f32[512,1536]{1,0:T(8,128)S(1)} %project.2.refs_2_), custom_call_target="tpu_custom_call" | custom-call | flops 402653184 | bytes 786432 | tf_op jit(solution)/shard_map/project/pallas_call | solution.py:572
  (29 shorter events, 0.1 us)
Async XLA Ops:
  0.0 7.9 %copy-start = (bf16[16,32,1536]{2,1,0:T(8,128)(2,1)S(1)}, bf16[16,32,1536]{2,1,0:T(8,128)(2,1)}, u32[]{:S(2)}) copy-start(bf16[16,32,1536]{2,1,0:T(8,128)(2,1)} %refs_2_.9) | copy-start | bytes 4718596
  0.0 7.9 %copy-start.1 = (bf16[16,32,1536]{2,1,0:T(8,128)(2,1)S(1)}, bf16[16,32,1536]{2,1,0:T(8,128)(2,1)}, u32[]{:S(2)}) copy-start(bf16[16,32,1536]{2,1,0:T(8,128)(2,1)} %refs_3_.9) | copy-start | bytes 4718596
  3.0 4.9 %collective-permute-start.1 = (bf16[9,16,32,256]{3,2,1,0:T(8,128)(2,1)}, bf16[9,16,32,256]{3,2,1,0:T(8,128)(2,1)S(1)}, u32[]{:S(2)}, u32[]{:S(2)}) collective-permute-start(bf16[9,16,32,256]{3,2,1,0:T(8,128)(2,1)} %give_half.1), channel_id=1, source_target_pairs={{0,8},{8,0},{16,24},{24,16},{1,9},{9,1},{17,25},{25,17},{2,10},{10... | collective-permute-start | bytes 7077896 | tf_op jit(solution)/shard_map/ppermute | solution.py:39
  7.9 2.1 %copy-start.3 = (bf16[9,16,32,256]{3,2,1,0:T(8,128)(2,1)}, bf16[9,16,32,256]{3,2,1,0:T(8,128)(2,1)S(1)}, u32[]{:S(2)}) copy-start(bf16[9,16,32,256]{3,2,1,0:T(8,128)(2,1)S(1)} %collective-permute-done.1.refs_2_.refs_5_) | copy-start | bytes 7077892
  10.0 17.4 %collective-permute-start.5 = (bf16[2,18,32,256]{3,2,1,0:T(8,128)(2,1)}, bf16[2,18,32,256]{3,2,1,0:T(8,128)(2,1)}, u32[]{:S(2)}, u32[]{:S(2)}) collective-permute-start(bf16[2,18,32,256]{3,2,1,0:T(8,128)(2,1)} %get-tuple-element.20), channel_id=1, source_target_pairs={{0,16},{8,24},{16,0},{24,8},{1,17},{9,25},{17,1},{25,9},{2,18},{10... | collective-permute-start | bytes 1769480 | tf_op jit(solution)/shard_map/ppermute | solution.py:53
  12.9 18.6 %collective-permute-start.3 = (bf16[2,36,16,256]{3,2,1,0:T(8,128)(2,1)}, bf16[2,36,16,256]{3,2,1,0:T(8,128)(2,1)}, u32[]{:S(2)}, u32[]{:S(2)}) collective-permute-start(bf16[2,36,16,256]{3,2,1,0:T(8,128)(2,1)} %get-tuple-element.19), channel_id=1, source_target_pairs={{0,2},{2,0},{4,6},{6,4},{8,10},{10,8},{12,14},{14,12},{16,18},{18,... | collective-permute-start | bytes 1769480 | tf_op jit(solution)/shard_map/ppermute | solution.py:34
  14.5 4.9 %copy-start.4 = (bf16[9,16,32,256]{3,2,1,0:T(8,128)(2,1)S(1)}, bf16[9,16,32,256]{3,2,1,0:T(8,128)(2,1)}, u32[]{:S(2)}) copy-start(bf16[9,16,32,256]{3,2,1,0:T(8,128)(2,1)} %copy-done.3) | copy-start | bytes 7077892
  17.9 83.4 %collective-permute-start.14 = (bf16[768,1536]{1,0:T(8,128)(2,1)}, bf16[768,1536]{1,0:T(8,128)(2,1)}, u32[]{:S(2)}, u32[]{:S(2)}) collective-permute-start(bf16[768,1536]{1,0:T(8,128)(2,1)} %dynamic_slice.3), channel_id=1, source_target_pairs={{0,1},{1,0},{2,3},{3,2},{4,5},{5,4},{6,7},{7,6},{8,9},{9,8},{10,11... | collective-permute-start | bytes 7077896 | tf_op jit(solution)/shard_map/ppermute | solution.py:43
  19.4 4.1 %copy-start.10 = (s32[1,1,13,13]{3,1,2,0:T(1,128)S(1)}, s32[1,1,13,13]{3,1,2,0:T(1,128)}, u32[]{:S(2)}) copy-start(s32[1,1,13,13]{3,1,2,0:T(1,128)} %param.11) | copy-start | bytes 2032
  20.6 0.9 copy-start.9
  21.5 18.0 %collective-permute-start.8 = (bf16[2,18,32,256]{3,2,1,0:T(8,128)(2,1)}, bf16[2,18,32,256]{3,2,1,0:T(8,128)(2,1)}, u32[]{:S(2)}, u32[]{:S(2)}) collective-permute-start(bf16[2,18,32,256]{3,2,1,0:T(8,128)(2,1)} %get-tuple-element.23), channel_id=1, source_target_pairs={{0,16},{8,24},{16,0},{24,8},{1,17},{9,25},{17,1},{25,9},{2,18},{10... | collective-permute-start | bytes 1769480 | tf_op jit(solution)/shard_map/ppermute | solution.py:53
  22.1 29.2 %collective-permute-start.4 = (bf16[2,36,16,256]{3,2,1,0:T(8,128)(2,1)}, bf16[2,36,16,256]{3,2,1,0:T(8,128)(2,1)}, u32[]{:S(2)}, u32[]{:S(2)}) collective-permute-start(bf16[2,36,16,256]{3,2,1,0:T(8,128)(2,1)} %get-tuple-element.17.refs_3_), channel_id=1, source_target_pairs={{2,4},{4,2},{10,12},{12,10},{18,20},{20,18},{26,28},{28,26},{3,5},... | collective-permute-start | bytes 1769480 | tf_op jit(solution)/shard_map/ppermute | solution.py:34
  27.4 1.9 %collective-permute-start = (s32[171]{0:T(256)S(1)}, s32[171]{0:T(256)S(1)}, u32[]{:S(2)}, u32[]{:S(2)}) collective-permute-start(s32[171]{0:T(256)S(1)} %pad_add_fusion.1), channel_id=1, source_target_pairs={{0,8},{8,0},{16,24},{24,16},{1,9},{9,1},{17,25},{25,17},{2,10},{10... | collective-permute-start | bytes 2060 | tf_op jit(solution)/shard_map/ppermute | solution.py:39
  29.3 23.6 %collective-permute-start.6 = (bf16[2,21,16,256]{3,2,1,0:T(8,128)(2,1)}, bf16[2,21,16,256]{3,2,1,0:T(8,128)(2,1)}, u32[]{:S(2)}, u32[]{:S(2)}) collective-permute-start(bf16[2,21,16,256]{3,2,1,0:T(8,128)(2,1)} %get-tuple-element.21), channel_id=1, source_target_pairs={{0,2},{2,0},{4,6},{6,4},{8,10},{10,8},{12,14},{14,12},{16,18},{18,... | collective-permute-start | bytes 1032200 | tf_op jit(solution)/shard_map/ppermute | solution.py:34
  31.5 22.2 %collective-permute-start.7 = (bf16[2,21,16,256]{3,2,1,0:T(8,128)(2,1)S(1)}, bf16[2,21,16,256]{3,2,1,0:T(8,128)(2,1)}, u32[]{:S(2)}, u32[]{:S(2)}) collective-permute-start(bf16[2,21,16,256]{3,2,1,0:T(8,128)(2,1)S(1)} %get-tuple-element.22.refs_4_), channel_id=1, source_target_pairs={{2,4},{4,2},{10,12},{12,10},{18,20},{20,18},{26,28},{28,26},{3,5},... | collective-permute-start | bytes 1032200 | tf_op jit(solution)/shard_map/ppermute | solution.py:34
  39.4 28.4 %collective-permute-start.2 = (bf16[2,18,32,256]{3,2,1,0:T(8,128)(2,1)}, bf16[2,18,32,256]{3,2,1,0:T(8,128)(2,1)}, u32[]{:S(2)}, u32[]{:S(2)}) collective-permute-start(bf16[2,18,32,256]{3,2,1,0:T(8,128)(2,1)} %copy-done.9), channel_id=1, source_target_pairs={{0,16},{8,24},{16,0},{24,8},{1,17},{9,25},{17,1},{25,9},{2,18},{10... | collective-permute-start | bytes 1769480 | tf_op jit(solution)/shard_map/ppermute | solution.py:53
  47.5 1.7 %copy-start.5 = (bf16[9,16,32,256]{3,2,1,0:T(8,128)(2,1)S(1)}, bf16[9,16,32,256]{3,2,1,0:T(8,128)(2,1)}, u32[]{:S(2)}) copy-start(bf16[9,16,32,256]{3,2,1,0:T(8,128)(2,1)} %copy-done.3) | copy-start | bytes 7077892
  49.1 4.6 %copy-start.7 = (f32[2,12,1280]{2,1,0:T(8,128)S(1)}, f32[2,12,1280]{2,1,0:T(8,128)}, u32[]{:S(2)}) copy-start(f32[2,12,1280]{2,1,0:T(8,128)} %tables.1.refs_1_) | copy-start | bytes 368644
  49.2 4.6 %copy-start.8 = (s32[2,171]{1,0:T(2,128)S(1)}, s32[2,171]{1,0:T(2,128)}, u32[]{:S(2)}) copy-start(s32[2,171]{1,0:T(2,128)} %pad_add_fusion.refs_0_.refs_1_) | copy-start | bytes 4108
  51.3 24.1 %collective-permute-start.11 = (bf16[2,57,16,256]{3,2,1,0:T(8,128)(2,1)S(1)}, bf16[2,57,16,256]{3,2,1,0:T(8,128)(2,1)S(1)}, u32[]{:S(2)}, u32[]{:S(2)}) collective-permute-start(bf16[2,57,16,256]{3,2,1,0:T(8,128)(2,1)S(1)} %get-tuple-element.27), channel_id=1, source_target_pairs={{0,2},{2,0},{4,6},{6,4},{8,10},{10,8},{12,14},{14,12},{16,18},{18,... | collective-permute-start | bytes 2801672 | tf_op jit(solution)/shard_map/ppermute | solution.py:34
  52.9 14.9 %copy-start.2 = (bf16[16,32,1536]{2,1,0:T(8,128)(2,1)S(1)}, bf16[16,32,1536]{2,1,0:T(8,128)(2,1)}, u32[]{:S(2)}) copy-start(bf16[16,32,1536]{2,1,0:T(8,128)(2,1)} %refs_3_.9) | copy-start | bytes 4718596
  52.9 15.0 %copy-start.6 = (bf16[9,16,32,256]{3,2,1,0:T(8,128)(2,1)S(1)}, bf16[9,16,32,256]{3,2,1,0:T(8,128)(2,1)}, u32[]{:S(2)}) copy-start(bf16[9,16,32,256]{3,2,1,0:T(8,128)(2,1)} %copy-done.3) | copy-start | bytes 7077892
  52.9 22.5 %collective-permute-start.12 = (bf16[2,57,16,256]{3,2,1,0:T(8,128)(2,1)S(1)}, bf16[2,57,16,256]{3,2,1,0:T(8,128)(2,1)S(1)}, u32[]{:S(2)}, u32[]{:S(2)}) collective-permute-start(bf16[2,57,16,256]{3,2,1,0:T(8,128)(2,1)S(1)} %get-tuple-element.24.refs_11_), channel_id=1, source_target_pairs={{2,4},{4,2},{10,12},{12,10},{18,20},{20,18},{26,28},{28,26},{3,5},... | collective-permute-start | bytes 2801672 | tf_op jit(solution)/shard_map/ppermute | solution.py:34
  70.0 23.7 %collective-permute-start.9 = (bf16[2,57,16,256]{3,2,1,0:T(8,128)(2,1)S(1)}, bf16[2,57,16,256]{3,2,1,0:T(8,128)(2,1)S(1)}, u32[]{:S(2)}, u32[]{:S(2)}) collective-permute-start(bf16[2,57,16,256]{3,2,1,0:T(8,128)(2,1)S(1)} %get-tuple-element.25), channel_id=1, source_target_pairs={{0,2},{2,0},{4,6},{6,4},{8,10},{10,8},{12,14},{14,12},{16,18},{18,... | collective-permute-start | bytes 2801672 | tf_op jit(solution)/shard_map/ppermute | solution.py:34
  74.5 19.2 %collective-permute-start.10 = (bf16[2,57,16,256]{3,2,1,0:T(8,128)(2,1)S(1)}, bf16[2,57,16,256]{3,2,1,0:T(8,128)(2,1)S(1)}, u32[]{:S(2)}, u32[]{:S(2)}) collective-permute-start(bf16[2,57,16,256]{3,2,1,0:T(8,128)(2,1)S(1)} %get-tuple-element.26.refs_9_), channel_id=1, source_target_pairs={{2,4},{4,2},{10,12},{12,10},{18,20},{20,18},{26,28},{28,26},{3,5},... | collective-permute-start | bytes 2801672 | tf_op jit(solution)/shard_map/ppermute | solution.py:34
  101.3 32.1 %collective-permute-start.15 = (bf16[768,1536]{1,0:T(8,128)(2,1)}, bf16[768,1536]{1,0:T(8,128)(2,1)S(1)}, u32[]{:S(2)}, u32[]{:S(2)}) collective-permute-start(bf16[768,1536]{1,0:T(8,128)(2,1)} %collective-permute-done.14.refs_12_.refs_16_.refs_20_), channel_id=1, source_target_pairs={{0,8},{8,0},{16,24},{24,16},{1,9},{9,1},{17,25},{25,17},{2,10},{10... | collective-permute-start | bytes 7077896 | tf_op jit(solution)/shard_map/ppermute | solution.py:39
  101.5 15.0 %collective-permute-start.17 = (bf16[1,16,32,256]{3,2,1,0:T(8,128)(2,1)S(1)}, bf16[1,16,32,256]{3,2,1,0:T(8,128)(2,1)S(1)}, u32[]{:S(2)}, u32[]{:S(2)}) collective-permute-start(bf16[1,16,32,256]{3,2,1,0:T(8,128)(2,1)S(1)} %get-tuple-element.32), channel_id=1, source_target_pairs={{0,8},{8,0},{16,24},{24,16},{1,9},{9,1},{17,25},{25,17},{2,10},{10... | collective-permute-start | bytes 786440 | tf_op jit(solution)/shard_map/ppermute | solution.py:39
  102.0 16.1 %collective-permute-start.18 = (bf16[1,16,32,256]{3,2,1,0:T(8,128)(2,1)S(1)}, bf16[1,16,32,256]{3,2,1,0:T(8,128)(2,1)S(1)}, u32[]{:S(2)}, u32[]{:S(2)}) collective-permute-start(bf16[1,16,32,256]{3,2,1,0:T(8,128)(2,1)S(1)} %get-tuple-element.32), channel_id=1, source_target_pairs={{0,9},{1,8},{8,1},{9,0},{16,25},{17,24},{24,17},{25,16},{2,11},{3,... | collective-permute-start | bytes 786440 | tf_op jit(solution)/shard_map/ppermute | solution.py:49
  103.2 13.3 %collective-permute-start.16 = (bf16[1,16,32,256]{3,2,1,0:T(8,128)(2,1)S(1)}, bf16[1,16,32,256]{3,2,1,0:T(8,128)(2,1)S(1)}, u32[]{:S(2)}, u32[]{:S(2)}) collective-permute-start(bf16[1,16,32,256]{3,2,1,0:T(8,128)(2,1)S(1)} %get-tuple-element.33), channel_id=1, source_target_pairs={{0,1},{1,0},{2,3},{3,2},{4,5},{5,4},{6,7},{7,6},{8,9},{9,8},{10,11... | collective-permute-start | bytes 786440 | tf_op jit(solution)/shard_map/ppermute | solution.py:43
  103.8 18.3 %collective-permute-start.19 = (bf16[1,16,32,256]{3,2,1,0:T(8,128)(2,1)S(1)}, bf16[1,16,32,256]{3,2,1,0:T(8,128)(2,1)S(1)}, u32[]{:S(2)}, u32[]{:S(2)}) collective-permute-start(bf16[1,16,32,256]{3,2,1,0:T(8,128)(2,1)S(1)} %get-tuple-element.30), channel_id=1, source_target_pairs={{0,1},{1,0},{2,3},{3,2},{4,5},{5,4},{6,7},{7,6},{8,9},{9,8},{10,11... | collective-permute-start | bytes 786440 | tf_op jit(solution)/shard_map/ppermute | solution.py:43
  116.5 5.7 %collective-permute-start.20 = (bf16[1,16,32,256]{3,2,1,0:T(8,128)(2,1)S(1)}, bf16[1,16,32,256]{3,2,1,0:T(8,128)(2,1)S(1)}, u32[]{:S(2)}, u32[]{:S(2)}) collective-permute-start(bf16[1,16,32,256]{3,2,1,0:T(8,128)(2,1)S(1)} %get-tuple-element.29), channel_id=1, source_target_pairs={{0,8},{8,0},{16,24},{24,16},{1,9},{9,1},{17,25},{25,17},{2,10},{10... | collective-permute-start | bytes 786440 | tf_op jit(solution)/shard_map/ppermute | solution.py:39
  116.5 10.7 %collective-permute-start.21 = (bf16[1,16,32,256]{3,2,1,0:T(8,128)(2,1)S(1)}, bf16[1,16,32,256]{3,2,1,0:T(8,128)(2,1)S(1)}, u32[]{:S(2)}, u32[]{:S(2)}) collective-permute-start(bf16[1,16,32,256]{3,2,1,0:T(8,128)(2,1)S(1)} %get-tuple-element.29), channel_id=1, source_target_pairs={{0,9},{1,8},{8,1},{9,0},{16,25},{17,24},{24,17},{25,16},{2,11},{3,... | collective-permute-start | bytes 786440 | tf_op jit(solution)/shard_map/ppermute | solution.py:49
  118.1 15.2 %collective-permute-start.22 = (bf16[1,16,32,256]{3,2,1,0:T(8,128)(2,1)S(1)}, bf16[1,16,32,256]{3,2,1,0:T(8,128)(2,1)S(1)}, u32[]{:S(2)}, u32[]{:S(2)}) collective-permute-start(bf16[1,16,32,256]{3,2,1,0:T(8,128)(2,1)S(1)} %bitcast.33), channel_id=1, source_target_pairs={{0,1},{1,0},{2,3},{3,2},{4,5},{5,4},{6,7},{7,6},{8,9},{9,8},{10,11... | collective-permute-start | bytes 786440 | tf_op jit(solution)/shard_map/ppermute | solution.py:43
  122.1 11.2 %collective-permute-start.23 = (bf16[1,16,32,256]{3,2,1,0:T(8,128)(2,1)S(1)}, bf16[1,16,32,256]{3,2,1,0:T(8,128)(2,1)S(1)}, u32[]{:S(2)}, u32[]{:S(2)}) collective-permute-start(bf16[1,16,32,256]{3,2,1,0:T(8,128)(2,1)S(1)} %bitcast.45), channel_id=1, source_target_pairs={{0,8},{8,0},{16,24},{24,16},{1,9},{9,1},{17,25},{25,17},{2,10},{10... | collective-permute-start | bytes 786440 | tf_op jit(solution)/shard_map/ppermute | solution.py:39
  122.2 18.8 %collective-permute-start.13 = (bf16[1,16,32,256]{3,2,1,0:T(8,128)(2,1)S(1)}, bf16[1,16,32,256]{3,2,1,0:T(8,128)(2,1)S(1)}, u32[]{:S(2)}, u32[]{:S(2)}) collective-permute-start(bf16[1,16,32,256]{3,2,1,0:T(8,128)(2,1)S(1)} %bitcast.46), channel_id=1, source_target_pairs={{0,9},{1,8},{8,1},{9,0},{16,25},{17,24},{24,17},{25,16},{2,11},{3,... | collective-permute-start | bytes 786440 | tf_op jit(solution)/shard_map/ppermute | solution.py:49

commit v3 on v2

--- a/solution.py
+++ b/solution.py
@@ -537,7 +537,7 @@
 def project(spots, terms, out_weight, far_weights, half_feats, before, dtype):
     tokens, feats = terms[0][2].shape
     model = far_weights[0].shape[1]
-    block = model // 3
+    block = model // 2
     per_half = half_feats // feats
     columns = model // block
     whole = pl.BlockSpec((tokens, feats), lambda n, spot: (0, 0))
@@ -619,8 +619,13 @@
     *edges, first, second = pack(
         key_map, value_map, recv, 0, feats, downs, lows[:1], [], True, []
     )
+    own_wires = [[first, second]]
     if downs and lows[1:]:
-        edges += pack(key_map, value_map, recv, 0, feats, downs, lows[1:], [], False, [second])
+        *more, first, second = pack(
+            key_map, value_map, recv, lows[1], feats, downs, lows[1:], [], True, [second]
+        )
+        edges += more
+        own_wires.append([first, second])
     middles = []
     for n in range(total_groups):
         if pairs_count == 2:
@@ -632,8 +637,9 @@
     order = []
 
     def prepare(n):
-        halos, wires = [], [first, second]
-        if n == 0:
+        halos = []
+        if n < len(own_wires):
+            wires = own_wires[n]
             for middle, row_ok in zip(middles[n], row_oks):
                 outs = pack_halo(middle, order[-1:])
                 order.append(outs[1])
@@ -656,7 +662,7 @@
     for index, (n, tiles) in enumerate(calls):
         sides, halos = ready[n]
         done = attend(
-            dims, base, key_map, value_map, query_map, recv, *sides, halos, n > 0, order[-1:],
+            dims, base, key_map, value_map, query_map, recv, *sides, halos, n >= len(own_wires), order[-1:],
             lows[n], feats, slots, tiles, 2 * n, 2 * total_groups + n,
         )
         if index == len(calls) - 2:

time: 146 us -> 161 us (1.10)
  waiting for transfers between devices: 34.5 us -> 50.5 us
  Pallas kernels: 68.1 us -> 65.1 us
  starting transfers between devices: 29.5 us -> 32.3 us
    ppermute x8 -> x10, waiting for transfers between devices: 4.85 us -> 23.7 us  [col_swap_where(): return lax.ppermute(value, ('row', 'col'), pairs)]
    ppermute x3, waiting for transfers between devices: 8.82 us -> 5.9 us  [row_pair_swap(): return lax.ppermute(value, 'row', [(s, s ^ 2) for s in range(4)])]
    pallas_call x4 -> x3, Pallas kernels: 7.24 us -> 4.45 us  [pack(): pl.pallas_call(body, out_shape=[jax.ShapeDtypeStruct((2, HALO, cols, feat...]
    ppermute x8 -> x10, starting transfers between devices: 14.5 us -> 17.3 us  [col_swap_where(): return lax.ppermute(value, ('row', 'col'), pairs)]
    unnamed x22 -> x28, local copies, waits for them, and re-layouts: 2.73 us -> 4.2 us
  transfers between devices with their start and end apart: 24 -> 26, of which waited for: 8 -> 8; matrix products, arithmetic and copies ran while one was open for 5% -> 4% of each run, Pallas kernels for 42% -> 36%
where the time goes in v3:
time: 161 us; the launch traced here: 160 us
  Pallas kernels  65.1 us (40%)
  waiting for transfers between devices  50.5 us (31%)
  starting transfers between devices  32.3 us (20%)
  local copies, waits for them, and re-layouts  9.39 us (6%)
    pallas_call x4, Pallas kernels, attend(): pl.pallas_call(body, out_shape=jax.ShapeDtypeStruct((len(tiles), groups,...  42.6 us
    ppermute x10, waiting for transfers between devices, col_swap_where(): return lax.ppermute(value, ('row', 'col'), pairs)  23.7 us
    ppermute x10, starting transfers between devices, col_swap_where(): return lax.ppermute(value, ('row', 'col'), pairs)  17.3 us
    ppermute x4, waiting for transfers between devices, head_swap(): return lax.ppermute(value, 'head', [(0, 1), (1, 0)])  13.1 us
    pallas_call x2, Pallas kernels, project(): pl.pallas_call(body, grid_spec=pltpu.PrefetchScalarGridSpec(num_scalar_pr...  10.2 us
    ppermute x3, waiting for transfers between devices, row_pair_swap(): return lax.ppermute(value, 'row', [(s, s ^ 2) for s in range(4)])  5.9 us
    ppermute x3, starting transfers between devices, row_pair_swap(): return lax.ppermute(value, 'row', [(s, s ^ 2) for s in range(4)])  5.27 us
    ppermute x3, starting transfers between devices, head_partner(): return lax.ppermute(value, ('row', 'head'), pairs)  4.51 us
  transfers between devices with their start and end apart: 26, of which 8 were waited for; matrix products, arithmetic and copies ran while one was open for 4% of the time, Pallas kernels for 36%

profile of v3, /device:TPU:0, one launch (start us, length us, event | category | flops | bytes accessed | tf_op | source)
XLA Modules:
  0.0 159.7 jit_solution(9694165565290513411)
XLA Ops:
  0.0 3.1 %give_half.1 = bf16[9,16,32,256]{3,2,1,0:T(8,128)(2,1)} custom-call(s32[1]{0:T(128)} %bitcast.parity_ref, bf16[16,32,1536]{2,1,0:T(8,128)(2,1)} %refs_2_.9, bf16[16,32,1536]{2,1,0:T(8,128)(2,1)} %refs_3_.9, bf16[16,32,1536]{2,1,0:T(8,128)(2,1)} %refs_2_.9, bf16[16,32,1536]{2,1,0:T(8,128)(2,1)} %refs_3_.9, bf16[16,32,1536]{2,1,0:T(8,128)(2,1)} %refs_2_.9, ...), custom_call_target="tpu_custom_call" | custom-call | tf_op jit(solution)/shard_map/give_half/pallas_call | solution.py:107
  3.1 0.5 collective-permute-start.1
  3.6 4.4 %collective-permute-done.1.refs_2_.refs_5_ = bf16[9,16,32,256]{3,2,1,0:T(8,128)(2,1)S(1)} collective-permute-done((bf16[9,16,32,256]{3,2,1,0:T(8,128)(2,1)}, bf16[9,16,32,256]{3,2,1,0:T(8,128)(2,1)S(1)}, u32[]{:S(2)}, u32[]{:S(2)}) %collective-permute-start.1) | collective-permute-done | bytes 2359328 | tf_op jit(solution)/shard_map/ppermute | solution.py:39
  7.9 2.0 %pack.3 = (bf16[2,18,32,256]{3,2,1,0:T(8,128)(2,1)}, bf16[2,36,16,256]{3,2,1,0:T(8,128)(2,1)}, bf16[2,36,16,256]{3,2,1,0:T(8,128)(2,1)}) custom-call(bf16[16,32,1536]{2,1,0:T(8,128)(2,1)S(1)} %copy-done, bf16[16,32,1536]{2,1,0:T(8,128)(2,1)S(1)} %copy-done.1, bf16[9,16,32,256]{3,2,1,0:T(8,128)(2,1)S(1)} %collective-permute-done.1.refs_2_.refs_5_), custom_call_target="tpu_custom_call" | custom-call | tf_op jit(solution)/shard_map/pack/pallas_call | solution.py:257
  9.9 0.1 copy-done.3
  10.0 2.9 %collective-permute-start.5 = (bf16[2,18,32,256]{3,2,1,0:T(8,128)(2,1)}, bf16[2,18,32,256]{3,2,1,0:T(8,128)(2,1)}, u32[]{:S(2)}, u32[]{:S(2)}) collective-permute-start(bf16[2,18,32,256]{3,2,1,0:T(8,128)(2,1)} %get-tuple-element.22), channel_id=1, source_target_pairs={{0,16},{8,24},{16,0},{24,8},{1,17},{9,25},{17,1},{25,9},{2,18},{10... | collective-permute-start | bytes 1769480 | tf_op jit(solution)/shard_map/ppermute | solution.py:53
  12.9 1.6 collective-permute-start.3
  14.5 3.4 %dynamic_slice.3 = bf16[768,1536]{1,0:T(8,128)(2,1)} dynamic-slice(bf16[1536,3072]{1,0:T(8,128)(2,1)} %refs_21_.1, s32[]{:T(128)S(6)} %select_n.14, s32[]{:T(128)S(6)} %select_n.15), dynamic_slice_sizes={768,1536} | dynamic-slice | bytes 4718596 | tf_op jit(solution)/shard_map/dynamic_slice | solution.py:654
  17.9 1.5 collective-permute-start.16
  19.4 1.4 pack.4
  20.8 0.8 copy-done.10
  21.7 0.8 copy-done.11
  22.5 0.8 copy-done.12
  23.3 0.6 collective-permute-start.8
  23.9 1.5 collective-permute-start.4
  25.4 0.1 reshape_squeeze.12
  26.8 0.1 pad_add_fusion.1
  26.9 0.6 collective-permute-done.5.in_ref.refs_8_
  27.4 0.0 collective-permute-start
  27.4 1.9 %pack_halo.2 = (bf16[2,21,16,256]{3,2,1,0:T(8,128)(2,1)}, bf16[2,21,16,256]{3,2,1,0:T(8,128)(2,1)S(1)}) custom-call(bf16[2,18,32,256]{3,2,1,0:T(8,128)(2,1)} %collective-permute-done.5.in_ref.refs_8_), custom_call_target="tpu_custom_call" | custom-call | tf_op jit(solution)/shard_map/pack_halo/pallas_call | solution.py:296
  29.3 0.0 collective-permute-done
  29.3 3.3 %collective-permute-start.6 = (bf16[2,21,16,256]{3,2,1,0:T(8,128)(2,1)}, bf16[2,21,16,256]{3,2,1,0:T(8,128)(2,1)S(1)}, u32[]{:S(2)}, u32[]{:S(2)}) collective-permute-start(bf16[2,21,16,256]{3,2,1,0:T(8,128)(2,1)} %get-tuple-element.23), channel_id=1, source_target_pairs={{0,2},{2,0},{4,6},{6,4},{8,10},{10,8},{12,14},{14,12},{16,18},{18,... | collective-permute-start | bytes 1032200 | tf_op jit(solution)/shard_map/ppermute | solution.py:34
  32.6 0.0 collective-permute-done.3.refs_6_
  32.6 1.4 collective-permute-start.7
  34.0 5.3 %collective-permute-done.8.in_ref.refs_8_ = bf16[2,18,32,256]{3,2,1,0:T(8,128)(2,1)S(1)} collective-permute-done((bf16[2,18,32,256]{3,2,1,0:T(8,128)(2,1)}, bf16[2,18,32,256]{3,2,1,0:T(8,128)(2,1)S(1)}, u32[]{:S(2)}, u32[]{:S(2)}) %collective-permute-start.8) | collective-permute-done | bytes 589856 | tf_op jit(solution)/shard_map/ppermute | solution.py:53
  39.3 1.7 %collective-permute-start.2 = (bf16[2,18,32,256]{3,2,1,0:T(8,128)(2,1)}, bf16[2,18,32,256]{3,2,1,0:T(8,128)(2,1)S(1)}, u32[]{:S(2)}, u32[]{:S(2)}) collective-permute-start(bf16[2,18,32,256]{3,2,1,0:T(8,128)(2,1)} %copy-done.12), channel_id=1, source_target_pairs={{0,16},{8,24},{16,0},{24,8},{1,17},{9,25},{17,1},{25,9},{2,18},{10... | collective-permute-start | bytes 1769480 | tf_op jit(solution)/shard_map/ppermute | solution.py:53
  41.1 0.9 reshape.33
  42.0 0.7 copy.10.refs_2_
  42.6 0.6 pad_add_fusion.refs_0_.refs_1_
  43.2 2.6 %tables.1.refs_1_ = f32[2,12,1280]{2,1,0:T(8,128)} custom-call(s32[2,171]{1,0:T(2,128)} %pad_add_fusion.refs_0_.refs_1_, s32[2,171]{1,0:T(2,128)} %pad_add_fusion.refs_0_.refs_1_, f32[24,169]{1,0:T(8,128)} %copy.10.refs_2_), custom_call_target="tpu_custom_call" | custom-call | tf_op jit(solution)/shard_map/tables/pallas_call | solution.py:86
  45.9 0.3 pack_halo.3
  46.2 0.0 collective-permute-done.4.refs_7_
  46.2 1.6 %collective-permute-start.11 = (bf16[2,36,16,256]{3,2,1,0:T(8,128)(2,1)}, bf16[2,36,16,256]{3,2,1,0:T(8,128)(2,1)S(1)}, u32[]{:S(2)}, u32[]{:S(2)}) collective-permute-start(bf16[2,36,16,256]{3,2,1,0:T(8,128)(2,1)} %copy-done.11), channel_id=1, source_target_pairs={{0,2},{2,0},{4,6},{6,4},{8,10},{10,8},{12,14},{14,12},{16,18},{18,... | collective-permute-start | bytes 1769480 | tf_op jit(solution)/shard_map/ppermute | solution.py:34
  47.9 0.7 collective-permute-start.12
  48.6 0.0 collective-permute-done.7.refs_10_
  48.6 0.9 copy-done.6
  49.5 0.7 copy-done.8
  50.2 14.1 %attend.4.refs_4_ = bf16[2,1,16,32,256]{4,3,2,1,0:T(8,128)(2,1)S(1)} custom-call(s32[2,171]{1,0:T(2,128)S(1)} %copy-done.8, f32[2,12,1280]{2,1,0:T(8,128)S(1)} %copy-done.6, bf16[16,32,1536]{2,1,0:T(8,128)(2,1)S(1)} %copy-done, bf16[16,32,1536]{2,1,0:T(8,128)(2,1)} %refs_3_.9, bf16[16,32,1536]{2,1,0:T(8,128)(2,1)} %refs_4_.9, ...), custom_call_target="tpu_custom_call" | custom-call | flops 4362076160 | bytes 4096000 | tf_op jit(solution)/shard_map/attend/pallas_call | solution.py:516
  64.3 1.1 pack.5
  65.4 4.4 %collective-permute-start.9 = (bf16[2,57,16,256]{3,2,1,0:T(8,128)(2,1)S(1)}, bf16[2,57,16,256]{3,2,1,0:T(8,128)(2,1)S(1)}, u32[]{:S(2)}, u32[]{:S(2)}) collective-permute-start(bf16[2,57,16,256]{3,2,1,0:T(8,128)(2,1)S(1)} %get-tuple-element.27), channel_id=1, source_target_pairs={{0,2},{2,0},{4,6},{6,4},{8,10},{10,8},{12,14},{14,12},{16,18},{18,... | collective-permute-start | bytes 2801672 | tf_op jit(solution)/shard_map/ppermute | solution.py:34
  69.8 0.7 collective-permute-start.10
  70.5 1.4 collective-permute-start.13
  71.9 0.9 collective-permute-start.14
  72.8 23.7 %collective-permute-done.13.refs_9_ = bf16[2,21,16,256]{3,2,1,0:T(8,128)(2,1)S(1)} collective-permute-done((bf16[2,21,16,256]{3,2,1,0:T(8,128)(2,1)S(1)}, bf16[2,21,16,256]{3,2,1,0:T(8,128)(2,1)S(1)}, u32[]{:S(2)}, u32[]{:S(2)}) %collective-permute-start.13) | collective-permute-done | bytes 344096 | tf_op jit(solution)/shard_map/ppermute | solution.py:34
  96.5 13.3 %attend.5.refs_9_ = bf16[2,1,16,32,256]{4,3,2,1,0:T(8,128)(2,1)S(1)} custom-call(s32[2,171]{1,0:T(2,128)S(1)} %copy-done.9, f32[2,12,1280]{2,1,0:T(8,128)S(1)} %copy-done.7, bf16[16,32,1536]{2,1,0:T(8,128)(2,1)S(1)} %copy-done, bf16[16,32,1536]{2,1,0:T(8,128)(2,1)} %refs_3_.9, bf16[16,32,1536]{2,1,0:T(8,128)(2,1)} %refs_4_.9, ...), custom_call_target="tpu_custom_call" | custom-call | flops 4362076160 | bytes 4096000 | tf_op jit(solution)/shard_map/attend/pallas_call | solution.py:516
  109.9 7.5 %attend.6.refs_9_ = bf16[1,1,16,32,256]{4,3,2,1,0:T(8,128)(2,1)S(1)} custom-call(s32[2,171]{1,0:T(2,128)S(1)} %copy-done.9, f32[2,12,1280]{2,1,0:T(8,128)S(1)} %copy-done.7, bf16[16,32,1536]{2,1,0:T(8,128)(2,1)S(1)} %copy-done, bf16[16,32,1536]{2,1,0:T(8,128)(2,1)} %refs_3_.9, bf16[16,32,1536]{2,1,0:T(8,128)(2,1)} %refs_4_.9, ...), custom_call_target="tpu_custom_call" | custom-call | flops 2181038080 | bytes 4096000 | tf_op jit(solution)/shard_map/attend/pallas_call | solution.py:516
  117.4 0.1 collective-permute-start.17
  117.5 0.1 slice_bitcast_fusion.1
  117.6 0.6 collective-permute-start.19
  118.1 1.2 collective-permute-start.20
  119.3 0.5 collective-permute-start.18
  119.8 0.1 slice_bitcast_fusion
  119.9 1.6 %collective-permute-start.21 = (bf16[1,16,32,256]{3,2,1,0:T(8,128)(2,1)S(1)}, bf16[1,16,32,256]{3,2,1,0:T(8,128)(2,1)S(1)}, u32[]{:S(2)}, u32[]{:S(2)}) collective-permute-start(bf16[1,16,32,256]{3,2,1,0:T(8,128)(2,1)S(1)} %get-tuple-element.34), channel_id=1, source_target_pairs={{0,1},{1,0},{2,3},{3,2},{4,5},{5,4},{6,7},{7,6},{8,9},{9,8},{10,11... | collective-permute-start | bytes 786440 | tf_op jit(solution)/shard_map/ppermute | solution.py:43
  121.5 7.6 %attend.7 = bf16[1,1,16,32,256]{4,3,2,1,0:T(8,128)(2,1)S(1)} custom-call(s32[2,171]{1,0:T(2,128)S(1)} %copy-done.9, f32[2,12,1280]{2,1,0:T(8,128)S(1)} %copy-done.7, bf16[16,32,1536]{2,1,0:T(8,128)(2,1)S(1)} %copy-done, bf16[16,32,1536]{2,1,0:T(8,128)(2,1)} %refs_3_.9, bf16[16,32,1536]{2,1,0:T(8,128)(2,1)} %refs_4_.9, bf16[9,16,32,256]{3,2,1,0:T(8,128)(2,1)} %copy-done.3, ...), custom_call_target="tpu_custom_call" | custom-call | flops 2181038080 | bytes 4096000 | tf_op jit(solution)/shard_map/attend/pallas_call | solution.py:516
  129.1 3.5 %collective-permute-done.18 = bf16[1,16,32,256]{3,2,1,0:T(8,128)(2,1)S(1)} collective-permute-done((bf16[1,16,32,256]{3,2,1,0:T(8,128)(2,1)S(1)}, bf16[1,16,32,256]{3,2,1,0:T(8,128)(2,1)S(1)}, u32[]{:S(2)}, u32[]{:S(2)}) %collective-permute-start.18) | collective-permute-done | bytes 262176 | tf_op jit(solution)/shard_map/ppermute | solution.py:43
  132.6 1.6 %collective-permute-start.23 = (bf16[1,16,32,256]{3,2,1,0:T(8,128)(2,1)S(1)}, bf16[1,16,32,256]{3,2,1,0:T(8,128)(2,1)S(1)}, u32[]{:S(2)}, u32[]{:S(2)}) collective-permute-start(bf16[1,16,32,256]{3,2,1,0:T(8,128)(2,1)S(1)} %get-tuple-element.33), channel_id=1, source_target_pairs={{0,9},{1,8},{8,1},{9,0},{16,25},{17,24},{24,17},{25,16},{2,11},{3,... | collective-permute-start | bytes 786440 | tf_op jit(solution)/shard_map/ppermute | solution.py:49
  134.3 0.5 collective-permute-start.24
  134.8 3.5 %collective-permute-done.21 = bf16[1,16,32,256]{3,2,1,0:T(8,128)(2,1)S(1)} collective-permute-done((bf16[1,16,32,256]{3,2,1,0:T(8,128)(2,1)S(1)}, bf16[1,16,32,256]{3,2,1,0:T(8,128)(2,1)S(1)}, u32[]{:S(2)}, u32[]{:S(2)}) %collective-permute-start.21) | collective-permute-done | bytes 262176 | tf_op jit(solution)/shard_map/ppermute | solution.py:43
  138.2 0.1 pad_add_fusion.2.spot_ref
  138.3 1.6 %collective-permute-start.15 = (bf16[1,16,32,256]{3,2,1,0:T(8,128)(2,1)S(1)}, bf16[1,16,32,256]{3,2,1,0:T(8,128)(2,1)S(1)}, u32[]{:S(2)}, u32[]{:S(2)}) collective-permute-start(bf16[1,16,32,256]{3,2,1,0:T(8,128)(2,1)S(1)} %bitcast.46), channel_id=1, source_target_pairs={{0,9},{1,8},{8,1},{9,0},{16,25},{17,24},{24,17},{25,16},{2,11},{3,... | collective-permute-start | bytes 786440 | tf_op jit(solution)/shard_map/ppermute | solution.py:49
  139.9 3.4 %collective-permute-done.23 = bf16[1,16,32,256]{3,2,1,0:T(8,128)(2,1)S(1)} collective-permute-done((bf16[1,16,32,256]{3,2,1,0:T(8,128)(2,1)S(1)}, bf16[1,16,32,256]{3,2,1,0:T(8,128)(2,1)S(1)}, u32[]{:S(2)}, u32[]{:S(2)}) %collective-permute-start.23) | collective-permute-done | bytes 262176 | tf_op jit(solution)/shard_map/ppermute | solution.py:49
  143.3 6.1 %collective-permute-done.24 = bf16[1,16,32,256]{3,2,1,0:T(8,128)(2,1)S(1)} collective-permute-done((bf16[1,16,32,256]{3,2,1,0:T(8,128)(2,1)S(1)}, bf16[1,16,32,256]{3,2,1,0:T(8,128)(2,1)S(1)}, u32[]{:S(2)}, u32[]{:S(2)}) %collective-permute-start.24) | collective-permute-done | bytes 262176 | tf_op jit(solution)/shard_map/ppermute | solution.py:43
  149.5 7.7 %project.2.refs_2_ = f32[512,1536]{1,0:T(8,128)S(1)} custom-call(s32[2]{0:T(128)S(1)} %pad_add_fusion.2.spot_ref, bf16[512,256]{1,0:T(8,128)(2,1)S(1)} %bitcast.35, bf16[512,256]{1,0:T(8,128)(2,1)S(1)} %bitcast.39, bf16[512,256]{1,0:T(8,128)(2,1)S(1)} %bitcast.37, bf16[512,256]{1,0:T(8,128)(2,1)S(1)} %bitcast.38, bf16[512,256]{1,0:T(8,128)(2,1)S(1)} %bitcast.36, ...), custom_call_target="tpu_custom_call" | custom-call | flops 4429185024 | bytes 8650752 | tf_op jit(solution)/shard_map/project/pallas_call | solution.py:572
  157.2 2.5 %project.3 = bf16[512,1536]{1,0:T(8,128)(2,1)} custom-call(s32[2]{0:T(128)S(1)} %pad_add_fusion.2.spot_ref, bf16[512,256]{1,0:T(8,128)(2,1)S(1)} %bitcast.47, bf16[768,1536]{1,0:T(8,128)(2,1)S(1)} %collective-permute-done.17.refs_14_.refs_18_.refs_1_, f32[512,1536]{1,0:T(8,128)S(1)} %project.2.refs_2_), custom_call_target="tpu_custom_call" | custom-call | flops 402653184 | bytes 786432 | tf_op jit(solution)/shard_map/project/pallas_call | solution.py:572
  (39 shorter events, 0.1 us)
Async XLA Ops:
  0.0 7.9 %copy-start = (bf16[16,32,1536]{2,1,0:T(8,128)(2,1)S(1)}, bf16[16,32,1536]{2,1,0:T(8,128)(2,1)}, u32[]{:S(2)}) copy-start(bf16[16,32,1536]{2,1,0:T(8,128)(2,1)} %refs_2_.9) | copy-start | bytes 4718596
  0.0 7.9 %copy-start.1 = (bf16[16,32,1536]{2,1,0:T(8,128)(2,1)S(1)}, bf16[16,32,1536]{2,1,0:T(8,128)(2,1)}, u32[]{:S(2)}) copy-start(bf16[16,32,1536]{2,1,0:T(8,128)(2,1)} %refs_3_.9) | copy-start | bytes 4718596
  3.1 4.9 %collective-permute-start.1 = (bf16[9,16,32,256]{3,2,1,0:T(8,128)(2,1)}, bf16[9,16,32,256]{3,2,1,0:T(8,128)(2,1)S(1)}, u32[]{:S(2)}, u32[]{:S(2)}) collective-permute-start(bf16[9,16,32,256]{3,2,1,0:T(8,128)(2,1)} %give_half.1), channel_id=1, source_target_pairs={{0,8},{8,0},{16,24},{24,16},{1,9},{9,1},{17,25},{25,17},{2,10},{10... | collective-permute-start | bytes 7077896 | tf_op jit(solution)/shard_map/ppermute | solution.py:39
  7.9 2.1 %copy-start.3 = (bf16[9,16,32,256]{3,2,1,0:T(8,128)(2,1)}, bf16[9,16,32,256]{3,2,1,0:T(8,128)(2,1)S(1)}, u32[]{:S(2)}) copy-start(bf16[9,16,32,256]{3,2,1,0:T(8,128)(2,1)S(1)} %collective-permute-done.1.refs_2_.refs_5_) | copy-start | bytes 7077892
  10.0 17.4 %collective-permute-start.5 = (bf16[2,18,32,256]{3,2,1,0:T(8,128)(2,1)}, bf16[2,18,32,256]{3,2,1,0:T(8,128)(2,1)}, u32[]{:S(2)}, u32[]{:S(2)}) collective-permute-start(bf16[2,18,32,256]{3,2,1,0:T(8,128)(2,1)} %get-tuple-element.22), channel_id=1, source_target_pairs={{0,16},{8,24},{16,0},{24,8},{1,17},{9,25},{17,1},{25,9},{2,18},{10... | collective-permute-start | bytes 1769480 | tf_op jit(solution)/shard_map/ppermute | solution.py:53
  12.9 19.7 %collective-permute-start.3 = (bf16[2,36,16,256]{3,2,1,0:T(8,128)(2,1)}, bf16[2,36,16,256]{3,2,1,0:T(8,128)(2,1)}, u32[]{:S(2)}, u32[]{:S(2)}) collective-permute-start(bf16[2,36,16,256]{3,2,1,0:T(8,128)(2,1)} %get-tuple-element.21), channel_id=1, source_target_pairs={{0,2},{2,0},{4,6},{6,4},{8,10},{10,8},{12,14},{14,12},{16,18},{18,... | collective-permute-start | bytes 1769480 | tf_op jit(solution)/shard_map/ppermute | solution.py:34
  14.5 4.9 %copy-start.4 = (bf16[9,16,32,256]{3,2,1,0:T(8,128)(2,1)S(1)}, bf16[9,16,32,256]{3,2,1,0:T(8,128)(2,1)}, u32[]{:S(2)}) copy-start(bf16[9,16,32,256]{3,2,1,0:T(8,128)(2,1)} %copy-done.3) | copy-start | bytes 7077892
  17.9 99.5 %collective-permute-start.16 = (bf16[768,1536]{1,0:T(8,128)(2,1)}, bf16[768,1536]{1,0:T(8,128)(2,1)}, u32[]{:S(2)}, u32[]{:S(2)}) collective-permute-start(bf16[768,1536]{1,0:T(8,128)(2,1)} %dynamic_slice.3), channel_id=1, source_target_pairs={{0,1},{1,0},{2,3},{3,2},{4,5},{5,4},{6,7},{7,6},{8,9},{9,8},{10,11... | collective-permute-start | bytes 7077896 | tf_op jit(solution)/shard_map/ppermute | solution.py:43
  19.4 5.9 %copy-start.13 = (s32[1,1,13,13]{3,1,2,0:T(1,128)S(1)}, s32[1,1,13,13]{3,1,2,0:T(1,128)}, u32[]{:S(2)}) copy-start(s32[1,1,13,13]{3,1,2,0:T(1,128)} %param.11) | copy-start | bytes 2032
  20.8 0.8 copy-start.10
  21.7 0.8 copy-start.11
  22.5 0.8 copy-start.12
  23.3 16.0 %collective-permute-start.8 = (bf16[2,18,32,256]{3,2,1,0:T(8,128)(2,1)}, bf16[2,18,32,256]{3,2,1,0:T(8,128)(2,1)S(1)}, u32[]{:S(2)}, u32[]{:S(2)}) collective-permute-start(bf16[2,18,32,256]{3,2,1,0:T(8,128)(2,1)} %get-tuple-element.25), channel_id=1, source_target_pairs={{0,16},{8,24},{16,0},{24,8},{1,17},{9,25},{17,1},{25,9},{2,18},{10... | collective-permute-start | bytes 1769480 | tf_op jit(solution)/shard_map/ppermute | solution.py:53
  23.9 22.3 %collective-permute-start.4 = (bf16[2,36,16,256]{3,2,1,0:T(8,128)(2,1)}, bf16[2,36,16,256]{3,2,1,0:T(8,128)(2,1)}, u32[]{:S(2)}, u32[]{:S(2)}) collective-permute-start(bf16[2,36,16,256]{3,2,1,0:T(8,128)(2,1)} %get-tuple-element.19.refs_3_), channel_id=1, source_target_pairs={{2,4},{4,2},{10,12},{12,10},{18,20},{20,18},{26,28},{28,26},{3,5},... | collective-permute-start | bytes 1769480 | tf_op jit(solution)/shard_map/ppermute | solution.py:34
  27.4 1.9 %collective-permute-start = (s32[171]{0:T(256)S(1)}, s32[171]{0:T(256)S(1)}, u32[]{:S(2)}, u32[]{:S(2)}) collective-permute-start(s32[171]{0:T(256)S(1)} %pad_add_fusion.1), channel_id=1, source_target_pairs={{0,8},{8,0},{16,24},{24,16},{1,9},{9,1},{17,25},{25,17},{2,10},{10... | collective-permute-start | bytes 2060 | tf_op jit(solution)/shard_map/ppermute | solution.py:39
  29.3 18.5 %collective-permute-start.6 = (bf16[2,21,16,256]{3,2,1,0:T(8,128)(2,1)}, bf16[2,21,16,256]{3,2,1,0:T(8,128)(2,1)S(1)}, u32[]{:S(2)}, u32[]{:S(2)}) collective-permute-start(bf16[2,21,16,256]{3,2,1,0:T(8,128)(2,1)} %get-tuple-element.23), channel_id=1, source_target_pairs={{0,2},{2,0},{4,6},{6,4},{8,10},{10,8},{12,14},{14,12},{16,18},{18,... | collective-permute-start | bytes 1032200 | tf_op jit(solution)/shard_map/ppermute | solution.py:34
  32.6 16.0 %collective-permute-start.7 = (bf16[2,21,16,256]{3,2,1,0:T(8,128)(2,1)S(1)}, bf16[2,21,16,256]{3,2,1,0:T(8,128)(2,1)}, u32[]{:S(2)}, u32[]{:S(2)}) collective-permute-start(bf16[2,21,16,256]{3,2,1,0:T(8,128)(2,1)S(1)} %get-tuple-element.24.refs_0_), channel_id=1, source_target_pairs={{2,4},{4,2},{10,12},{12,10},{18,20},{20,18},{26,28},{28,26},{3,5},... | collective-permute-start | bytes 1032200 | tf_op jit(solution)/shard_map/ppermute | solution.py:34
  39.3 25.0 %collective-permute-start.2 = (bf16[2,18,32,256]{3,2,1,0:T(8,128)(2,1)}, bf16[2,18,32,256]{3,2,1,0:T(8,128)(2,1)S(1)}, u32[]{:S(2)}, u32[]{:S(2)}) collective-permute-start(bf16[2,18,32,256]{3,2,1,0:T(8,128)(2,1)} %copy-done.12), channel_id=1, source_target_pairs={{0,16},{8,24},{16,0},{24,8},{1,17},{9,25},{17,1},{25,9},{2,18},{10... | collective-permute-start | bytes 1769480 | tf_op jit(solution)/shard_map/ppermute | solution.py:53
  46.2 24.3 %collective-permute-start.11 = (bf16[2,36,16,256]{3,2,1,0:T(8,128)(2,1)}, bf16[2,36,16,256]{3,2,1,0:T(8,128)(2,1)S(1)}, u32[]{:S(2)}, u32[]{:S(2)}) collective-permute-start(bf16[2,36,16,256]{3,2,1,0:T(8,128)(2,1)} %copy-done.11), channel_id=1, source_target_pairs={{0,2},{2,0},{4,6},{6,4},{8,10},{10,8},{12,14},{14,12},{16,18},{18,... | collective-permute-start | bytes 1769480 | tf_op jit(solution)/shard_map/ppermute | solution.py:34
  47.9 24.0 %collective-permute-start.12 = (bf16[2,36,16,256]{3,2,1,0:T(8,128)(2,1)}, bf16[2,36,16,256]{3,2,1,0:T(8,128)(2,1)S(1)}, u32[]{:S(2)}, u32[]{:S(2)}) collective-permute-start(bf16[2,36,16,256]{3,2,1,0:T(8,128)(2,1)} %copy-done.10), channel_id=1, source_target_pairs={{2,4},{4,2},{10,12},{12,10},{18,20},{20,18},{26,28},{28,26},{3,5},... | collective-permute-start | bytes 1769480 | tf_op jit(solution)/shard_map/ppermute | solution.py:34
  48.6 0.9 copy-start.6
  49.5 0.7 copy-start.8
  50.2 14.1 %copy-start.2 = (bf16[16,32,1536]{2,1,0:T(8,128)(2,1)S(1)}, bf16[16,32,1536]{2,1,0:T(8,128)(2,1)}, u32[]{:S(2)}) copy-start(bf16[16,32,1536]{2,1,0:T(8,128)(2,1)} %refs_3_.9) | copy-start | bytes 4718596
  50.2 14.1 %copy-start.5 = (bf16[9,16,32,256]{3,2,1,0:T(8,128)(2,1)S(1)}, bf16[9,16,32,256]{3,2,1,0:T(8,128)(2,1)}, u32[]{:S(2)}) copy-start(bf16[9,16,32,256]{3,2,1,0:T(8,128)(2,1)} %copy-done.3) | copy-start | bytes 7077892
  64.3 32.2 %copy-start.7 = (f32[2,12,1280]{2,1,0:T(8,128)S(1)}, f32[2,12,1280]{2,1,0:T(8,128)}, u32[]{:S(2)}) copy-start(f32[2,12,1280]{2,1,0:T(8,128)} %tables.1.refs_1_) | copy-start | bytes 368644
  64.3 32.2 %copy-start.9 = (s32[2,171]{1,0:T(2,128)S(1)}, s32[2,171]{1,0:T(2,128)}, u32[]{:S(2)}) copy-start(s32[2,171]{1,0:T(2,128)} %pad_add_fusion.refs_0_.refs_1_) | copy-start | bytes 4108
  65.4 44.4 %collective-permute-start.9 = (bf16[2,57,16,256]{3,2,1,0:T(8,128)(2,1)S(1)}, bf16[2,57,16,256]{3,2,1,0:T(8,128)(2,1)S(1)}, u32[]{:S(2)}, u32[]{:S(2)}) collective-permute-start(bf16[2,57,16,256]{3,2,1,0:T(8,128)(2,1)S(1)} %get-tuple-element.27), channel_id=1, source_target_pairs={{0,2},{2,0},{4,6},{6,4},{8,10},{10,8},{12,14},{14,12},{16,18},{18,... | collective-permute-start | bytes 2801672 | tf_op jit(solution)/shard_map/ppermute | solution.py:34
  69.8 40.1 %collective-permute-start.10 = (bf16[2,57,16,256]{3,2,1,0:T(8,128)(2,1)S(1)}, bf16[2,57,16,256]{3,2,1,0:T(8,128)(2,1)S(1)}, u32[]{:S(2)}, u32[]{:S(2)}) collective-permute-start(bf16[2,57,16,256]{3,2,1,0:T(8,128)(2,1)S(1)} %get-tuple-element.28.refs_11_), channel_id=1, source_target_pairs={{2,4},{4,2},{10,12},{12,10},{18,20},{20,18},{26,28},{28,26},{3,5},... | collective-permute-start | bytes 2801672 | tf_op jit(solution)/shard_map/ppermute | solution.py:34
  70.5 26.0 %collective-permute-start.13 = (bf16[2,21,16,256]{3,2,1,0:T(8,128)(2,1)S(1)}, bf16[2,21,16,256]{3,2,1,0:T(8,128)(2,1)S(1)}, u32[]{:S(2)}, u32[]{:S(2)}) collective-permute-start(bf16[2,21,16,256]{3,2,1,0:T(8,128)(2,1)S(1)} %get-tuple-element.31), channel_id=1, source_target_pairs={{0,2},{2,0},{4,6},{6,4},{8,10},{10,8},{12,14},{14,12},{16,18},{18,... | collective-permute-start | bytes 1032200 | tf_op jit(solution)/shard_map/ppermute | solution.py:34
  71.9 24.6 %collective-permute-start.14 = (bf16[2,21,16,256]{3,2,1,0:T(8,128)(2,1)S(1)}, bf16[2,21,16,256]{3,2,1,0:T(8,128)(2,1)S(1)}, u32[]{:S(2)}, u32[]{:S(2)}) collective-permute-start(bf16[2,21,16,256]{3,2,1,0:T(8,128)(2,1)S(1)} %get-tuple-element.26.refs_11_), channel_id=1, source_target_pairs={{2,4},{4,2},{10,12},{12,10},{18,20},{20,18},{26,28},{28,26},{3,5},... | collective-permute-start | bytes 1032200 | tf_op jit(solution)/shard_map/ppermute | solution.py:34
  117.4 32.1 %collective-permute-start.17 = (bf16[768,1536]{1,0:T(8,128)(2,1)}, bf16[768,1536]{1,0:T(8,128)(2,1)S(1)}, u32[]{:S(2)}, u32[]{:S(2)}) collective-permute-start(bf16[768,1536]{1,0:T(8,128)(2,1)} %collective-permute-done.16.refs_12_.refs_16_.refs_20_), channel_id=1, source_target_pairs={{0,8},{8,0},{16,24},{24,16},{1,9},{9,1},{17,25},{25,17},{2,10},{10... | collective-permute-start | bytes 7077896 | tf_op jit(solution)/shard_map/ppermute | solution.py:39
  117.6 15.0 %collective-permute-start.19 = (bf16[1,16,32,256]{3,2,1,0:T(8,128)(2,1)S(1)}, bf16[1,16,32,256]{3,2,1,0:T(8,128)(2,1)S(1)}, u32[]{:S(2)}, u32[]{:S(2)}) collective-permute-start(bf16[1,16,32,256]{3,2,1,0:T(8,128)(2,1)S(1)} %get-tuple-element.36), channel_id=1, source_target_pairs={{0,8},{8,0},{16,24},{24,16},{1,9},{9,1},{17,25},{25,17},{2,10},{10... | collective-permute-start | bytes 786440 | tf_op jit(solution)/shard_map/ppermute | solution.py:39
  118.1 16.1 %collective-permute-start.20 = (bf16[1,16,32,256]{3,2,1,0:T(8,128)(2,1)S(1)}, bf16[1,16,32,256]{3,2,1,0:T(8,128)(2,1)S(1)}, u32[]{:S(2)}, u32[]{:S(2)}) collective-permute-start(bf16[1,16,32,256]{3,2,1,0:T(8,128)(2,1)S(1)} %get-tuple-element.36), channel_id=1, source_target_pairs={{0,9},{1,8},{8,1},{9,0},{16,25},{17,24},{24,17},{25,16},{2,11},{3,... | collective-permute-start | bytes 786440 | tf_op jit(solution)/shard_map/ppermute | solution.py:49
  119.3 13.3 %collective-permute-start.18 = (bf16[1,16,32,256]{3,2,1,0:T(8,128)(2,1)S(1)}, bf16[1,16,32,256]{3,2,1,0:T(8,128)(2,1)S(1)}, u32[]{:S(2)}, u32[]{:S(2)}) collective-permute-start(bf16[1,16,32,256]{3,2,1,0:T(8,128)(2,1)S(1)} %get-tuple-element.37), channel_id=1, source_target_pairs={{0,1},{1,0},{2,3},{3,2},{4,5},{5,4},{6,7},{7,6},{8,9},{9,8},{10,11... | collective-permute-start | bytes 786440 | tf_op jit(solution)/shard_map/ppermute | solution.py:43
  119.9 18.3 %collective-permute-start.21 = (bf16[1,16,32,256]{3,2,1,0:T(8,128)(2,1)S(1)}, bf16[1,16,32,256]{3,2,1,0:T(8,128)(2,1)S(1)}, u32[]{:S(2)}, u32[]{:S(2)}) collective-permute-start(bf16[1,16,32,256]{3,2,1,0:T(8,128)(2,1)S(1)} %get-tuple-element.34), channel_id=1, source_target_pairs={{0,1},{1,0},{2,3},{3,2},{4,5},{5,4},{6,7},{7,6},{8,9},{9,8},{10,11... | collective-permute-start | bytes 786440 | tf_op jit(solution)/shard_map/ppermute | solution.py:43
  132.6 5.7 %collective-permute-start.22 = (bf16[1,16,32,256]{3,2,1,0:T(8,128)(2,1)S(1)}, bf16[1,16,32,256]{3,2,1,0:T(8,128)(2,1)S(1)}, u32[]{:S(2)}, u32[]{:S(2)}) collective-permute-start(bf16[1,16,32,256]{3,2,1,0:T(8,128)(2,1)S(1)} %get-tuple-element.33), channel_id=1, source_target_pairs={{0,8},{8,0},{16,24},{24,16},{1,9},{9,1},{17,25},{25,17},{2,10},{10... | collective-permute-start | bytes 786440 | tf_op jit(solution)/shard_map/ppermute | solution.py:39
  132.6 10.7 %collective-permute-start.23 = (bf16[1,16,32,256]{3,2,1,0:T(8,128)(2,1)S(1)}, bf16[1,16,32,256]{3,2,1,0:T(8,128)(2,1)S(1)}, u32[]{:S(2)}, u32[]{:S(2)}) collective-permute-start(bf16[1,16,32,256]{3,2,1,0:T(8,128)(2,1)S(1)} %get-tuple-element.33), channel_id=1, source_target_pairs={{0,9},{1,8},{8,1},{9,0},{16,25},{17,24},{24,17},{25,16},{2,11},{3,... | collective-permute-start | bytes 786440 | tf_op jit(solution)/shard_map/ppermute | solution.py:49
  134.3 15.2 %collective-permute-start.24 = (bf16[1,16,32,256]{3,2,1,0:T(8,128)(2,1)S(1)}, bf16[1,16,32,256]{3,2,1,0:T(8,128)(2,1)S(1)}, u32[]{:S(2)}, u32[]{:S(2)}) collective-permute-start(bf16[1,16,32,256]{3,2,1,0:T(8,128)(2,1)S(1)} %bitcast.33), channel_id=1, source_target_pairs={{0,1},{1,0},{2,3},{3,2},{4,5},{5,4},{6,7},{7,6},{8,9},{9,8},{10,11... | collective-permute-start | bytes 786440 | tf_op jit(solution)/shard_map/ppermute | solution.py:43
  138.2 11.2 %collective-permute-start.25 = (bf16[1,16,32,256]{3,2,1,0:T(8,128)(2,1)S(1)}, bf16[1,16,32,256]{3,2,1,0:T(8,128)(2,1)S(1)}, u32[]{:S(2)}, u32[]{:S(2)}) collective-permute-start(bf16[1,16,32,256]{3,2,1,0:T(8,128)(2,1)S(1)} %bitcast.45), channel_id=1, source_target_pairs={{0,8},{8,0},{16,24},{24,16},{1,9},{9,1},{17,25},{25,17},{2,10},{10... | collective-permute-start | bytes 786440 | tf_op jit(solution)/shard_map/ppermute | solution.py:39
  138.3 18.9 %collective-permute-start.15 = (bf16[1,16,32,256]{3,2,1,0:T(8,128)(2,1)S(1)}, bf16[1,16,32,256]{3,2,1,0:T(8,128)(2,1)S(1)}, u32[]{:S(2)}, u32[]{:S(2)}) collective-permute-start(bf16[1,16,32,256]{3,2,1,0:T(8,128)(2,1)S(1)} %bitcast.46), channel_id=1, source_target_pairs={{0,9},{1,8},{8,1},{9,0},{16,25},{17,24},{24,17},{25,16},{2,11},{3,... | collective-permute-start | bytes 786440 | tf_op jit(solution)/shard_map/ppermute | solution.py:49
